TPU v7x, 32 devices: a whole 2x2x4 slice. The times are simulated.
32 devices in a mesh: rep: 2 (over x), data: 4 (over z), expert: 4 (over y, core).
Axes of the slice: x: 2, y: 2, z: 4, core: 2. Of those that a mesh axis runs over, the one named last changes fastest.
Arguments:
- x: bfloat16 [64, 512, 1536], P(('rep', 'expert', 'data')), parts along dimension 0
- expert_idx: int32 [64, 512, 8], P(('rep', 'expert', 'data')), parts along dimension 0
- gate: float32 [64, 512, 8], P(('rep', 'expert', 'data')), parts along dimension 0
- attn_gain: float32 [1536], replicated
- w_qkv: bfloat16 [1536, 40, 64], P(('data', 'expert'))
- w_out: bfloat16 [24, 64, 1536], P(None, None, ('data', 'expert'))
- moe_gain: float32 [1536], replicated
- w_gate: bfloat16 [40, 1536, 512], P('expert', 'data')
- w_up: bfloat16 [40, 1536, 512], P('expert', 'data')
- w_down: bfloat16 [40, 512, 1536], P('expert', None, 'data')
Outputs:
- output: bfloat16 [64, 512, 1536], P(('rep', 'expert', 'data')), parts along dimension 0
There are 2 independent parts. A program takes and returns all parts, laid end to end along the dimension named above; an argument that names none is the same for every part.
All inputs are finite; a program needn't handle non-finite values.
Results may differ from a plain program's by a relative error of at most 0.0150391.
Values are sent between devices in bfloat16 or wider.
A program may use at most 1 GiB of HBM per device.

v0:
```python
import jax
import jax.numpy as jnp
from jax import lax
from jax.sharding import PartitionSpec as P

NORM_EPS = 1e-6
ROPE_BASE = 10000.0


def rms_scale(tok_rows, gain):
    rows_f32 = tok_rows.astype(jnp.float32)
    inv_rms = lax.rsqrt(jnp.mean(rows_f32 * rows_f32, axis=-1, keepdims=True) + NORM_EPS)
    return (rows_f32 * inv_rms * gain).astype(jnp.bfloat16)


def rope_apply(head_vals):
    seq_len, head_dim = head_vals.shape[1], head_vals.shape[-1]
    half_dim = head_dim // 2
    inv_freq = ROPE_BASE ** (-jnp.arange(half_dim, dtype=jnp.float32) * 2.0 / head_dim)
    angles = jnp.arange(seq_len, dtype=jnp.float32)[:, None] * inv_freq[None, :]
    cos_b = jnp.cos(angles)[None, :, None, :]
    sin_b = jnp.sin(angles)[None, :, None, :]
    vals_f32 = head_vals.astype(jnp.float32)
    low_half = vals_f32[..., :half_dim]
    high_half = vals_f32[..., half_dim:]
    return jnp.concatenate([low_half * cos_b - high_half * sin_b, high_half * cos_b + low_half * sin_b], axis=-1).astype(jnp.bfloat16)


def attention_block(seqs, attn_gain, w_qkv, w_out):
    num_seqs, seq_len, model_dim = seqs.shape
    head_dim = w_qkv.shape[2]
    num_heads = w_out.shape[0]
    kv_heads = (w_qkv.shape[1] - num_heads) // 2
    group_len = num_heads // kv_heads
    normed = rms_scale(seqs, attn_gain)
    qkv_all = jnp.einsum('uno,ojf->unjf', normed, w_qkv, preferred_element_type=jnp.float32).astype(jnp.bfloat16)
    queries = rope_apply(qkv_all[:, :, :num_heads]).reshape(num_seqs, seq_len, kv_heads, group_len, head_dim)
    keys_rot = rope_apply(qkv_all[:, :, num_heads:num_heads + kv_heads])
    values = qkv_all[:, :, num_heads + kv_heads:]
    scores = jnp.einsum('slkgd,smkd->skglm', queries, keys_rot, preferred_element_type=jnp.float32) * (head_dim ** -0.5)
    causal = lax.broadcasted_iota(jnp.int32, (seq_len, seq_len), 0) >= lax.broadcasted_iota(jnp.int32, (seq_len, seq_len), 1)
    attn_probs = jax.nn.softmax(jnp.where(causal, scores, -1e30), axis=-1).astype(jnp.bfloat16)
    mixed = jnp.einsum('skglm,smkd->slkgd', attn_probs, values, preferred_element_type=jnp.float32).astype(jnp.bfloat16)
    out_grouped = w_out.reshape(kv_heads, group_len, head_dim, model_dim)
    attn_proj = jnp.einsum('slkgd,kgdm->slm', mixed, out_grouped, preferred_element_type=jnp.float32)
    return (seqs.astype(jnp.float32) + attn_proj).astype(jnp.bfloat16)


def capacity_of(tok_dev, top_k, num_experts):
    return 8 * ((5 * top_k * tok_dev + 32 * num_experts - 1) // (32 * num_experts))


def dispatch_target(flat_ids, num_experts, capacity):
    onehot = (flat_ids[:, None] == jnp.arange(num_experts, dtype=jnp.int32)[None, :]).astype(jnp.int32)
    earlier = jnp.cumsum(onehot, axis=0) - onehot
    slot_pos = jnp.sum(earlier * onehot, axis=1)
    return jnp.where(slot_pos < capacity, flat_ids * capacity + slot_pos, num_experts * capacity)


def gather_rows(normed, target_rows, num_experts, capacity, top_k):
    tok_dev = normed.shape[0]
    source = jnp.full((num_experts * capacity + 1,), tok_dev, jnp.int32)
    source = source.at[target_rows].set(jnp.arange(tok_dev * top_k, dtype=jnp.int32) // top_k)
    padded = jnp.concatenate([normed, jnp.zeros((1, normed.shape[1]), normed.dtype)], axis=0)
    return jnp.take(padded, source[:num_experts * capacity], axis=0)


def combine_rows(expert_rows, target_rows, gate_rows):
    tok_dev, top_k = gate_rows.shape
    padded = jnp.concatenate([expert_rows, jnp.zeros((1, expert_rows.shape[1]), expert_rows.dtype)], axis=0)
    picked = jnp.take(padded, target_rows, axis=0).reshape(tok_dev, top_k, expert_rows.shape[1])
    return jnp.sum(picked.astype(jnp.float32) * gate_rows[:, :, None], axis=1)


def solution(mesh):
    expert_size = mesh.shape['expert']
    tok_spec = P(('rep', 'expert', 'data'), None, None)
    group_axes = ('data', 'expert')

    def local_step(x_loc, idx_loc, gate_loc, attn_gain, qkv_part, out_part, moe_gain, gate_part, up_part, down_part):
        w_qkv = lax.all_gather(qkv_part, group_axes, axis=0, tiled=True)
        w_out = lax.all_gather(out_part, group_axes, axis=2, tiled=True)
        hidden = attention_block(x_loc, attn_gain, w_qkv, w_out)
        num_seqs, seq_len, model_dim = hidden.shape
        tok_dev = num_seqs * seq_len
        top_k = idx_loc.shape[-1]
        loc_experts = gate_part.shape[0]
        num_experts = loc_experts * expert_size
        capacity = capacity_of(tok_dev, top_k, num_experts)
        flat_hidden = hidden.reshape(tok_dev, model_dim)
        normed = rms_scale(flat_hidden, moe_gain)
        target_rows = dispatch_target(idx_loc.reshape(tok_dev * top_k), num_experts, capacity)
        send_buf = gather_rows(normed, target_rows, num_experts, capacity, top_k).reshape(expert_size, loc_experts, capacity, model_dim)
        recv_buf = lax.all_to_all(send_buf, 'expert', 0, 2, tiled=True).reshape(loc_experts, expert_size * capacity, model_dim)
        w_gate = lax.all_gather(gate_part, 'data', axis=1, tiled=True)
        w_up = lax.all_gather(up_part, 'data', axis=1, tiled=True)
        w_down = lax.all_gather(down_part, 'data', axis=2, tiled=True)
        act_gate = jnp.einsum('ncm,nmf->ncf', recv_buf, w_gate, preferred_element_type=jnp.float32)
        act_up = jnp.einsum('ncm,nmf->ncf', recv_buf, w_up, preferred_element_type=jnp.float32)
        mid_act = (jax.nn.silu(act_gate) * act_up).astype(jnp.bfloat16)
        expert_out = jnp.einsum('ncf,nfm->ncm', mid_act, w_down, preferred_element_type=jnp.float32).astype(jnp.bfloat16)
        returned = lax.all_to_all(expert_out.reshape(1, loc_experts, expert_size * capacity, model_dim), 'expert', 2, 0, tiled=True)
        mixed_sum = combine_rows(returned.reshape(num_experts * capacity, model_dim), target_rows, gate_loc.reshape(tok_dev, top_k))
        total = flat_hidden.astype(jnp.float32) + mixed_sum
        return total.astype(jnp.bfloat16).reshape(num_seqs, seq_len, model_dim)

    in_specs = (tok_spec, tok_spec, tok_spec, P(None), P(group_axes, None, None), P(None, None, group_axes), P(None), P('expert', 'data', None), P('expert', 'data', None), P('expert', None, 'data'))
    return jax.shard_map(local_step, mesh=mesh, in_specs=in_specs, out_specs=tok_spec, check_vma=False)
```

profile of v0, /device:TPU:0, one launch (start us, length us, event | category | flops | bytes accessed | tf_op | source)
XLA Modules:
  0.0 1908.0 jit_solution(458231543107567525)
XLA Ops:
  16.4 11.9 reduce-window.6
  32.4 30.6 %scatter_custom_fusion = s32[10241]{0:T(1024)S(1)} fusion(s32[8192]{0:T(1024)S(1)} %bitcast.142, s32[8192]{0:T(1024)S(1)} %add_select_fusion, s32[]{:T(128)} %constant.78.clone.1), kind=kCustom, calls=%fused_computation.83 | custom fusion | bytes 40968 | tf_op jit(solution)/shard_map/scatter | solution.py:63
  64.3 29.0 %all-gather.8.cloned.1.call-done = bf16[24,64,1536]{1,0,2:T(8,128)(2,1)} async-done(((bf16[24,64,96]{1,0,2:T(8,128)(2,1)}), bf16[24,64,1536]{1,0,2:T(8,128)(2,1)}) %all-gather.8.cloned.1.call-update) | async-done | bytes 4718608 | tf_op jit(solution)/shard_map/all_gather | solution.py:82
  93.3 11.0 copy.26
  104.4 108.9 %all-gather.6.cloned.1.call-done = bf16[1536,40,64]{2,1,0:T(8,128)(2,1)} async-done(((bf16[96,40,64]{2,1,0:T(8,128)(2,1)}), bf16[1536,40,64]{2,1,0:T(8,128)(2,1)}) %all-gather.6.cloned.1.call-update) | async-done | bytes 7864336 | tf_op jit(solution)/shard_map/all_gather | solution.py:81
  213.2 17.4 copy.23
  230.7 10.9 fusion.38
  247.3 24.4 %fusion.64 = (f32[2,8,3,512]{3,2,1,0:T(4,128)}, f32[2,8,3,512,512]{3,4,2,1,0:T(8,128)}) fusion(pred[512,512]{0,1:T(8,128)(4,1)S(1)} %iota_compare_fusion.2, bf16[2,512,8,3,32]{1,4,3,2,0:T(8,128)(2,1)} %bitcast.139, bf16[2,512,8,3,32]{1,4,3,2,0:T(8,128)(2,1)} %bitcast.138, bf16[2,512,8,32]{1,3,2,0:T(8,128)(2,1)} %get-tuple-element.8, ...), kind=kOutput, calls=%fused_computation.96 | convolution fusion | flops 1669333504 | bytes 54886400 | tf_op jit(solution)/shard_map/sub | solution.py:42
  271.6 26.6 %multiply_reduce_fusion.1 = (f32[2,512]{1,0:T(2,128)S(1)}, f32[2,512,1536]{2,1,0:T(8,128)}) fusion(bf16[8,3,64,1536,1]{3,2,1,0,4:T(8,128)(2,1)} %bitcast.137, bf16[2,512,40,64]{1,3,2,0:T(8,128)(2,1)} %copy-done, bf16[2,512,1536]{2,1,0:T(8,128)(2,1)S(1)} %copy-done.1, f32[2,8,3,512,512]{3,4,2,1,0:T(8,128)} %get-tuple-element.14, ...), kind=kOutput, calls=%fused_computation.33 | convolution fusion | flops 6478625792 | bytes 65671168 | tf_op jit(solution)/shard_map/slkgd,kgdm->slm/dot_general | solution.py:45
  301.8 46.5 %gather_fusion = bf16[10240,1536]{1,0:T(8,128)(2,1)} fusion(bf16[1025,1536]{1,0:T(8,128)(2,1)S(1)} %concatenate.23, s32[10240]{0:T(1024)S(1)} %copy-done.6), kind=kCustom, calls=%fused_computation | custom fusion | bytes 62955520 | tf_op jit(solution)/shard_map/jit(_take)/gather | solution.py:65
  348.3 21.6 %broadcast_select_fusion = bf16[4,10,256,1536]{3,2,1,0:T(8,128)(2,1)} fusion(bf16[4,10,256,1536]{3,2,1,0:T(8,128)(2,1)} %bitcast.132, pred[4,10,256]{2,1,0:T(8,128)(4,1)S(1)} %copy-done.10), kind=kLoop, calls=%fused_computation.10 | loop fusion | flops 15728640 | bytes 62924800 | tf_op jit(solution)/shard_map/jit(_take)/select_n | solution.py:65
  380.0 339.4 %all-to-all-done = bf16[4,10,256,1536]{3,2,1,0:T(8,128)(2,1)} async-done(((bf16[4,10,256,1536]{3,2,1,0:T(8,128)(2,1)}), bf16[4,10,256,1536]{3,2,1,0:T(8,128)(2,1)}, u32[]{:S(2)}, u32[]{:S(2)}) %all-to-all-start) | async-done | bytes 31457312 | tf_op jit(solution)/shard_map/all_to_all | solution.py:94
  719.4 21.6 %copy.33 = bf16[1,10,4,256,1536]{4,3,2,1,0:T(8,128)(2,1)} copy(bf16[1,10,4,256,1536]{4,3,1,2,0:T(8,128)(2,1)} %bitcast.22) | data formatting | bytes 62914560 | tf_op jit(solution)/shard_map/all_to_all | solution.py:94
  741.0 29.1 %fusion.67 = f32[10,1024,512]{2,1,0:T(8,128)} fusion(bf16[10,1024,1536]{2,1,0:T(8,128)(2,1)} %bitcast.133, bf16[10,1536,512]{2,1,0:T(8,128)(2,1)} %all-gather.10.cloned.1.call-done), kind=kOutput, calls=%fused_computation.97 | convolution fusion | flops 16106127360 | bytes 68157440 | tf_op jit(solution)/shard_map/ncm,nmf->ncf/dot_general | solution.py:98
  770.0 30.2 %multiply_convert_fusion.4 = bf16[10,1024,512]{2,1,0:T(8,128)(2,1)} fusion(f32[10,1024,512]{2,1,0:T(8,128)} %fusion.67, bf16[10,1024,1536]{2,1,0:T(8,128)(2,1)} %bitcast.134, bf16[10,1536,512]{2,1,0:T(8,128)(2,1)} %all-gather.12.cloned.1.call-done), kind=kOutput, calls=%fused_computation.17.clone.clone.1 | convolution fusion | flops 16137584640 | bytes 78643200 | tf_op jit(solution)/shard_map/ncm,nmf->ncf/dot_general | solution.py:99
  800.2 224.0 %all-gather.14.cloned.1.call-done = bf16[10,512,1536]{2,1,0:T(8,128)(2,1)} async-done(((bf16[10,512,384]{2,1,0:T(8,128)(2,1)}), bf16[10,512,1536]{2,1,0:T(8,128)(2,1)}) %all-gather.14.cloned.1.call-update) | async-done | bytes 15728656 | tf_op jit(solution)/shard_map/all_gather | solution.py:97
  1024.2 26.6 %convert_bitcast_fusion = bf16[1,10,1024,1536]{3,2,1,0:T(8,128)(2,1)} fusion(bf16[10,512,1536]{2,1,0:T(8,128)(2,1)} %all-gather.14.cloned.1.call-done, bf16[10,1024,512]{2,1,0:T(8,128)(2,1)} %multiply_convert_fusion.4), kind=kOutput, calls=%fused_computation.9 | convolution fusion | flops 16121856000 | bytes 57671680 | tf_op jit(solution)/shard_map/ncf,nfm->ncm/dot_general | solution.py:101
  1050.8 35.8 %copy.34 = bf16[1,10,1024,1536]{3,1,0,2:T(8,128)(2,1)} copy(bf16[1,10,1024,1536]{3,2,1,0:T(8,128)(2,1)} %convert_bitcast_fusion) | data formatting | bytes 62914560 | tf_op jit(solution)/shard_map/reshape | solution.py:102
  1086.6 11.9 all-to-all-start.1
  1099.5 541.3 %all-to-all-done.1 = bf16[1,10,1024,1536]{3,1,0,2:T(8,128)(2,1)} async-done(((bf16[1,10,1024,1536]{3,1,0,2:T(8,128)(2,1)}), bf16[1,10,1024,1536]{3,1,0,2:T(8,128)(2,1)}, u32[]{:S(2)}, u32[]{:S(2)}) %all-to-all-start.1) | async-done | bytes 31457312 | tf_op jit(solution)/shard_map/all_to_all | solution.py:102
  1640.8 29.0 %copy.35 = bf16[1,10,4,256,1536]{4,3,1,2,0:T(8,128)(2,1)} copy(bf16[1,10,4,256,1536]{4,1,3,2,0:T(8,128)(2,1)} %bitcast.25) | data formatting | bytes 62914560 | tf_op jit(solution)/shard_map/all_to_all | solution.py:102
  1669.8 21.4 %concatenate.24 = bf16[10241,1536]{1,0:T(8,128)(2,1)} pad(bf16[10240,1536]{1,0:T(8,128)(2,1)} %bitcast.131, bf16[]{:T(256)} %constant.84.clone.1), padding=0_1x0_0 | pad | bytes 62917632 | tf_op jit(solution)/shard_map/concatenate | solution.py:70
  1691.2 175.8 %gather_fusion.1 = bf16[8192,1536]{1,0:T(8,128)(2,1)} fusion(bf16[10241,1536]{1,0:T(8,128)(2,1)} %concatenate.24, s32[8192]{0:T(1024)S(1)} %broadcast_clamp_fusion), kind=kCustom, calls=%fused_computation.1 | custom fusion | bytes 50364416 | tf_op jit(solution)/shard_map/jit(_take)/gather | solution.py:71
  1867.0 26.8 %multiply_reduce_fusion = f32[1024,1536]{1,0:T(8,128)} fusion(bf16[8192,1536]{1,0:T(8,128)(2,1)} %gather_fusion.1, f32[1024,8]{1,0:T(8,128)S(1)} %copy.36, pred[1024,8]{1,0:T(8,128)(4,1)S(1)} %compare_and_fusion), kind=kLoop, calls=%fused_computation.5 | loop fusion | flops 48758784 | bytes 31498240 | tf_op jit(solution)/shard_map/reduce_sum | solution.py:72
  (78 shorter events, 42.6 us)
Async XLA Ops:
  6.5 6.0 copy-start.7
  6.5 86.8 %all-gather.8.cloned.1.call-start = ((), (), s32[]{:S(2)}) async-start(), calls=%async_computation.3 | async-start | bytes 10027008 | tf_op jit(solution)/shard_map/all_gather | solution.py:82
  8.7 204.5 %all-gather.6.cloned.1.call-start = ((), (), s32[]{:S(2)}) async-start(), calls=%async_computation.2 | async-start | bytes 16711680 | tf_op jit(solution)/shard_map/all_gather | solution.py:81
  11.2 729.8 %all-gather.10.cloned.1.call-start = ((), (), s32[]{:S(2)}) async-start(), calls=%async_computation.4 | async-start | bytes 19660800 | tf_op jit(solution)/shard_map/all_gather | solution.py:95
  11.9 758.1 %all-gather.12.cloned.1.call-start = ((), (), s32[]{:S(2)}) async-start(), calls=%async_computation.5 | async-start | bytes 19660800 | tf_op jit(solution)/shard_map/all_gather | solution.py:96
  13.3 17.4 copy-start.4
  31.7 61.6 %copy-start.2 = (s32[8192]{0:T(1024)}, s32[8192]{0:T(1024)S(1)}, u32[]{:S(2)}) copy-start(s32[8192]{0:T(1024)S(1)} %fusion.46) | copy-start | bytes 98308
  31.8 0.6 copy-start.8
  104.3 126.3 %copy-start.1 = (bf16[2,512,1536]{2,1,0:T(8,128)(2,1)S(1)}, bf16[2,512,1536]{2,1,0:T(8,128)(2,1)}, u32[]{:S(2)}) copy-start(bf16[2,512,1536]{2,1,0:T(8,128)(2,1)} %param.10) | copy-start | bytes 9437188
  104.4 126.3 %copy-start.13 = (f32[1536]{0:T(1024)S(1)}, f32[1536]{0:T(1024)}, u32[]{:S(2)}) copy-start(f32[1536]{0:T(1024)} %param.13) | copy-start | bytes 18436
  241.5 2.9 copy-start
  271.6 26.6 %copy-start.12 = (f32[1536]{0:T(1024)S(1)}, f32[1536]{0:T(1024)}, u32[]{:S(2)}) copy-start(f32[1536]{0:T(1024)} %param.16) | copy-start | bytes 18436
  298.2 3.6 copy-start.6
  301.8 46.5 %copy-start.10 = (pred[4,10,256]{2,1,0:T(8,128)(4,1)S(1)}, pred[4,10,256]{2,1,0:T(8,128)(4,1)}, u32[]{:S(2)}) copy-start(pred[4,10,256]{2,1,0:T(8,128)(4,1)} %compare_and_fusion.1) | copy-start | bytes 30724
  370.0 349.4 %all-to-all-start = ((bf16[4,10,256,1536]{3,2,1,0:T(8,128)(2,1)}), bf16[4,10,256,1536]{3,2,1,0:T(8,128)(2,1)}, u32[]{:S(2)}, u32[]{:S(2)}) async-start(bf16[4,10,256,1536]{3,2,1,0:T(8,128)(2,1)} %broadcast_select_fusion), calls=%async_computation | async-start | bytes 62914560 | tf_op jit(solution)/shard_map/all_to_all | solution.py:94
  379.4 644.8 %all-gather.14.cloned.1.call-start = ((), (), s32[]{:S(2)}) async-start(), calls=%async_computation.6 | async-start | bytes 19660800 | tf_op jit(solution)/shard_map/all_gather | solution.py:97
  1086.5 12.0 copy-start.3
  1086.5 12.3 copy-start.5
  1086.6 12.5 copy-start.11
  1086.6 12.7 copy-start.9
  1086.6 554.2 %all-to-all-start.1 = ((bf16[1,10,1024,1536]{3,1,0,2:T(8,128)(2,1)}), bf16[1,10,1024,1536]{3,1,0,2:T(8,128)(2,1)}, u32[]{:S(2)}, u32[]{:S(2)}) async-start(bf16[1,10,1024,1536]{3,1,0,2:T(8,128)(2,1)} %copy.34), calls=%async_computation.1 | async-start | bytes 100663296 | tf_op jit(solution)/shard_map/all_to_all | solution.py:102
Sparse Core Ops, SparseCore 0:
  9.6 83.6 all-gather.7
  95.6 117.5 all-gather.5
  214.8 269.1 all-gather.9
  485.4 268.6 all-gather.11
  755.5 268.6 all-gather.13
where the time goes:
time: 1920 us; the launch traced here: 1910 us
  waiting for transfers between devices  1240 us (65%)
  local copies, waits for them, and re-layouts  398 us (21%)
  matrix products  148 us (8%)
  other arithmetic  83.1 us (4%)
  starting transfers between devices  21.5 us (1%)
    all_to_all x1, waiting for transfers between devices, local_step(): lax.all_to_all(expert_out.reshape(1, loc_experts, expert_size * capacity,...  541 us
    all_to_all x1, waiting for transfers between devices, local_step(): lax.all_to_all(send_buf, 'expert', 0, 2, tiled=True)  339 us
    all_gather x1, waiting for transfers between devices, local_step(): w_down = lax.all_gather(down_part, 'data', axis=2, tiled=True)  224 us
    gather x1, local copies, waits for them, and re-layouts, combine_rows(): jnp.take(padded, target_rows, axis=0)  176 us
    all_gather x1, waiting for transfers between devices, local_step(): w_qkv = lax.all_gather(qkv_part, group_axes, axis=0, tiled=True)  109 us
    gather x1, local copies, waits for them, and re-layouts, gather_rows(): return jnp.take(padded, source[:num_experts * capacity], axis=0)  46.5 us
  transfers between devices with their start and end apart: 7, of which 5 were waited for; matrix products, arithmetic and copies ran while one was open for 16% of the time, Pallas kernels for 0%

commit v1 on v0

v1 whole, which is shorter than its diff:
```python
import functools

import jax
import jax.numpy as jnp
from jax import lax
from jax.experimental import pallas as pl
from jax.experimental.pallas import tpu as pltpu
from jax.sharding import PartitionSpec as P


NORM_EPS = 1e-6
ROPE_BASE = 10000.0
F32 = jnp.float32
BF16 = jnp.bfloat16
VMEM_LIMIT = 58 * 1024 * 1024


def qkv_kernel(rope_cols, half_dim, x_ref, gain_ref, w_ref, cos_ref, sin_ref, o_ref):
    rows_f32 = x_ref[...].astype(F32)
    inv_rms = lax.rsqrt(jnp.mean(rows_f32 * rows_f32, axis=-1, keepdims=True) + NORM_EPS)
    normed = (rows_f32 * inv_rms * gain_ref[...]).astype(BF16)
    lanes = 128
    low = lax.broadcasted_iota(jnp.int32, cos_ref.shape, 1) % (2 * half_dim) < half_dim
    for c in range(0, w_ref.shape[1], 2 * lanes):
        part = jnp.dot(normed, w_ref[:, c:c + 2 * lanes], preferred_element_type=F32).astype(BF16)
        if c >= rope_cols:
            o_ref[:, c:c + 2 * lanes] = part
            continue
        for b in range(0, 2 * lanes, lanes):
            vals = part[:, b:b + lanes].astype(F32)
            other = jnp.where(low, pltpu.roll(vals, lanes - half_dim, 1), pltpu.roll(vals, half_dim, 1))
            o_ref[:, c + b:c + b + lanes] = (vals * cos_ref[...] + other * sin_ref[...]).astype(BF16)


def qkv_project(x, gain, w_qkv, cos_t, sin_t, rope_cols, half_dim):
    toks, width = x.shape
    seq_len = cos_t.shape[0]
    cols = w_qkv.shape[1]
    fixed = lambda shape: pl.BlockSpec(shape, lambda i: (0, 0))
    return pl.pallas_call(
        functools.partial(qkv_kernel, rope_cols, half_dim), name="k_qkv", grid=(toks // seq_len,),
        in_specs=[pl.BlockSpec((seq_len, width), lambda i: (i, 0)), fixed((1, width)), fixed(w_qkv.shape), fixed(cos_t.shape), fixed(sin_t.shape)],
        out_specs=pl.BlockSpec((seq_len, cols), lambda i: (i, 0)),
        out_shape=jax.ShapeDtypeStruct((toks, cols), BF16),
        cost_estimate=pl.CostEstimate(flops=2 * toks * width * cols, bytes_accessed=2 * (toks * width + width * cols + toks * cols), transcendentals=0),
        compiler_params=pltpu.CompilerParams(vmem_limit_bytes=VMEM_LIMIT),
    )(x, gain, w_qkv, cos_t, sin_t)


def attend_kernel(group_len, head_dim, q_ref, k_ref, v_ref, o_ref):
    seq_len = q_ref.shape[0]
    tile = 256
    scale = head_dim ** -0.5 * 1.4426950408889634
    for kh in range(k_ref.shape[1] // head_dim):
        keys = k_ref[:, kh * head_dim:(kh + 1) * head_dim]
        vals = v_ref[:, kh * head_dim:(kh + 1) * head_dim]
        for g in range(group_len):
            c = (kh * group_len + g) * head_dim
            for r in range(0, seq_len, tile):
                seen = r + tile
                scores = lax.dot_general(q_ref[r:seen, c:c + head_dim], keys[:seen], (((1,), (1,)), ((), ())), preferred_element_type=F32)
                causal = lax.broadcasted_iota(jnp.int32, scores.shape, 0) + r >= lax.broadcasted_iota(jnp.int32, scores.shape, 1)
                scores = jnp.where(causal, scores, -1e30)
                top = jnp.max(scores, axis=-1, keepdims=True)
                weights = jnp.exp2((scores - top) * scale)
                probs = (weights * (1.0 / jnp.sum(weights, axis=-1, keepdims=True))).astype(BF16)
                o_ref[r:seen, c:c + head_dim] = jnp.dot(probs, vals[:seen], preferred_element_type=F32).astype(BF16)


def attend(qkv, seq_len, num_heads, kv_heads, head_dim):
    toks = qkv.shape[0]
    group_len = num_heads // kv_heads
    pair = 128 // head_dim
    qcols = pair * group_len * head_dim
    kcol0 = num_heads * head_dim // 128
    vcol0 = (num_heads + kv_heads) * head_dim // 128
    return pl.pallas_call(
        functools.partial(attend_kernel, group_len, head_dim), name="k_attn", grid=(toks // seq_len, kv_heads // pair),
        in_specs=[pl.BlockSpec((seq_len, qcols), lambda s, j: (s, j)), pl.BlockSpec((seq_len, 128), lambda s, j: (s, kcol0 + j)),
                  pl.BlockSpec((seq_len, 128), lambda s, j: (s, vcol0 + j))],
        out_specs=pl.BlockSpec((seq_len, qcols), lambda s, j: (s, j)),
        out_shape=jax.ShapeDtypeStruct((toks, num_heads * head_dim), BF16),
        cost_estimate=pl.CostEstimate(flops=16 * toks * seq_len * num_heads * head_dim, bytes_accessed=2 * toks * (qkv.shape[1] + num_heads * head_dim), transcendentals=toks * seq_len * num_heads),
        compiler_params=pltpu.CompilerParams(vmem_limit_bytes=VMEM_LIMIT),
    )(qkv, qkv, qkv)


def project_kernel(a_ref, w_ref, x_ref, gain_ref, h_ref, z_ref):
    proj = lax.dot_general(a_ref[...], w_ref[...], (((1,), (1,)), ((), ())), preferred_element_type=F32)
    hidden = (x_ref[...].astype(F32) + proj).astype(BF16)
    h_ref[...] = hidden
    rows_f32 = hidden.astype(F32)
    inv_rms = lax.rsqrt(jnp.mean(rows_f32 * rows_f32, axis=-1, keepdims=True) + NORM_EPS)
    z_ref[...] = (rows_f32 * inv_rms * gain_ref[...]).astype(BF16)


def project(mixed, w_out_t, x, gain):
    toks, width = x.shape
    tile = 256
    row = lambda n: pl.BlockSpec((tile, n), lambda i: (i, 0))
    fixed = lambda shape: pl.BlockSpec(shape, lambda i: (0, 0))
    return pl.pallas_call(
        project_kernel, name="k_out", grid=(toks // tile,),
        in_specs=[row(mixed.shape[1]), fixed(w_out_t.shape), row(width), fixed((1, width))],
        out_specs=[row(width)] * 2,
        out_shape=[jax.ShapeDtypeStruct((toks, width), BF16)] * 2,
        cost_estimate=pl.CostEstimate(flops=2 * toks * width * mixed.shape[1], bytes_accessed=2 * (4 * toks * width + width * width), transcendentals=0),
        compiler_params=pltpu.CompilerParams(vmem_limit_bytes=VMEM_LIMIT),
    )(mixed, w_out_t, x, gain)


def attention_block(seqs, attn_gain, w_qkv, w_out_t, num_heads, kv_heads, head_dim, moe_gain):
    num_seqs, seq_len, width = seqs.shape
    half_dim = head_dim // 2
    inv_freq = ROPE_BASE ** (-jnp.arange(half_dim, dtype=F32) * 2.0 / head_dim)
    angles = jnp.arange(seq_len, dtype=F32)[:, None] * inv_freq[None, :]
    cos_t, sin_t = jnp.cos(angles), jnp.sin(angles)
    cos_t = jnp.concatenate([cos_t] * (128 // half_dim), axis=1)
    sin_t = jnp.concatenate([-sin_t, sin_t] * (64 // half_dim), axis=1)
    x = seqs.reshape(num_seqs * seq_len, width)
    qkv = qkv_project(x, attn_gain.reshape(1, width), w_qkv, cos_t, sin_t, (num_heads + kv_heads) * head_dim, half_dim)
    mixed = attend(qkv, seq_len, num_heads, kv_heads, head_dim)
    return project(mixed, w_out_t, x, moe_gain.reshape(1, width))


def dispatch_kernel(half, cap, rank_ref, rows_ref, buf_ref, out_ref, hot_ref):
    del buf_ref
    step = pl.program_id(0)
    toks, width = rows_ref.shape
    slots = lax.broadcasted_iota(jnp.int32, (cap, toks), 0).astype(F32)
    for i in range(half):
        ranks = rank_ref[pl.ds(step * half + i, 1), :]
        hot_ref[i * cap:(i + 1) * cap, :] = jnp.where(slots == ranks, 1.0, 0.0).astype(BF16)
    for c in range(0, width, 512):
        part = jnp.dot(hot_ref[...], rows_ref[:, c:c + 512], preferred_element_type=F32)
        out_ref[:, 0, :, c:c + 512] = part.astype(BF16).reshape(half, cap, 512)


def dispatch(rank_rows, rows, buf, slot, experts, cap, sources):
    toks, width = rows.shape
    half = experts // 2
    alias = {} if buf is None else {2: 0}
    args = (rank_rows, rows) + (() if buf is None else (buf,))
    body = functools.partial(dispatch_kernel, half, cap)
    if buf is None:
        def body(rank_ref, rows_ref, out_ref, hot_ref):
            dispatch_kernel(half, cap, rank_ref, rows_ref, None, out_ref, hot_ref)
    in_specs = [pl.BlockSpec(rank_rows.shape, lambda g: (0, 0)), pl.BlockSpec((toks, width), lambda g: (0, 0))]
    if buf is not None:
        in_specs.append(pl.BlockSpec(memory_space=pl.ANY))
    return pl.pallas_call(
        body, grid=(2,),
        out_shape=jax.ShapeDtypeStruct((experts, sources, cap, width), BF16),
        in_specs=in_specs,
        out_specs=pl.BlockSpec((half, 1, cap, width), lambda g: (g, slot, 0, 0)),
        scratch_shapes=[pltpu.VMEM((half * cap, toks), BF16)],
        input_output_aliases=alias,
        cost_estimate=pl.CostEstimate(flops=2 * experts * cap * toks * width, bytes_accessed=2 * (toks + experts * cap) * width, transcendentals=0),
        compiler_params=pltpu.CompilerParams(vmem_limit_bytes=VMEM_LIMIT),
    )(*args)


def gate_up_kernel(steps, s_ref, x_ref, *refs):
    g_refs, u_refs = refs[:steps], refs[steps:2 * steps]
    m_ref, wg_ref, wu_ref = refs[2 * steps:]
    d = s_ref[1]
    depth = g_refs[0].shape[1]
    for t in range(steps):
        rows = pl.ds(pl.multiple_of(lax.rem(d + steps - t, steps) * depth, depth), depth)
        wg_ref[rows, :] = g_refs[t][0]
        wu_ref[rows, :] = u_refs[t][0]
    x = x_ref[0]
    act = jnp.dot(x, wg_ref[...], preferred_element_type=F32)
    up = jnp.dot(x, wu_ref[...], preferred_element_type=F32)
    m_ref[0] = (act * jax.nn.sigmoid(act) * up).astype(BF16)


def gate_up(scal, x, which, gates, ups):
    half, depth, ff = gates[1].shape
    steps = len(gates)
    _, rows, width = x.shape
    own = pl.BlockSpec((1, depth, ff), lambda i, s: (s[0] + i, 0, 0))
    piece = pl.BlockSpec((1, depth, ff), lambda i, s: (i, 0, 0))
    return pl.pallas_call(
        functools.partial(gate_up_kernel, steps),
        grid_spec=pltpu.PrefetchScalarGridSpec(
            num_scalar_prefetch=1, grid=(half,),
            in_specs=[pl.BlockSpec((1, rows, width), lambda i, s: (which * half + i, 0, 0))] + ([own] + [piece] * (steps - 1)) * 2,
            out_specs=pl.BlockSpec((1, rows, ff), lambda i, s: (i, 0, 0)),
            scratch_shapes=[pltpu.VMEM((width, ff), BF16)] * 2),
        out_shape=jax.ShapeDtypeStruct((half, rows, ff), BF16),
        cost_estimate=pl.CostEstimate(flops=4 * half * rows * width * ff, bytes_accessed=2 * half * (rows * width + 2 * width * ff), transcendentals=0),
        compiler_params=pltpu.CompilerParams(vmem_limit_bytes=VMEM_LIMIT),
    )(scal, x, *gates, *ups)


def combine_kernel(half, adds, s_ref, table_ref, ma_ref, mb_ref, wa_ref, wb_ref, *refs):
    del s_ref
    add_refs, (o0_ref, o1_ref, acc_ref) = refs[:adds], refs[adds:]
    g = pl.program_id(0)
    toks, cap = table_ref.shape[1], ma_ref.shape[1]
    table = table_ref[0]
    slots = lax.broadcasted_iota(jnp.int32, (toks, cap), 1).astype(F32)
    for e in range(2 * half):
        m_ref, w_ref, i = (ma_ref, wa_ref, e) if e < half else (mb_ref, wb_ref, e - half)
        o = jnp.dot(m_ref[i], w_ref[i], preferred_element_type=F32).astype(BF16)
        hot = jnp.where(slots == table[:, e:e + 1], 1.0, 0.0).astype(BF16)
        picked = jnp.dot(hot, o, preferred_element_type=F32) * table[:, 2 * half + e:2 * half + e + 1]
        if e == 0:
            acc_ref[...] = picked
        else:
            acc_ref[...] += picked

    @pl.when(g == 0)
    def _():
        o0_ref[...] = acc_ref[...] + add_refs[0][...] if adds else acc_ref[...]

    @pl.when(g == 1)
    def _():
        o1_ref[...] = acc_ref[...] + add_refs[1][...] if adds else acc_ref[...]


def combine(scal, table, first, stride, mids, downs, adds):
    sources, toks, lanes = table.shape
    half, rows, ff = mids[0].shape
    cap = rows // sources
    cols = downs[0].shape[2]
    src = lambda g: first + stride * g
    whole = pl.BlockSpec((toks, cols), lambda g, s: (0, 0))
    return pl.pallas_call(
        functools.partial(combine_kernel, half, len(adds)),
        grid_spec=pltpu.PrefetchScalarGridSpec(
            num_scalar_prefetch=1, grid=(2,),
            in_specs=[pl.BlockSpec((1, toks, lanes), lambda g, s: (src(g), 0, 0)),
                      pl.BlockSpec((half, cap, ff), lambda g, s: (0, src(g), 0)),
                      pl.BlockSpec((half, cap, ff), lambda g, s: (0, src(g), 0)),
                      pl.BlockSpec((half, ff, cols), lambda g, s: (s[0], 0, 0)),
                      pl.BlockSpec((half, ff, cols), lambda g, s: (s[1], 0, 0))] + [whole] * len(adds),
            out_specs=[whole, whole],
            scratch_shapes=[pltpu.VMEM((toks, cols), F32)]),
        out_shape=[jax.ShapeDtypeStruct((toks, cols), F32)] * 2,
        cost_estimate=pl.CostEstimate(flops=2 * 2 * half * 2 * cap * cols * (ff + toks), bytes_accessed=2 * 2 * half * (ff * cols + 2 * cap * ff) + 8 * toks * cols * (1 + len(adds) // 2), transcendentals=0),
        compiler_params=pltpu.CompilerParams(vmem_limit_bytes=VMEM_LIMIT),
    )(scal, table, *mids, *downs, *adds)


def finish_kernel(steps, s_ref, h_ref, *refs):
    own, far, y_ref = refs[:steps], refs[steps:2 * steps], refs[2 * steps]
    cols = own[0].shape[1]
    for t in range(steps):
        at = pl.ds(pl.multiple_of(lax.rem(s_ref[0] + steps - t, steps) * cols, 128), cols)
        y_ref[:, at] = (h_ref[:, at].astype(F32) + (own[t][...] + far[t][...])).astype(BF16)


def finish(scal, hidden, own, far):
    toks, width = hidden.shape
    cols = own[0].shape[1]
    tile = 256
    wide = pl.BlockSpec((tile, width), lambda i, s: (i, 0))
    part = pl.BlockSpec((tile, cols), lambda i, s: (i, 0))
    return pl.pallas_call(
        functools.partial(finish_kernel, len(own)), name="finish",
        grid_spec=pltpu.PrefetchScalarGridSpec(
            num_scalar_prefetch=1, grid=(toks // tile,),
            in_specs=[wide] + [part] * (2 * len(own)), out_specs=wide),
        out_shape=jax.ShapeDtypeStruct((toks, width), BF16),
        cost_estimate=pl.CostEstimate(flops=2 * toks * width, bytes_accessed=12 * toks * width, transcendentals=0),
        compiler_params=pltpu.CompilerParams(vmem_limit_bytes=VMEM_LIMIT),
    )(scal, hidden, *own, *far)


def solution(mesh):
    sources = mesh.shape['expert']
    steps = mesh.shape['data']
    tok_spec = P(('rep', 'expert', 'data'), None, None)
    group_axes = ('data', 'expert')
    ring = [(i, (i + 1) % steps) for i in range(steps)]
    flip = [[(i, i ^ k) for i in range(sources)] for k in range(sources)]
    swap = [(0, 1), (1, 0)]

    def local_step(x_loc, idx_loc, gate_loc, attn_gain, qkv_part, out_part, moe_gain, gate_part, up_part, down_part):
        rep, data, expert = (lax.axis_index(a) for a in ('rep', 'data', 'expert'))
        num_seqs, seq_len, width = x_loc.shape
        toks = num_seqs * seq_len
        top_k = idx_loc.shape[-1]
        experts = gate_part.shape[0]
        half = experts // 2
        cap = 8 * ((5 * top_k * toks + 32 * experts * sources - 1) // (32 * experts * sources))
        heads_all, head_dim = qkv_part.shape[1:]
        num_heads = out_part.shape[0]

        def pieces(w):
            mine = lax.dynamic_slice_in_dim(w, rep * half, half, 0)
            near, far = [], []
            for _ in range(1, steps):
                mine = lax.ppermute(mine, 'data', ring)
                near.append(mine)
                far.append(lax.ppermute(mine, 'rep', swap))
            return near, far

        w_qkv = lax.all_gather(qkv_part.reshape(qkv_part.shape[0], heads_all * head_dim), group_axes, axis=0, tiled=True)
        w_out_t = lax.all_gather(out_part.reshape(num_heads * head_dim, -1).T, group_axes, axis=0, tiled=True)
        g_near, g_far = pieces(gate_part)
        u_near, u_far = pieces(up_part)
        d_near, d_far = pieces(down_part)

        idx_t = idx_loc.reshape(toks, top_k).T
        gate_t = gate_loc.reshape(toks, top_k).T
        idx_all = jnp.stack([idx_t] + [lax.ppermute(idx_t, 'expert', flip[k]) for k in range(1, sources)])
        gate_all = jnp.stack([gate_t] + [lax.ppermute(gate_t, 'expert', flip[k]) for k in range(1, sources)])
        order = lax.iota(jnp.int32, experts)
        local_ids = expert * experts + (order // half + rep) % 2 * half + order % half
        match = idx_all[:, :, None, :] == local_ids[None, None, :, None]
        taken = jnp.any(match, axis=1)
        weight = jnp.sum(jnp.where(match, gate_all[:, :, None, :], 0.0), axis=1)
        before = (lax.broadcasted_iota(jnp.int32, (toks, toks), 0) < lax.broadcasted_iota(jnp.int32, (toks, toks), 1)).astype(BF16)
        rank = jnp.dot(taken.reshape(sources * experts, toks).astype(BF16), before, preferred_element_type=F32).reshape(sources, experts, toks)
        rank = jnp.where(taken & (rank < cap), rank, -1.0)
        rank_rows = jnp.pad(rank, ((0, 0), (0, 16 - experts), (0, 0)), constant_values=-1.0)
        table = jnp.pad(jnp.concatenate([rank, weight], axis=1), ((0, 0), (0, 128 - 2 * experts), (0, 0))).transpose(0, 2, 1)

        attn_gain, rank_rows, table = lax.optimization_barrier((attn_gain, rank_rows, table))
        hidden, normed = attention_block(x_loc, attn_gain, w_qkv, w_out_t, num_heads, (heads_all - num_heads) // 2, head_dim, moe_gain)
        z_y = lax.ppermute(normed, 'expert', flip[2])
        z_c = lax.ppermute(normed, 'expert', flip[1])
        z_yc = lax.ppermute(z_y, 'expert', flip[1])
        buf = None
        for k, rows in enumerate((normed, z_c, z_y, z_yc)):
            buf = dispatch(rank_rows[k], rows, buf, k, experts, cap, sources)
        x_all = buf.reshape(experts, sources * cap, width)

        scal = jnp.stack([rep * half, data]).astype(jnp.int32)
        scal_far = jnp.stack([(1 - rep) * half, data]).astype(jnp.int32)
        mid_near = gate_up(scal, x_all, 0, [gate_part] + g_near, [up_part] + u_near)
        mid_far = gate_up(scal_far, x_all, 1, [gate_part] + g_far, [up_part] + u_far)
        mids = (mid_near, mid_far)

        own_s = jnp.stack([rep, 1 - rep]).astype(jnp.int32)
        zero_s = jnp.zeros((2,), jnp.int32)
        own, far = [], []
        for t in range(steps):
            downs = (down_part, down_part) if t == 0 else (d_near[t - 1], d_far[t - 1])
            s = own_s if t == 0 else zero_s
            p1, p3 = combine(s, table, 1, 2, mids, downs, ())
            r1, r3 = lax.ppermute(p1, 'expert', flip[1]), lax.ppermute(p3, 'expert', flip[1])
            a0, a2 = combine(s, table, 0, 2, mids, downs, (r1, r3))
            own.append(a0)
            far.append(lax.ppermute(a2, 'expert', flip[2]))
        y = finish(data.reshape(1).astype(jnp.int32), hidden, own, far)
        return y.reshape(num_seqs, seq_len, width)

    in_specs = (tok_spec, tok_spec, tok_spec, P(None), P(group_axes, None, None), P(None, None, group_axes), P(None), P('expert', 'data', None), P('expert', 'data', None), P('expert', None, 'data'))

    return jax.shard_map(local_step, mesh=mesh, in_specs=in_specs, out_specs=tok_spec, check_vma=False)
```

time: 1920 us -> 939 us (0.49)
  waiting for transfers between devices: 1240 us -> 545 us
  local copies, waits for them, and re-layouts: 398 us -> 25 us
  Pallas kernels: 0 us -> 311 us
  matrix products: 148 us -> 1.46 us
  other arithmetic: 83.1 us -> 6.49 us
    all_to_all x2 -> x0, waiting for transfers between devices: 881 us -> none  [the longest x1 541 us: local_step(): lax.all_to_all(expert_out.reshape(1, loc_experts, expert_size * capacity,...]
    ppermute x0 -> x39, waiting for transfers between devices: none -> 450 us  [the longest x9 231 us: pieces(): mine = lax.ppermute(mine, 'data', ring)]
    pallas_call x0 -> x18, Pallas kernels: none -> 311 us  [the longest x8 141 us: combine(): pl.pallas_call(functools.partial(combine_kernel, half, len(adds)), grid_s...]
    all_gather x5 -> x2, waiting for transfers between devices: 362 us -> 95 us  [the longest x1 91.1 us: local_step(): lax.all_gather(qkv_part.reshape(qkv_part.shape[0], heads_all * head_dim),...]
    gather x2 -> x0, local copies, waits for them, and re-layouts: 222 us -> none  [the longest x1 176 us: combine_rows(): jnp.take(padded, target_rows, axis=0)]
    dot_general x5 -> x1, matrix products: 123 us -> 1.46 us  [local_step(): jnp.dot(taken.reshape(sources * experts, toks).astype(BF16), before, pref...]
    all_to_all x2 -> x0, local copies, waits for them, and re-layouts: 50.6 us -> none  [the longest x1 29 us: local_step(): lax.all_to_all(expert_out.reshape(1, loc_experts, expert_size * capacity,...]
    scatter x1 -> x0, local copies, waits for them, and re-layouts: 30.6 us -> none  [gather_rows(): source.at[target_rows]]
  transfers between devices with their start and end apart: 7 -> 41, of which waited for: 5 -> 16; matrix products, arithmetic and copies ran while one was open for 16% -> 3% of each run, Pallas kernels for 0% -> 33%
where the time goes in v1:
time: 939 us; the launch traced here: 933 us
  waiting for transfers between devices  545 us (58%)
  Pallas kernels  311 us (33%)
  starting transfers between devices  30.2 us (3%)
  local copies, waits for them, and re-layouts  25 us (3%)
  between operations  13.8 us (1%)
    ppermute x9, waiting for transfers between devices, pieces(): mine = lax.ppermute(mine, 'data', ring)  231 us
    ppermute x9, waiting for transfers between devices, pieces(): far.append(lax.ppermute(mine, 'rep', swap))  141 us
    pallas_call x8, Pallas kernels, combine(): pl.pallas_call(functools.partial(combine_kernel, half, len(adds)), grid_s...  141 us
    all_gather x1, waiting for transfers between devices, local_step(): lax.all_gather(qkv_part.reshape(qkv_part.shape[0], heads_all * head_dim),...  91.1 us
    ppermute x4, waiting for transfers between devices, local_step(): far.append(lax.ppermute(a2, 'expert', flip[2]))  76.8 us
    pallas_call x4, Pallas kernels, dispatch(): pl.pallas_call(body, grid=(2,), out_shape=jax.ShapeDtypeStruct((experts,...  49.5 us
    pallas_call x2, Pallas kernels, gate_up(): pl.pallas_call(functools.partial(gate_up_kernel, steps), grid_spec=pltpu....  45 us
    pallas_call x1, Pallas kernels, attend(): pl.pallas_call(functools.partial(attend_kernel, group_len, head_dim), nam...  43.3 us
  transfers between devices with their start and end apart: 41, of which 16 were waited for; matrix products, arithmetic and copies ran while one was open for 3% of the time, Pallas kernels for 33%

profile of v1, /device:TPU:0, one launch (start us, length us, event | category | flops | bytes accessed | tf_op | source)
XLA Modules:
  0.0 932.8 jit_solution(6378463071774579426)
XLA Ops:
  34.9 91.1 %all-gather.3.cloned.1.call-done.w_ref = bf16[1536,2560]{1,0:T(8,128)(2,1)} async-done(((bf16[96,2560]{1,0:T(8,128)(2,1)}), bf16[1536,2560]{1,0:T(8,128)(2,1)}) %all-gather.3.cloned.1.call-update) | async-done | bytes 7864336 | tf_op jit(solution)/shard_map/all_gather | solution.py:301
  140.7 43.3 %k_attn.1.a_ref = bf16[1024,1536]{1,0:T(8,128)(2,1)} custom-call(bf16[1024,2560]{1,0:T(8,128)(2,1)} %k_qkv.1.q_ref.k_ref.v_ref, bf16[1024,2560]{1,0:T(8,128)(2,1)} %k_qkv.1.q_ref.k_ref.v_ref, bf16[1024,2560]{1,0:T(8,128)(2,1)} %k_qkv.1.q_ref.k_ref.v_ref), custom_call_target="tpu_custom_call" | custom-call | flops 12884901888 | bytes 8388608 | tf_op jit(solution)/shard_map/k_attn/pallas_call | solution.py:77
  202.4 44.8 %collective-permute-done.23.wa_ref = bf16[5,512,384]{2,1,0:T(8,128)(2,1)} collective-permute-done((bf16[5,512,384]{2,1,0:T(8,128)(2,1)S(1)}, bf16[5,512,384]{2,1,0:T(8,128)(2,1)}, u32[]{:S(2)}, u32[]{:S(2)}) %collective-permute-start.23) | collective-permute-done | bytes 1966112 | tf_op jit(solution)/shard_map/ppermute | solution.py:296
  248.7 40.7 %collective-permute-done.10.refs_2_ = bf16[5,384,512]{2,1,0:T(8,128)(2,1)} collective-permute-done((bf16[5,384,512]{2,1,0:T(8,128)(2,1)}, bf16[5,384,512]{2,1,0:T(8,128)(2,1)}, u32[]{:S(2)}, u32[]{:S(2)}) %collective-permute-start.10) | collective-permute-done | bytes 1966112 | tf_op jit(solution)/shard_map/ppermute | solution.py:296
  296.5 35.0 %collective-permute-done.13.refs_6_ = bf16[5,384,512]{2,1,0:T(8,128)(2,1)} collective-permute-done((bf16[5,384,512]{2,1,0:T(8,128)(2,1)}, bf16[5,384,512]{2,1,0:T(8,128)(2,1)}, u32[]{:S(2)}, u32[]{:S(2)}) %collective-permute-start.13) | collective-permute-done | bytes 1966112 | tf_op jit(solution)/shard_map/ppermute | solution.py:296
  333.0 40.7 %collective-permute-done.27.wa_ref = bf16[5,512,384]{2,1,0:T(8,128)(2,1)} collective-permute-done((bf16[5,512,384]{2,1,0:T(8,128)(2,1)}, bf16[5,512,384]{2,1,0:T(8,128)(2,1)}, u32[]{:S(2)}, u32[]{:S(2)}) %collective-permute-start.27) | collective-permute-done | bytes 1966112 | tf_op jit(solution)/shard_map/ppermute | solution.py:296
  417.2 40.7 %collective-permute-done.14.refs_7_ = bf16[5,384,512]{2,1,0:T(8,128)(2,1)} collective-permute-done((bf16[5,384,512]{2,1,0:T(8,128)(2,1)}, bf16[5,384,512]{2,1,0:T(8,128)(2,1)}, u32[]{:S(2)}, u32[]{:S(2)}) %collective-permute-start.14) | collective-permute-done | bytes 1966112 | tf_op jit(solution)/shard_map/ppermute | solution.py:296
  472.2 26.7 %collective-permute-done.31.wa_ref = bf16[5,512,384]{2,1,0:T(8,128)(2,1)S(1)} collective-permute-done((bf16[5,512,384]{2,1,0:T(8,128)(2,1)}, bf16[5,512,384]{2,1,0:T(8,128)(2,1)S(1)}, u32[]{:S(2)}, u32[]{:S(2)}) %collective-permute-start.31) | collective-permute-done | bytes 1966112 | tf_op jit(solution)/shard_map/ppermute | solution.py:296
  500.4 22.3 %shard_map.104.ma_ref = bf16[5,1024,512]{2,1,0:T(8,128)(2,1)} custom-call(s32[2]{0:T(128)} %get-tuple-element.54.s_ref, bf16[10,1024,1536]{2,1,0:T(8,128)(2,1)} %bitcast.43, bf16[10,384,512]{2,1,0:T(8,128)(2,1)} %refs_0_.3, bf16[5,384,512]{2,1,0:T(8,128)(2,1)} %collective-permute-done.9.refs_1_, bf16[5,384,512]{2,1,0:T(8,128)(2,1)} %collective-permute-done.10.refs_2_, ...), custom_call_target="tpu_custom_call" | custom-call | flops 16106127360 | bytes 31457280 | tf_op jit(solution)/shard_map/pallas_call | solution.py:184
  524.8 16.8 %collective-permute-done.17.refs_3_ = bf16[5,384,512]{2,1,0:T(8,128)(2,1)} collective-permute-done((bf16[5,384,512]{2,1,0:T(8,128)(2,1)}, bf16[5,384,512]{2,1,0:T(8,128)(2,1)}, u32[]{:S(2)}, u32[]{:S(2)}) %collective-permute-start.17) | collective-permute-done | bytes 1966112 | tf_op jit(solution)/shard_map/ppermute | solution.py:298
  541.5 42.1 %collective-permute-done.20.refs_7_ = bf16[5,384,512]{2,1,0:T(8,128)(2,1)} collective-permute-done((bf16[5,384,512]{2,1,0:T(8,128)(2,1)}, bf16[5,384,512]{2,1,0:T(8,128)(2,1)}, u32[]{:S(2)}, u32[]{:S(2)}) %collective-permute-start.20) | collective-permute-done | bytes 1966112 | tf_op jit(solution)/shard_map/ppermute | solution.py:298
  583.7 22.7 %shard_map.105.mb_ref = bf16[5,1024,512]{2,1,0:T(8,128)(2,1)} custom-call(s32[2]{0:T(128)} %get-tuple-element.55.s_ref, bf16[10,1024,1536]{2,1,0:T(8,128)(2,1)} %bitcast.44, bf16[10,384,512]{2,1,0:T(8,128)(2,1)} %refs_0_.3, bf16[5,384,512]{2,1,0:T(8,128)(2,1)} %collective-permute-done.15.refs_1_, bf16[5,384,512]{2,1,0:T(8,128)(2,1)} %collective-permute-done.16.refs_2_, ...), custom_call_target="tpu_custom_call" | custom-call | flops 16106127360 | bytes 31457280 | tf_op jit(solution)/shard_map/pallas_call | solution.py:184
  606.4 19.4 %collective-permute-done.32.wb_ref = bf16[5,512,384]{2,1,0:T(8,128)(2,1)} collective-permute-done((bf16[5,512,384]{2,1,0:T(8,128)(2,1)S(1)}, bf16[5,512,384]{2,1,0:T(8,128)(2,1)}, u32[]{:S(2)}, u32[]{:S(2)}) %collective-permute-start.32) | collective-permute-done | bytes 1966112 | tf_op jit(solution)/shard_map/ppermute | solution.py:298
  626.3 17.0 %shard_map.112 = (f32[1024,384]{1,0:T(8,128)}, f32[1024,384]{1,0:T(8,128)}) custom-call(s32[2]{0:T(128)} %broadcast_8_s_ref.2.s_ref, f32[4,1024,128]{2,1,0:T(8,128)} %fusion.3.table_ref, bf16[5,1024,512]{2,1,0:T(8,128)(2,1)} %shard_map.104.ma_ref, bf16[5,1024,512]{2,1,0:T(8,128)(2,1)} %shard_map.105.mb_ref, bf16[5,512,384]{2,1,0:T(8,128)(2,1)} %copy-done.11, ...), custom_call_target="tpu_custom_call" | custom-call | flops 6039797760 | bytes 12320768 | tf_op jit(solution)/shard_map/pallas_call | solution.py:230
  643.8 63.0 %collective-permute-done.28.wb_ref = bf16[5,512,384]{2,1,0:T(8,128)(2,1)} collective-permute-done((bf16[5,512,384]{2,1,0:T(8,128)(2,1)}, bf16[5,512,384]{2,1,0:T(8,128)(2,1)}, u32[]{:S(2)}, u32[]{:S(2)}) %collective-permute-start.28) | collective-permute-done | bytes 1966112 | tf_op jit(solution)/shard_map/ppermute | solution.py:298
  706.8 17.2 %shard_map.110 = (f32[1024,384]{1,0:T(8,128)}, f32[1024,384]{1,0:T(8,128)}) custom-call(s32[2]{0:T(128)} %broadcast_8_s_ref.2.s_ref, f32[4,1024,128]{2,1,0:T(8,128)} %fusion.3.table_ref, bf16[5,1024,512]{2,1,0:T(8,128)(2,1)} %shard_map.104.ma_ref, bf16[5,1024,512]{2,1,0:T(8,128)(2,1)} %shard_map.105.mb_ref, ...), custom_call_target="tpu_custom_call" | custom-call | flops 6039797760 | bytes 12320768 | tf_op jit(solution)/shard_map/pallas_call | solution.py:230
  726.4 16.9 %shard_map.108 = (f32[1024,384]{1,0:T(8,128)}, f32[1024,384]{1,0:T(8,128)}) custom-call(s32[2]{0:T(128)} %broadcast_8_s_ref.2.s_ref, f32[4,1024,128]{2,1,0:T(8,128)} %fusion.3.table_ref, bf16[5,1024,512]{2,1,0:T(8,128)(2,1)} %shard_map.104.ma_ref, bf16[5,1024,512]{2,1,0:T(8,128)(2,1)} %shard_map.105.mb_ref, ...), custom_call_target="tpu_custom_call" | custom-call | flops 6039797760 | bytes 12320768 | tf_op jit(solution)/shard_map/pallas_call | solution.py:230
  743.9 17.1 %shard_map.106 = (f32[1024,384]{1,0:T(8,128)}, f32[1024,384]{1,0:T(8,128)}) custom-call(s32[2]{0:T(128)} %pad_add_fusion.1.s_ref, f32[4,1024,128]{2,1,0:T(8,128)} %fusion.3.table_ref, bf16[5,1024,512]{2,1,0:T(8,128)(2,1)} %shard_map.104.ma_ref, bf16[5,1024,512]{2,1,0:T(8,128)(2,1)} %shard_map.105.mb_ref, bf16[10,512,384]{2,1,0:T(8,128)(2,1)} %wb_ref.3, ...), custom_call_target="tpu_custom_call" | custom-call | flops 6039797760 | bytes 12320768 | tf_op jit(solution)/shard_map/pallas_call | solution.py:230
  761.6 17.9 %shard_map.113 = (f32[1024,384]{1,0:T(8,128)}, f32[1024,384]{1,0:T(8,128)}) custom-call(s32[2]{0:T(128)} %broadcast_8_s_ref.2.s_ref, f32[4,1024,128]{2,1,0:T(8,128)} %fusion.3.table_ref, bf16[5,1024,512]{2,1,0:T(8,128)(2,1)} %shard_map.104.ma_ref, bf16[5,1024,512]{2,1,0:T(8,128)(2,1)} %shard_map.105.mb_ref, bf16[5,512,384]{2,1,0:T(8,128)(2,1)} %copy-done.11, ...), custom_call_target="tpu_custom_call" | custom-call | flops 6039797760 | bytes 15466496 | tf_op jit(solution)/shard_map/pallas_call | solution.py:230
  780.8 18.5 %shard_map.111 = (f32[1024,384]{1,0:T(8,128)}, f32[1024,384]{1,0:T(8,128)}) custom-call(s32[2]{0:T(128)} %broadcast_8_s_ref.2.s_ref, f32[4,1024,128]{2,1,0:T(8,128)} %fusion.3.table_ref, bf16[5,1024,512]{2,1,0:T(8,128)(2,1)} %shard_map.104.ma_ref, bf16[5,1024,512]{2,1,0:T(8,128)(2,1)} %shard_map.105.mb_ref, ...), custom_call_target="tpu_custom_call" | custom-call | flops 6039797760 | bytes 15466496 | tf_op jit(solution)/shard_map/pallas_call | solution.py:230
  800.0 18.0 %shard_map.109 = (f32[1024,384]{1,0:T(8,128)}, f32[1024,384]{1,0:T(8,128)}) custom-call(s32[2]{0:T(128)} %broadcast_8_s_ref.2.s_ref, f32[4,1024,128]{2,1,0:T(8,128)} %fusion.3.table_ref, bf16[5,1024,512]{2,1,0:T(8,128)(2,1)} %shard_map.104.ma_ref, bf16[5,1024,512]{2,1,0:T(8,128)(2,1)} %shard_map.105.mb_ref, ...), custom_call_target="tpu_custom_call" | custom-call | flops 6039797760 | bytes 15466496 | tf_op jit(solution)/shard_map/pallas_call | solution.py:230
  821.6 18.1 %shard_map.107 = (f32[1024,384]{1,0:T(8,128)}, f32[1024,384]{1,0:T(8,128)}) custom-call(s32[2]{0:T(128)} %pad_add_fusion.1.s_ref, f32[4,1024,128]{2,1,0:T(8,128)} %fusion.3.table_ref, bf16[5,1024,512]{2,1,0:T(8,128)(2,1)} %shard_map.104.ma_ref, bf16[5,1024,512]{2,1,0:T(8,128)(2,1)} %shard_map.105.mb_ref, bf16[10,512,384]{2,1,0:T(8,128)(2,1)} %wb_ref.3, ...), custom_call_target="tpu_custom_call" | custom-call | flops 6039797760 | bytes 15466496 | tf_op jit(solution)/shard_map/pallas_call | solution.py:230
  850.8 33.7 %collective-permute-done.36.refs_5_ = f32[1024,384]{1,0:T(8,128)} collective-permute-done((f32[1024,384]{1,0:T(8,128)}, f32[1024,384]{1,0:T(8,128)}, u32[]{:S(2)}, u32[]{:S(2)}) %collective-permute-start.36) | collective-permute-done | bytes 1572896 | tf_op jit(solution)/shard_map/ppermute | solution.py:348
  884.5 32.7 %collective-permute-done.35.refs_4_ = f32[1024,384]{1,0:T(8,128)S(1)} collective-permute-done((f32[1024,384]{1,0:T(8,128)}, f32[1024,384]{1,0:T(8,128)S(1)}, u32[]{:S(2)}, u32[]{:S(2)}) %collective-permute-start.35) | collective-permute-done | bytes 1572896 | tf_op jit(solution)/shard_map/ppermute | solution.py:348
  (136 shorter events, 162.7 us)
Async XLA Ops:
  6.5 119.5 %all-gather.3.cloned.1.call-start = ((), (), s32[]{:S(2)}) async-start(), calls=%async_computation | async-start | bytes 8355840 | tf_op jit(solution)/shard_map/all_gather | solution.py:301
  8.7 179.2 %all-gather.5.cloned.1.call-start = ((), (), s32[]{:S(2)}) async-start(), calls=%async_computation.1 | async-start | bytes 5013504 | tf_op jit(solution)/shard_map/all_gather | solution.py:302
  23.8 177.1 %collective-permute-start.9 = (bf16[5,384,512]{2,1,0:T(8,128)(2,1)}, bf16[5,384,512]{2,1,0:T(8,128)(2,1)}, u32[]{:S(2)}, u32[]{:S(2)}) collective-permute-start(bf16[5,384,512]{2,1,0:T(8,128)(2,1)} %constant_dynamic-slice_fusion.2), channel_id=1, source_target_pairs={{0,4},{4,8},{8,12},{12,0},{1,5},{5,9},{9,13},{13,1},{2,6},{6,10},{... | collective-permute-start | bytes 5898248 | tf_op jit(solution)/shard_map/ppermute | solution.py:296
  25.4 176.5 %collective-permute-start.12 = (bf16[5,384,512]{2,1,0:T(8,128)(2,1)}, bf16[5,384,512]{2,1,0:T(8,128)(2,1)}, u32[]{:S(2)}, u32[]{:S(2)}) collective-permute-start(bf16[5,384,512]{2,1,0:T(8,128)(2,1)} %constant_dynamic-slice_fusion.1), channel_id=1, source_target_pairs={{0,4},{4,8},{8,12},{12,0},{1,5},{5,9},{9,13},{13,1},{2,6},{6,10},{... | collective-permute-start | bytes 5898248 | tf_op jit(solution)/shard_map/ppermute | solution.py:296
  198.6 90.7 %collective-permute-start.6 = (bf16[1024,1536]{1,0:T(8,128)(2,1)}, bf16[1024,1536]{1,0:T(8,128)(2,1)}, u32[]{:S(2)}, u32[]{:S(2)}) collective-permute-start(bf16[1024,1536]{1,0:T(8,128)(2,1)} %get-tuple-element.30.rows_ref), channel_id=1, source_target_pairs={{0,2},{1,3},{2,0},{3,1},{4,6},{5,7},{6,4},{7,5},{8,10},{9,11},{10,... | collective-permute-start | bytes 9437192 | tf_op jit(solution)/shard_map/ppermute | solution.py:324
  200.9 88.4 %collective-permute-start.10 = (bf16[5,384,512]{2,1,0:T(8,128)(2,1)}, bf16[5,384,512]{2,1,0:T(8,128)(2,1)}, u32[]{:S(2)}, u32[]{:S(2)}) collective-permute-start(bf16[5,384,512]{2,1,0:T(8,128)(2,1)} %collective-permute-done.9.refs_1_), channel_id=1, source_target_pairs={{0,4},{4,8},{8,12},{12,0},{1,5},{5,9},{9,13},{13,1},{2,6},{6,10},{... | collective-permute-start | bytes 5898248 | tf_op jit(solution)/shard_map/ppermute | solution.py:296
  201.8 184.1 %collective-permute-start.8 = (bf16[1024,1536]{1,0:T(8,128)(2,1)}, bf16[1024,1536]{1,0:T(8,128)(2,1)}, u32[]{:S(2)}, u32[]{:S(2)}) collective-permute-start(bf16[1024,1536]{1,0:T(8,128)(2,1)} %get-tuple-element.30.rows_ref), channel_id=1, source_target_pairs={{0,1},{1,0},{2,3},{3,2},{4,5},{5,4},{6,7},{7,6},{8,9},{9,8},{10,11... | collective-permute-start | bytes 9437192 | tf_op jit(solution)/shard_map/ppermute | solution.py:325
  201.8 129.6 %collective-permute-start.13 = (bf16[5,384,512]{2,1,0:T(8,128)(2,1)}, bf16[5,384,512]{2,1,0:T(8,128)(2,1)}, u32[]{:S(2)}, u32[]{:S(2)}) collective-permute-start(bf16[5,384,512]{2,1,0:T(8,128)(2,1)} %collective-permute-done.12.refs_5_), channel_id=1, source_target_pairs={{0,4},{4,8},{8,12},{12,0},{1,5},{5,9},{9,13},{13,1},{2,6},{6,10},{... | collective-permute-start | bytes 5898248 | tf_op jit(solution)/shard_map/ppermute | solution.py:296
  247.2 85.7 %collective-permute-start.15 = (bf16[5,384,512]{2,1,0:T(8,128)(2,1)}, bf16[5,384,512]{2,1,0:T(8,128)(2,1)}, u32[]{:S(2)}, u32[]{:S(2)}) collective-permute-start(bf16[5,384,512]{2,1,0:T(8,128)(2,1)} %collective-permute-done.9.refs_1_), channel_id=1, source_target_pairs={{0,16},{16,0},{1,17},{17,1},{2,18},{18,2},{3,19},{19,3},{4,20},{20... | collective-permute-start | bytes 5898248 | tf_op jit(solution)/shard_map/ppermute | solution.py:298
  289.3 84.3 %collective-permute-start.27 = (bf16[5,512,384]{2,1,0:T(8,128)(2,1)}, bf16[5,512,384]{2,1,0:T(8,128)(2,1)}, u32[]{:S(2)}, u32[]{:S(2)}) collective-permute-start(bf16[5,512,384]{2,1,0:T(8,128)(2,1)} %collective-permute-done.23.wa_ref), channel_id=1, source_target_pairs={{0,4},{4,8},{8,12},{12,0},{1,5},{5,9},{9,13},{13,1},{2,6},{6,10},{... | collective-permute-start | bytes 5898248 | tf_op jit(solution)/shard_map/ppermute | solution.py:296
  289.3 170.0 %collective-permute-start.7 = (bf16[1024,1536]{1,0:T(8,128)(2,1)}, bf16[1024,1536]{1,0:T(8,128)(2,1)}, u32[]{:S(2)}, u32[]{:S(2)}) collective-permute-start(bf16[1024,1536]{1,0:T(8,128)(2,1)} %collective-permute-done.6.rows_ref), channel_id=1, source_target_pairs={{0,1},{1,0},{2,3},{3,2},{4,5},{5,4},{6,7},{7,6},{8,9},{9,8},{10,11... | collective-permute-start | bytes 9437192 | tf_op jit(solution)/shard_map/ppermute | solution.py:326
  331.5 79.8 %collective-permute-start.18 = (bf16[5,384,512]{2,1,0:T(8,128)(2,1)}, bf16[5,384,512]{2,1,0:T(8,128)(2,1)S(1)}, u32[]{:S(2)}, u32[]{:S(2)}) collective-permute-start(bf16[5,384,512]{2,1,0:T(8,128)(2,1)} %collective-permute-done.12.refs_5_), channel_id=1, source_target_pairs={{0,16},{16,0},{1,17},{17,1},{2,18},{18,2},{3,19},{19,3},{4,20},{20... | collective-permute-start | bytes 5898248 | tf_op jit(solution)/shard_map/ppermute | solution.py:298
  333.0 82.8 %collective-permute-start.11 = (bf16[5,384,512]{2,1,0:T(8,128)(2,1)}, bf16[5,384,512]{2,1,0:T(8,128)(2,1)}, u32[]{:S(2)}, u32[]{:S(2)}) collective-permute-start(bf16[5,384,512]{2,1,0:T(8,128)(2,1)} %collective-permute-done.10.refs_2_), channel_id=1, source_target_pairs={{0,4},{4,8},{8,12},{12,0},{1,5},{5,9},{9,13},{13,1},{2,6},{6,10},{... | collective-permute-start | bytes 5898248 | tf_op jit(solution)/shard_map/ppermute | solution.py:296
  373.6 84.3 %collective-permute-start.14 = (bf16[5,384,512]{2,1,0:T(8,128)(2,1)}, bf16[5,384,512]{2,1,0:T(8,128)(2,1)}, u32[]{:S(2)}, u32[]{:S(2)}) collective-permute-start(bf16[5,384,512]{2,1,0:T(8,128)(2,1)} %collective-permute-done.13.refs_6_), channel_id=1, source_target_pairs={{0,4},{4,8},{8,12},{12,0},{1,5},{5,9},{9,13},{13,1},{2,6},{6,10},{... | collective-permute-start | bytes 5898248 | tf_op jit(solution)/shard_map/ppermute | solution.py:296
  385.9 113.0 %collective-permute-start.31 = (bf16[5,512,384]{2,1,0:T(8,128)(2,1)}, bf16[5,512,384]{2,1,0:T(8,128)(2,1)S(1)}, u32[]{:S(2)}, u32[]{:S(2)}) collective-permute-start(bf16[5,512,384]{2,1,0:T(8,128)(2,1)} %collective-permute-done.27.wa_ref), channel_id=1, source_target_pairs={{0,4},{4,8},{8,12},{12,0},{1,5},{5,9},{9,13},{13,1},{2,6},{6,10},{... | collective-permute-start | bytes 5898248 | tf_op jit(solution)/shard_map/ppermute | solution.py:296
  411.3 111.4 %collective-permute-start.16 = (bf16[5,384,512]{2,1,0:T(8,128)(2,1)}, bf16[5,384,512]{2,1,0:T(8,128)(2,1)}, u32[]{:S(2)}, u32[]{:S(2)}) collective-permute-start(bf16[5,384,512]{2,1,0:T(8,128)(2,1)} %collective-permute-done.10.refs_2_), channel_id=1, source_target_pairs={{0,16},{16,0},{1,17},{17,1},{2,18},{18,2},{3,19},{19,3},{4,20},{20... | collective-permute-start | bytes 5898248 | tf_op jit(solution)/shard_map/ppermute | solution.py:298
  415.7 107.5 %collective-permute-start.19 = (bf16[5,384,512]{2,1,0:T(8,128)(2,1)}, bf16[5,384,512]{2,1,0:T(8,128)(2,1)}, u32[]{:S(2)}, u32[]{:S(2)}) collective-permute-start(bf16[5,384,512]{2,1,0:T(8,128)(2,1)} %collective-permute-done.13.refs_6_), channel_id=1, source_target_pairs={{0,16},{16,0},{1,17},{17,1},{2,18},{18,2},{3,19},{19,3},{4,20},{20... | collective-permute-start | bytes 5898248 | tf_op jit(solution)/shard_map/ppermute | solution.py:298
  457.9 83.7 %collective-permute-start.17 = (bf16[5,384,512]{2,1,0:T(8,128)(2,1)}, bf16[5,384,512]{2,1,0:T(8,128)(2,1)}, u32[]{:S(2)}, u32[]{:S(2)}) collective-permute-start(bf16[5,384,512]{2,1,0:T(8,128)(2,1)} %collective-permute-done.11.refs_3_), channel_id=1, source_target_pairs={{0,16},{16,0},{1,17},{17,1},{2,18},{18,2},{3,19},{19,3},{4,20},{20... | collective-permute-start | bytes 5898248 | tf_op jit(solution)/shard_map/ppermute | solution.py:298
  459.3 124.3 %collective-permute-start.20 = (bf16[5,384,512]{2,1,0:T(8,128)(2,1)}, bf16[5,384,512]{2,1,0:T(8,128)(2,1)}, u32[]{:S(2)}, u32[]{:S(2)}) collective-permute-start(bf16[5,384,512]{2,1,0:T(8,128)(2,1)} %collective-permute-done.14.refs_7_), channel_id=1, source_target_pairs={{0,16},{16,0},{1,17},{17,1},{2,18},{18,2},{3,19},{19,3},{4,20},{20... | collective-permute-start | bytes 5898248 | tf_op jit(solution)/shard_map/ppermute | solution.py:298
  498.9 126.9 %collective-permute-start.32 = (bf16[5,512,384]{2,1,0:T(8,128)(2,1)S(1)}, bf16[5,512,384]{2,1,0:T(8,128)(2,1)}, u32[]{:S(2)}, u32[]{:S(2)}) collective-permute-start(bf16[5,512,384]{2,1,0:T(8,128)(2,1)S(1)} %collective-permute-done.31.wa_ref), channel_id=1, source_target_pairs={{0,16},{16,0},{1,17},{17,1},{2,18},{18,2},{3,19},{19,3},{4,20},{20... | collective-permute-start | bytes 5898248 | tf_op jit(solution)/shard_map/ppermute | solution.py:298
  522.7 202.5 %collective-permute-start.24 = (bf16[5,512,384]{2,1,0:T(8,128)(2,1)}, bf16[5,512,384]{2,1,0:T(8,128)(2,1)S(1)}, u32[]{:S(2)}, u32[]{:S(2)}) collective-permute-start(bf16[5,512,384]{2,1,0:T(8,128)(2,1)} %collective-permute-done.23.wa_ref), channel_id=1, source_target_pairs={{0,16},{16,0},{1,17},{17,1},{2,18},{18,2},{3,19},{19,3},{4,20},{20... | collective-permute-start | bytes 5898248 | tf_op jit(solution)/shard_map/ppermute | solution.py:298
  523.3 183.5 %collective-permute-start.28 = (bf16[5,512,384]{2,1,0:T(8,128)(2,1)}, bf16[5,512,384]{2,1,0:T(8,128)(2,1)}, u32[]{:S(2)}, u32[]{:S(2)}) collective-permute-start(bf16[5,512,384]{2,1,0:T(8,128)(2,1)} %collective-permute-done.27.wa_ref), channel_id=1, source_target_pairs={{0,16},{16,0},{1,17},{17,1},{2,18},{18,2},{3,19},{19,3},{4,20},{20... | collective-permute-start | bytes 5898248 | tf_op jit(solution)/shard_map/ppermute | solution.py:298
  643.3 100.0 %collective-permute-start.33 = (f32[1024,384]{1,0:T(8,128)}, f32[1024,384]{1,0:T(8,128)S(1)}, u32[]{:S(2)}, u32[]{:S(2)}) collective-permute-start(f32[1024,384]{1,0:T(8,128)} %get-tuple-element.40), channel_id=1, source_target_pairs={{0,1},{1,0},{2,3},{3,2},{4,5},{5,4},{6,7},{7,6},{8,9},{9,8},{10,11... | collective-permute-start | bytes 4718600 | tf_op jit(solution)/shard_map/ppermute | solution.py:345
  643.3 117.7 %collective-permute-start.34 = (f32[1024,384]{1,0:T(8,128)}, f32[1024,384]{1,0:T(8,128)}, u32[]{:S(2)}, u32[]{:S(2)}) collective-permute-start(f32[1024,384]{1,0:T(8,128)} %get-tuple-element.41), channel_id=1, source_target_pairs={{0,1},{1,0},{2,3},{3,2},{4,5},{5,4},{6,7},{7,6},{8,9},{9,8},{10,11... | collective-permute-start | bytes 4718600 | tf_op jit(solution)/shard_map/ppermute | solution.py:345
  (32 other events, 1001.1 us)
Sparse Core Ops, SparseCore 0:
  9.6 116.3 all-gather.2
  128.3 59.4 all-gather.4

commit v2 on v1

--- a/solution.py
+++ b/solution.py
@@ -13,6 +13,100 @@
 F32 = jnp.float32
 BF16 = jnp.bfloat16
 VMEM_LIMIT = 58 * 1024 * 1024
+
+
+def gather_kernel(names, sizes, q_ref, o_ref, g_ref, wq_ref, wo_ref, g1_ref, send, recv, extra, local):
+    rep, data, expert = (lax.axis_index(n) for n in names)
+    steps, sources = sizes
+    after = lax.rem(data + 1, steps)
+    across = lax.rem(expert + 2, sources)
+    mate = expert + 1 - 2 * lax.rem(expert, 2)
+    pairs = ((q_ref, wq_ref), (o_ref, wo_ref))
+    share = q_ref.shape[0]
+    half = share // 2
+    right, twin, far, peer = {names[1]: after}, {names[0]: 1 - rep}, {names[2]: across}, {names[2]: mate}
+
+    def block(w, t, e, h):
+        d = lax.rem(data + steps - t, steps)
+        return pairs[w][1].at[pl.ds(pl.multiple_of((d * sources + e) * share + h * half, 16), half), :]
+
+    def whole(w, e):
+        return pairs[w][1].at[pl.ds(pl.multiple_of((data * sources + e) * share, 16), share), :]
+
+    def copy(w, j, src, dst, dev):
+        return pltpu.make_async_remote_copy(src_ref=src, dst_ref=dst, send_sem=send.at[w, j], recv_sem=recv.at[w, j], device_id=dev, device_id_type=pl.DeviceIdType.MESH)
+
+    jobs = {}
+    keep = []
+    for w, (own, full) in enumerate(pairs):
+        mine = own.at[pl.ds(pl.multiple_of(rep * half, 16), half), :]
+        keep.append(pltpu.make_async_copy(own, whole(w, expert), local.at[w]))
+        jobs[w, 6] = copy(w, 6, own, whole(w, expert), far)
+        jobs[w, 13] = copy(w, 13, own, whole(w, expert), peer)
+        jobs[w, 20] = copy(w, 20, whole(w, across), whole(w, across), peer)
+        for t in range(1, steps):
+            i = t - 1
+            z_src = mine if t == 1 else block(w, i, expert, rep)
+            jobs[w, i] = copy(w, i, z_src, block(w, i, expert, rep), right)
+            near, other = block(w, t, expert, rep), block(w, t, expert, 1 - rep)
+            y_near, y_other = block(w, t, across, rep), block(w, t, across, 1 - rep)
+            jobs[w, 3 + i] = copy(w, 3 + i, near, near, twin)
+            jobs[w, 7 + i] = copy(w, 7 + i, near, near, far)
+            jobs[w, 10 + i] = copy(w, 10 + i, y_near, y_near, twin)
+            for j, b in ((14, near), (17, other), (21, y_near), (24, y_other)):
+                jobs[w, j + i] = copy(w, j + i, b, b, peer)
+    experts = g1_ref.shape[0]
+    big = pltpu.make_async_remote_copy(src_ref=g_ref.at[pl.ds(rep * experts, experts)], dst_ref=g1_ref, send_sem=extra.at[0], recv_sem=extra.at[1],
+                                       device_id=right, device_id_type=pl.DeviceIdType.MESH)
+
+    def pass_on(arrived, *then):
+        for w in range(2):
+            jobs[w, arrived].wait_recv()
+            for j in then:
+                jobs[w, j].start()
+
+    for w in range(2):
+        for j in (0, 6, 13):
+            jobs[w, j].start()
+        keep[w].start()
+    for i in range(3):
+        pass_on(i, *(((i + 1,) if i < 2 else ()) + (3 + i, 7 + i, 14 + i)))
+        if i == 2:
+            big.start()
+        if i == 0:
+            pass_on(6, 20)
+        else:
+            pass_on(7 + i - 1, 10 + i - 1, 21 + i - 1)
+            pass_on(3 + i - 1, 17 + i - 1)
+    pass_on(9, 12, 23)
+    pass_on(5, 19)
+    for i in range(3):
+        pass_on(10 + i, 24 + i)
+    for j in (13, 14, 15, 16, 17, 18, 19, 20, 21, 22, 23, 24, 25, 26):
+        for w in range(2):
+            jobs[w, j].wait_recv()
+    for w in range(2):
+        for j in range(27):
+            jobs[w, j].wait_send()
+        keep[w].wait()
+    big.wait()
+
+
+def gather_attn(names, sizes, q_part, o_part, gate_part):
+    group = sizes[0] * sizes[1]
+    experts = gate_part.shape[0] // 2
+    hbm = pl.BlockSpec(memory_space=pl.ANY)
+    vmem = pl.BlockSpec(memory_space=pltpu.VMEM)
+    full = lambda a: jax.ShapeDtypeStruct((group * a.shape[0], a.shape[1]), a.dtype)
+    moved = 2 * group * q_part.shape[0] * (q_part.shape[1] + o_part.shape[1])
+    return pl.pallas_call(
+        functools.partial(gather_kernel, names, sizes), name="gather_attn",
+        in_specs=[vmem, vmem, hbm], out_specs=[hbm] * 3,
+        out_shape=[full(q_part), full(o_part), jax.ShapeDtypeStruct((experts,) + gate_part.shape[1:], gate_part.dtype)],
+        scratch_shapes=[pltpu.SemaphoreType.DMA((2, 27)), pltpu.SemaphoreType.DMA((2, 27)), pltpu.SemaphoreType.DMA((2,)), pltpu.SemaphoreType.DMA((2,))],
+        cost_estimate=pl.CostEstimate(flops=60_000_000_000, bytes_accessed=moved, transcendentals=0),
+        compiler_params=pltpu.CompilerParams(has_side_effects=True),
+    )(q_part, o_part, gate_part)
 
 
 def qkv_kernel(rope_cols, half_dim, x_ref, gain_ref, w_ref, cos_ref, sin_ref, o_ref):
@@ -47,7 +141,8 @@
     )(x, gain, w_qkv, cos_t, sin_t)
 
 
-def attend_kernel(group_len, head_dim, q_ref, k_ref, v_ref, o_ref):
+def attend_kernel(group_len, head_dim, q_ref, k_ref, v_ref, *rest):
+    o_ref = rest[-1]
     seq_len = q_ref.shape[0]
     tile = 256
     scale = head_dim ** -0.5 * 1.4426950408889634
@@ -67,7 +162,7 @@
                 o_ref[r:seen, c:c + head_dim] = jnp.dot(probs, vals[:seen], preferred_element_type=F32).astype(BF16)
 
 
-def attend(qkv, seq_len, num_heads, kv_heads, head_dim):
+def attend(qkv, seq, out, seq_len, num_heads, kv_heads, head_dim):
     toks = qkv.shape[0]
     group_len = num_heads // kv_heads
     pair = 128 // head_dim
@@ -75,14 +170,15 @@
     kcol0 = num_heads * head_dim // 128
     vcol0 = (num_heads + kv_heads) * head_dim // 128
     return pl.pallas_call(
-        functools.partial(attend_kernel, group_len, head_dim), name="k_attn", grid=(toks // seq_len, kv_heads // pair),
-        in_specs=[pl.BlockSpec((seq_len, qcols), lambda s, j: (s, j)), pl.BlockSpec((seq_len, 128), lambda s, j: (s, kcol0 + j)),
-                  pl.BlockSpec((seq_len, 128), lambda s, j: (s, vcol0 + j))],
-        out_specs=pl.BlockSpec((seq_len, qcols), lambda s, j: (s, j)),
+        functools.partial(attend_kernel, group_len, head_dim), grid=(kv_heads // pair,),
+        in_specs=[pl.BlockSpec((seq_len, qcols), lambda j: (seq, j)), pl.BlockSpec((seq_len, 128), lambda j: (seq, kcol0 + j)),
+                  pl.BlockSpec((seq_len, 128), lambda j: (seq, vcol0 + j))] + ([] if out is None else [pl.BlockSpec(memory_space=pl.ANY)]),
+        out_specs=pl.BlockSpec((seq_len, qcols), lambda j: (seq, j)),
+        input_output_aliases={} if out is None else {3: 0},
         out_shape=jax.ShapeDtypeStruct((toks, num_heads * head_dim), BF16),
-        cost_estimate=pl.CostEstimate(flops=16 * toks * seq_len * num_heads * head_dim, bytes_accessed=2 * toks * (qkv.shape[1] + num_heads * head_dim), transcendentals=toks * seq_len * num_heads),
-        compiler_params=pltpu.CompilerParams(vmem_limit_bytes=VMEM_LIMIT),
-    )(qkv, qkv, qkv)
+        cost_estimate=pl.CostEstimate(flops=16 * seq_len * seq_len * num_heads * head_dim, bytes_accessed=2 * seq_len * (qkv.shape[1] + num_heads * head_dim), transcendentals=seq_len * seq_len * num_heads),
+        compiler_params=pltpu.CompilerParams(vmem_limit_bytes=VMEM_LIMIT),
+    )(qkv, qkv, qkv, *(() if out is None else (out,)))
 
 
 def project_kernel(a_ref, w_ref, x_ref, gain_ref, h_ref, z_ref):
@@ -119,7 +215,9 @@
     sin_t = jnp.concatenate([-sin_t, sin_t] * (64 // half_dim), axis=1)
     x = seqs.reshape(num_seqs * seq_len, width)
     qkv = qkv_project(x, attn_gain.reshape(1, width), w_qkv, cos_t, sin_t, (num_heads + kv_heads) * head_dim, half_dim)
-    mixed = attend(qkv, seq_len, num_heads, kv_heads, head_dim)
+    mixed = None
+    for seq in range(num_seqs):
+        mixed = attend(qkv, seq, mixed, seq_len, num_heads, kv_heads, head_dim)
     return project(mixed, w_out_t, x, moe_gain.reshape(1, width))
 
 
@@ -194,79 +292,110 @@
     )(scal, x, *gates, *ups)
 
 
-def combine_kernel(half, adds, s_ref, table_ref, ma_ref, mb_ref, wa_ref, wb_ref, *refs):
+def combine_kernel(count, experts, halves, chunks, cuts, adds, s_ref, *refs):
+    refs = list(refs)
+    take = lambda n: [refs.pop(0) for _ in range(n)]
+    tables, mids = take(count), [take(count) for _ in halves]
+    parts = [[take(len(cuts[t])) for t in range(chunks)] for _ in halves]
+    added = [take(adds) for _ in range(count)]
+    outs, (w_ref,) = take(count), take(1)
+    i = pl.program_id(0)
+    cols = parts[0][0][0].shape[2]
+    spots = [pl.ds(0, cols)] if chunks == 1 else [pl.ds(pl.multiple_of(lax.rem(s_ref[1] + chunks - t, chunks) * cols, 128), cols) for t in range(chunks)]
+    plain = chunks == 1 and len(cuts[0]) == 1
+    if not plain:
+        for j in range(len(halves)):
+            for t in range(chunks):
+                for piece, (start, size) in zip(parts[j][t], cuts[t]):
+                    @pl.when((i >= start) & (i < start + size))
+                    def _(j=j, t=t, piece=piece):
+                        w_ref[j, :, spots[t]] = piece[0]
+    toks, cap = tables[0].shape[1], mids[0][0].shape[1]
+    slots = lax.broadcasted_iota(jnp.int32, (toks, cap), 1).astype(F32)
+    for n in range(count):
+        @pl.when(i == 0)
+        def _(n=n):
+            if chunks > 1:
+                for t in range(adds):
+                    outs[n][:, spots[t]] = added[n][t][...]
+            elif adds:
+                outs[n][...] = added[n][0][...] if adds == 1 else added[n][0][...] + added[n][1][...]
+            else:
+                outs[n][...] = jnp.zeros(outs[n].shape, F32)
+
+        table = pltpu.roll(tables[n][0], lax.rem(128 - i, 128), 1)
+        total = None
+        for j, h in enumerate(halves):
+            e = h * (experts // 2)
+            w = parts[j][0][0][0] if plain else w_ref[j]
+            o = jnp.dot(mids[j][n][0], w, preferred_element_type=F32).astype(BF16)
+            hot = jnp.where(slots == table[:, e:e + 1], 1.0, 0.0).astype(BF16)
+            picked = jnp.dot(hot, o, preferred_element_type=F32) * table[:, experts + e:experts + e + 1]
+            total = picked if total is None else total + picked
+        outs[n][...] += total
+
+
+def combine(scal, table, ks, groups, adds):
+    sources, toks, lanes = table.shape
+    half, rows, ff = groups[0][1].shape
+    cap = rows // sources
+    halves = [h for h, _, _ in groups]
+    chunks, count = len(groups[0][2]), len(ks)
+    cols = groups[0][2][0][0][0].shape[2]
+    cuts = [[(start, size) for _, start, size in pieces] for pieces in groups[0][2]]
+    table_spec = lambda k: pl.BlockSpec((1, toks, lanes), lambda i, s: (k, 0, 0))
+    mid_spec = lambda k: pl.BlockSpec((1, cap, ff), lambda i, s: (i, k, 0))
+
+    def piece_spec(array, start, size, h):
+        if array.shape[0] > half:
+            index = lambda i, s: (lax.rem(i + h * half + s[0], 2 * half), 0, 0)
+        else:
+            index = lambda i, s: (jnp.clip(i - start, 0, size - 1), 0, 0)
+        return pl.BlockSpec((1, ff, cols), index)
+
+    flat = [(h, p) for h, _, group in groups for pieces in group for p in pieces]
+    whole = pl.BlockSpec((toks, cols * chunks), lambda i, s: (0, 0))
+    single = pl.BlockSpec((toks, cols), lambda i, s: (0, 0))
+    flat_adds = [a for group in adds for a in group]
+    flops = count * 2 * half * len(halves) * cap * cols * chunks * (ff + toks)
+    return pl.pallas_call(
+        functools.partial(combine_kernel, count, 2 * half, halves, chunks, cuts, len(adds[0])),
+        grid_spec=pltpu.PrefetchScalarGridSpec(
+            num_scalar_prefetch=1, grid=(half,),
+            in_specs=[table_spec(k) for k in ks] + [mid_spec(k) for _ in groups for k in ks] + [piece_spec(*p, h) for h, p in flat] + [single] * len(flat_adds),
+            out_specs=[whole] * count,
+            scratch_shapes=[pltpu.VMEM((len(halves), ff, cols * chunks), BF16)]),
+        out_shape=[jax.ShapeDtypeStruct((toks, cols * chunks), F32)] * count,
+        cost_estimate=pl.CostEstimate(flops=flops, bytes_accessed=2 * len(halves) * half * ff * cols * chunks + count * 8 * toks * cols * chunks, transcendentals=0),
+        compiler_params=pltpu.CompilerParams(vmem_limit_bytes=VMEM_LIMIT),
+    )(scal, *[table] * count, *[m for _, m, _ in groups for _ in ks], *[p[0] for _, p in flat], *flat_adds)
+
+
+def finish_kernel(s_ref, h_ref, own_ref, far_ref, *refs):
     del s_ref
-    add_refs, (o0_ref, o1_ref, acc_ref) = refs[:adds], refs[adds:]
-    g = pl.program_id(0)
-    toks, cap = table_ref.shape[1], ma_ref.shape[1]
-    table = table_ref[0]
-    slots = lax.broadcasted_iota(jnp.int32, (toks, cap), 1).astype(F32)
-    for e in range(2 * half):
-        m_ref, w_ref, i = (ma_ref, wa_ref, e) if e < half else (mb_ref, wb_ref, e - half)
-        o = jnp.dot(m_ref[i], w_ref[i], preferred_element_type=F32).astype(BF16)
-        hot = jnp.where(slots == table[:, e:e + 1], 1.0, 0.0).astype(BF16)
-        picked = jnp.dot(hot, o, preferred_element_type=F32) * table[:, 2 * half + e:2 * half + e + 1]
-        if e == 0:
-            acc_ref[...] = picked
-        else:
-            acc_ref[...] += picked
-
-    @pl.when(g == 0)
-    def _():
-        o0_ref[...] = acc_ref[...] + add_refs[0][...] if adds else acc_ref[...]
-
-    @pl.when(g == 1)
-    def _():
-        o1_ref[...] = acc_ref[...] + add_refs[1][...] if adds else acc_ref[...]
-
-
-def combine(scal, table, first, stride, mids, downs, adds):
-    sources, toks, lanes = table.shape
-    half, rows, ff = mids[0].shape
-    cap = rows // sources
-    cols = downs[0].shape[2]
-    src = lambda g: first + stride * g
-    whole = pl.BlockSpec((toks, cols), lambda g, s: (0, 0))
-    return pl.pallas_call(
-        functools.partial(combine_kernel, half, len(adds)),
-        grid_spec=pltpu.PrefetchScalarGridSpec(
-            num_scalar_prefetch=1, grid=(2,),
-            in_specs=[pl.BlockSpec((1, toks, lanes), lambda g, s: (src(g), 0, 0)),
-                      pl.BlockSpec((half, cap, ff), lambda g, s: (0, src(g), 0)),
-                      pl.BlockSpec((half, cap, ff), lambda g, s: (0, src(g), 0)),
-                      pl.BlockSpec((half, ff, cols), lambda g, s: (s[0], 0, 0)),
-                      pl.BlockSpec((half, ff, cols), lambda g, s: (s[1], 0, 0))] + [whole] * len(adds),
-            out_specs=[whole, whole],
-            scratch_shapes=[pltpu.VMEM((toks, cols), F32)]),
-        out_shape=[jax.ShapeDtypeStruct((toks, cols), F32)] * 2,
-        cost_estimate=pl.CostEstimate(flops=2 * 2 * half * 2 * cap * cols * (ff + toks), bytes_accessed=2 * 2 * half * (ff * cols + 2 * cap * ff) + 8 * toks * cols * (1 + len(adds) // 2), transcendentals=0),
-        compiler_params=pltpu.CompilerParams(vmem_limit_bytes=VMEM_LIMIT),
-    )(scal, table, *mids, *downs, *adds)
-
-
-def finish_kernel(steps, s_ref, h_ref, *refs):
-    own, far, y_ref = refs[:steps], refs[steps:2 * steps], refs[2 * steps]
-    cols = own[0].shape[1]
-    for t in range(steps):
-        at = pl.ds(pl.multiple_of(lax.rem(s_ref[0] + steps - t, steps) * cols, 128), cols)
-        y_ref[:, at] = (h_ref[:, at].astype(F32) + (own[t][...] + far[t][...])).astype(BF16)
-
-
-def finish(scal, hidden, own, far):
+    refs[-1][...] = (h_ref[...].astype(F32) + (own_ref[...] + far_ref[...])).astype(BF16)
+
+
+def finish(scal, hidden, own, far, out):
     toks, width = hidden.shape
-    cols = own[0].shape[1]
-    tile = 256
-    wide = pl.BlockSpec((tile, width), lambda i, s: (i, 0))
+    cols = far.shape[1]
+    tile = toks // 2
+    wide = pl.BlockSpec((tile, cols), lambda i, s: (i, s[0]))
     part = pl.BlockSpec((tile, cols), lambda i, s: (i, 0))
     return pl.pallas_call(
-        functools.partial(finish_kernel, len(own)), name="finish",
+        finish_kernel,
         grid_spec=pltpu.PrefetchScalarGridSpec(
             num_scalar_prefetch=1, grid=(toks // tile,),
-            in_specs=[wide] + [part] * (2 * len(own)), out_specs=wide),
+            in_specs=[wide, wide, part] + ([] if out is None else [pl.BlockSpec(memory_space=pl.ANY)]), out_specs=wide),
         out_shape=jax.ShapeDtypeStruct((toks, width), BF16),
-        cost_estimate=pl.CostEstimate(flops=2 * toks * width, bytes_accessed=12 * toks * width, transcendentals=0),
-        compiler_params=pltpu.CompilerParams(vmem_limit_bytes=VMEM_LIMIT),
-    )(scal, hidden, *own, *far)
+        input_output_aliases={} if out is None else {4: 0},
+        cost_estimate=pl.CostEstimate(flops=2 * toks * cols, bytes_accessed=12 * toks * cols, transcendentals=0),
+        compiler_params=pltpu.CompilerParams(vmem_limit_bytes=VMEM_LIMIT),
+    )(scal, hidden, own, far, *(() if out is None else (out,)))
+
+
+def perm(value, axis, pairs):
+    return lax.ppermute(value, axis, pairs)
 
 
 def solution(mesh):
@@ -289,20 +418,29 @@
         heads_all, head_dim = qkv_part.shape[1:]
         num_heads = out_part.shape[0]
 
-        def pieces(w):
-            mine = lax.dynamic_slice_in_dim(w, rep * half, half, 0)
+        def pieces(tag, w, mine=None):
             near, far = [], []
-            for _ in range(1, steps):
-                mine = lax.ppermute(mine, 'data', ring)
+            for t in range(1, steps if tag != 'd' else steps - 1):
+                if t > 1 or mine is None:
+                    mine = perm(lax.dynamic_slice_in_dim(w, rep * half, half, 0) if mine is None else mine, 'data', ring)
                 near.append(mine)
-                far.append(lax.ppermute(mine, 'rep', swap))
+                far.append(perm(mine, 'rep', swap))
             return near, far
 
-        w_qkv = lax.all_gather(qkv_part.reshape(qkv_part.shape[0], heads_all * head_dim), group_axes, axis=0, tiled=True)
-        w_out_t = lax.all_gather(out_part.reshape(num_heads * head_dim, -1).T, group_axes, axis=0, tiled=True)
-        g_near, g_far = pieces(gate_part)
-        u_near, u_far = pieces(up_part)
-        d_near, d_far = pieces(down_part)
+        w_qkv, w_out_t, g_first = gather_attn(mesh.axis_names, (steps, sources), qkv_part.reshape(qkv_part.shape[0], heads_all * head_dim),
+                                              out_part.reshape(num_heads * head_dim, -1).T, gate_part)
+        g_near, g_far = pieces('g', gate_part, g_first)
+        u_near, u_far = pieces('u', up_part)
+        d_near, d_far = pieces('d', down_part)
+        whole_piece = lambda a: [(a, 0, half)]
+        d_near, d_far = [whole_piece(a) for a in d_near], [whole_piece(a) for a in d_far]
+        last_near, last_far = [], []
+        cut = half - half // 2
+        for start, stop in ((0, cut), (cut, half)):
+            moved = perm(d_near[-1][0][0][start:stop], 'data', ring)
+            last_near.append((moved, start, stop - start))
+            last_far.append((perm(moved, 'rep', swap), start, stop - start))
+        d_near, d_far = [whole_piece(down_part)] + d_near + [last_near], [whole_piece(down_part)] + d_far + [last_far]
 
         idx_t = idx_loc.reshape(toks, top_k).T
         gate_t = gate_loc.reshape(toks, top_k).T
@@ -321,9 +459,9 @@
 
         attn_gain, rank_rows, table = lax.optimization_barrier((attn_gain, rank_rows, table))
         hidden, normed = attention_block(x_loc, attn_gain, w_qkv, w_out_t, num_heads, (heads_all - num_heads) // 2, head_dim, moe_gain)
-        z_y = lax.ppermute(normed, 'expert', flip[2])
-        z_c = lax.ppermute(normed, 'expert', flip[1])
-        z_yc = lax.ppermute(z_y, 'expert', flip[1])
+        z_y = perm(normed, 'expert', flip[2])
+        z_c = perm(normed, 'expert', flip[1])
+        z_yc = perm(z_y, 'expert', flip[1])
         buf = None
         for k, rows in enumerate((normed, z_c, z_y, z_yc)):
             buf = dispatch(rank_rows[k], rows, buf, k, experts, cap, sources)
@@ -333,20 +471,29 @@
         scal_far = jnp.stack([(1 - rep) * half, data]).astype(jnp.int32)
         mid_near = gate_up(scal, x_all, 0, [gate_part] + g_near, [up_part] + u_near)
         mid_far = gate_up(scal_far, x_all, 1, [gate_part] + g_far, [up_part] + u_far)
-        mids = (mid_near, mid_far)
-
-        own_s = jnp.stack([rep, 1 - rep]).astype(jnp.int32)
-        zero_s = jnp.zeros((2,), jnp.int32)
-        own, far = [], []
+
+        near = lambda t: (0, mid_near, d_near[t:t + 1])
+        beyond = lambda t: (1, mid_far, d_far[t:t + 1])
+        start31, start2 = {}, {}
+        for t in (0, 2, 3):
+            start31[t] = combine(scal, table, (3, 1), [near(t)], [[], []])
+        for t in (0, 3):
+            start2[t] = list(combine(scal, table, (2,), [near(t)], [[]]))
+        r1, r3, far = [], [], []
         for t in range(steps):
-            downs = (down_part, down_part) if t == 0 else (d_near[t - 1], d_far[t - 1])
-            s = own_s if t == 0 else zero_s
-            p1, p3 = combine(s, table, 1, 2, mids, downs, ())
-            r1, r3 = lax.ppermute(p1, 'expert', flip[1]), lax.ppermute(p3, 'expert', flip[1])
-            a0, a2 = combine(s, table, 0, 2, mids, downs, (r1, r3))
-            own.append(a0)
-            far.append(lax.ppermute(a2, 'expert', flip[2]))
-        y = finish(data.reshape(1).astype(jnp.int32), hidden, own, far)
+            if t in start31:
+                p3, p1 = combine(scal, table, (3, 1), [beyond(t)], [[a] for a in start31[t]])
+            else:
+                p3, p1 = combine(scal, table, (3, 1), [near(t), beyond(t)], [[], []])
+            r3.append(perm(p3, 'expert', flip[1]))
+            r1.append(perm(p1, 'expert', flip[1]))
+            groups = [beyond(t)] if t in start2 else [near(t), beyond(t)]
+            a2, = combine(scal, table, (2,), groups, [start2.get(t, []) + [r3[t]]])
+            far.append(perm(a2, 'expert', flip[2]))
+        own, = combine(scal, table, (0,), [(0, mid_near, d_near), (1, mid_far, d_far)], [r1])
+        y = None
+        for t in range(steps):
+            y = finish(((data + steps - t) % steps).reshape(1).astype(jnp.int32), hidden, own, far[t], y)
         return y.reshape(num_seqs, seq_len, width)
 
     in_specs = (tok_spec, tok_spec, tok_spec, P(None), P(group_axes, None, None), P(None, None, group_axes), P(None), P('expert', 'data', None), P('expert', 'data', None), P('expert', None, 'data'))

time: 939 us -> 910 us (0.969)
  waiting for transfers between devices: 545 us -> 424 us
  Pallas kernels: 311 us -> 423 us
  between operations: 13.8 us -> 0.73 us
    pallas_call x10 -> x21, Pallas kernels: 191 us -> 303 us  [the longest x14 164 us: combine(): pl.pallas_call(functools.partial(combine_kernel, count, 2 * half, halves,...]
    all_gather x2 -> x0, waiting for transfers between devices: 95 us -> none  [the longest x1 91.1 us: local_step(): lax.all_gather(qkv_part.reshape(qkv_part.shape[0], heads_all * head_dim),...]
    ppermute x33 -> x34, waiting for transfers between devices: 450 us -> 423 us  [perm(): return lax.ppermute(value, axis, pairs)]
    ppermute x33 -> x34, starting transfers between devices: 24.8 us -> 20.6 us  [perm(): return lax.ppermute(value, axis, pairs)]
  transfers between devices with their start and end apart: 41 -> 40, of which waited for: 16 -> 16; matrix products, arithmetic and copies ran while one was open for 3% -> 2% of each run, Pallas kernels for 33% -> 39%
where the time goes in v2:
time: 910 us; the launch traced here: 904 us
  waiting for transfers between devices  424 us (47%)
  Pallas kernels  423 us (46%)
  starting transfers between devices  25.9 us (3%)
  local copies, waits for them, and re-layouts  21.6 us (2%)
    ppermute x34, waiting for transfers between devices, perm(): return lax.ppermute(value, axis, pairs)  423 us
    pallas_call x14, Pallas kernels, combine(): pl.pallas_call(functools.partial(combine_kernel, count, 2 * half, halves,...  164 us
    pallas_call x1, Pallas kernels, gather_attn(): pl.pallas_call(functools.partial(gather_kernel, names, sizes), name='gath...  81.3 us
    pallas_call x4, Pallas kernels, dispatch(): pl.pallas_call(body, grid=(2,), out_shape=jax.ShapeDtypeStruct((experts,...  49.6 us
    pallas_call x2, Pallas kernels, attend(): pl.pallas_call(functools.partial(attend_kernel, group_len, head_dim), gri...  45.1 us
    pallas_call x2, Pallas kernels, gate_up(): pl.pallas_call(functools.partial(gate_up_kernel, steps), grid_spec=pltpu....  44.6 us
    ppermute x34, starting transfers between devices, perm(): return lax.ppermute(value, axis, pairs)  20.6 us
  transfers between devices with their start and end apart: 40, of which 16 were waited for; matrix products, arithmetic and copies ran while one was open for 2% of the time, Pallas kernels for 39%

profile of v2, /device:TPU:0, one launch (start us, length us, event | category | flops | bytes accessed | tf_op | source)
XLA Modules:
  0.0 903.6 jit_solution(15611042485792626389)
XLA Ops:
  10.5 81.3 %gather_attn.1 = (bf16[1536,2560]{1,0:T(8,128)(2,1)}, bf16[1536,1536]{1,0:T(8,128)(2,1)}, bf16[5,384,512]{2,1,0:T(8,128)(2,1)}) custom-call(bf16[96,2560]{1,0:T(8,128)(2,1)} %copy.46.q_ref, bf16[96,1536]{1,0:T(8,128)(2,1)} %bitcast.49, bf16[10,384,512]{2,1,0:T(8,128)(2,1)} %refs_0_.3), custom_call_target="tpu_custom_call" | custom-call | flops 60000002048 | bytes 12582912 | tf_op jit(solution)/shard_map/gather_attn/pallas_call | solution.py:102
  103.8 14.7 %k_qkv.1.q_ref.k_ref.v_ref = bf16[1024,2560]{1,0:T(8,128)(2,1)} custom-call(bf16[1024,1536]{1,0:T(8,128)(2,1)} %bitcast.64, f32[1,1536]{1,0:T(1,128)} %reshape.87.gain_ref, bf16[1536,2560]{1,0:T(8,128)(2,1)} %get-tuple-element.28.w_ref, f32[512,128]{1,0:T(8,128)} %get-tuple-element.58.cos_ref, f32[512,128]{1,0:T(8,128)} %get-tuple-element.59.sin_ref), custom_call_target="tpu_custom_call" | custom-call | flops 8053063680 | bytes 16252928 | tf_op jit(solution)/shard_map/k_qkv/pallas_call | solution.py:134
  118.5 22.6 %shard_map.100.rest_0_ = bf16[1024,1536]{1,0:T(8,128)(2,1)} custom-call(bf16[1024,2560]{1,0:T(8,128)(2,1)} %k_qkv.1.q_ref.k_ref.v_ref, bf16[1024,2560]{1,0:T(8,128)(2,1)} %k_qkv.1.q_ref.k_ref.v_ref, bf16[1024,2560]{1,0:T(8,128)(2,1)} %k_qkv.1.q_ref.k_ref.v_ref), custom_call_target="tpu_custom_call" | custom-call | flops 6442450944 | bytes 4194304 | tf_op jit(solution)/shard_map/pallas_call | solution.py:172
  141.1 22.6 %shard_map.101.a_ref = bf16[1024,1536]{1,0:T(8,128)(2,1)} custom-call(bf16[1024,2560]{1,0:T(8,128)(2,1)} %k_qkv.1.q_ref.k_ref.v_ref, bf16[1024,2560]{1,0:T(8,128)(2,1)} %k_qkv.1.q_ref.k_ref.v_ref, bf16[1024,2560]{1,0:T(8,128)(2,1)} %k_qkv.1.q_ref.k_ref.v_ref, bf16[1024,1536]{1,0:T(8,128)(2,1)} %shard_map.100.rest_0_), custom_call_target="tpu_custom_call", output_to_operand_aliasing={{}: (3, {})} | custom-call | flops 6442450944 | bytes 4194304 | tf_op jit(solution)/shard_map/pallas_call | solution.py:172
  178.8 44.8 %collective-permute-done.11.refs_5_ = bf16[5,384,512]{2,1,0:T(8,128)(2,1)} collective-permute-done((bf16[5,384,512]{2,1,0:T(8,128)(2,1)S(1)}, bf16[5,384,512]{2,1,0:T(8,128)(2,1)}, u32[]{:S(2)}, u32[]{:S(2)}) %collective-permute-start.11) | collective-permute-done | bytes 1966112 | tf_op jit(solution)/shard_map/ppermute | solution.py:398
  225.0 40.7 %collective-permute-done.9.refs_2_ = bf16[5,384,512]{2,1,0:T(8,128)(2,1)} collective-permute-done((bf16[5,384,512]{2,1,0:T(8,128)(2,1)}, bf16[5,384,512]{2,1,0:T(8,128)(2,1)}, u32[]{:S(2)}, u32[]{:S(2)}) %collective-permute-start.9) | collective-permute-done | bytes 1966112 | tf_op jit(solution)/shard_map/ppermute | solution.py:398
  265.7 42.1 %collective-permute-done.20.refs_6_.refs_4_.refs_3_ = bf16[5,512,384]{2,1,0:T(8,128)(2,1)} collective-permute-done((bf16[5,512,384]{2,1,0:T(8,128)(2,1)S(1)}, bf16[5,512,384]{2,1,0:T(8,128)(2,1)}, u32[]{:S(2)}, u32[]{:S(2)}) %collective-permute-start.20) | collective-permute-done | bytes 1966112 | tf_op jit(solution)/shard_map/ppermute | solution.py:398
  315.1 34.8 %collective-permute-done.12.refs_6_ = bf16[5,384,512]{2,1,0:T(8,128)(2,1)} collective-permute-done((bf16[5,384,512]{2,1,0:T(8,128)(2,1)}, bf16[5,384,512]{2,1,0:T(8,128)(2,1)}, u32[]{:S(2)}, u32[]{:S(2)}) %collective-permute-start.12) | collective-permute-done | bytes 1966112 | tf_op jit(solution)/shard_map/ppermute | solution.py:398
  363.7 28.3 %collective-permute-done.21.refs_4_.refs_5_.refs_3_ = bf16[5,512,384]{2,1,0:T(8,128)(2,1)S(1)} collective-permute-done((bf16[5,512,384]{2,1,0:T(8,128)(2,1)}, bf16[5,512,384]{2,1,0:T(8,128)(2,1)S(1)}, u32[]{:S(2)}, u32[]{:S(2)}) %collective-permute-start.21) | collective-permute-done | bytes 1966112 | tf_op jit(solution)/shard_map/ppermute | solution.py:398
  393.4 12.4 %shard_map.103.buf_ref = bf16[10,4,256,1536]{3,2,1,0:T(8,128)(2,1)} custom-call(f32[16,1024]{1,0:T(8,128)} %copy.48.rank_ref, bf16[1024,1536]{1,0:T(8,128)(2,1)} %collective-permute-done.8.rows_ref, bf16[10,4,256,1536]{3,2,1,0:T(8,128)(2,1)} %shard_map.102.buf_ref), custom_call_target="tpu_custom_call", output_to_operand_aliasing={{}: (2, {})} | custom-call | flops 8053063680 | bytes 11010048 | tf_op jit(solution)/shard_map/pallas_call | solution.py:249
  419.4 14.8 %collective-permute-done.10.refs_3_ = bf16[5,384,512]{2,1,0:T(8,128)(2,1)} collective-permute-done((bf16[5,384,512]{2,1,0:T(8,128)(2,1)}, bf16[5,384,512]{2,1,0:T(8,128)(2,1)}, u32[]{:S(2)}, u32[]{:S(2)}) %collective-permute-start.10) | collective-permute-done | bytes 1966112 | tf_op jit(solution)/shard_map/ppermute | solution.py:398
  435.7 40.3 %collective-permute-done.13.refs_7_ = bf16[5,384,512]{2,1,0:T(8,128)(2,1)} collective-permute-done((bf16[5,384,512]{2,1,0:T(8,128)(2,1)}, bf16[5,384,512]{2,1,0:T(8,128)(2,1)}, u32[]{:S(2)}, u32[]{:S(2)}) %collective-permute-start.13) | collective-permute-done | bytes 1966112 | tf_op jit(solution)/shard_map/ppermute | solution.py:398
  478.0 12.5 %shard_map.105 = bf16[10,4,256,1536]{3,2,1,0:T(8,128)(2,1)} custom-call(f32[16,1024]{1,0:T(8,128)} %copy.50.rank_ref, bf16[1024,1536]{1,0:T(8,128)(2,1)} %collective-permute-done.7.rows_ref, bf16[10,4,256,1536]{3,2,1,0:T(8,128)(2,1)} %shard_map.104.buf_ref), custom_call_target="tpu_custom_call", output_to_operand_aliasing={{}: (2, {})} | custom-call | flops 8053063680 | bytes 11010048 | tf_op jit(solution)/shard_map/pallas_call | solution.py:249
  490.6 22.3 %shard_map.106.refs_2_.refs_3_.refs_1_ = bf16[5,1024,512]{2,1,0:T(8,128)(2,1)} custom-call(s32[2]{0:T(128)} %get-tuple-element.56.s_ref, bf16[10,1024,1536]{2,1,0:T(8,128)(2,1)} %bitcast.45, bf16[10,384,512]{2,1,0:T(8,128)(2,1)} %refs_0_.3, bf16[5,384,512]{2,1,0:T(8,128)(2,1)} %get-tuple-element.34.refs_1_, ...), custom_call_target="tpu_custom_call" | custom-call | flops 16106127360 | bytes 31457280 | tf_op jit(solution)/shard_map/pallas_call | solution.py:282
  512.9 23.6 %collective-permute-done.23.refs_5_.refs_7_.refs_3_ = bf16[2,512,384]{2,1,0:T(8,128)(2,1)} collective-permute-done((bf16[2,512,384]{2,1,0:T(8,128)(2,1)S(1)}, bf16[2,512,384]{2,1,0:T(8,128)(2,1)}, u32[]{:S(2)}, u32[]{:S(2)}) %collective-permute-start.23) | collective-permute-done | bytes 786464 | tf_op jit(solution)/shard_map/ppermute | solution.py:398
  551.5 25.3 %collective-permute-done.19.refs_7_ = bf16[5,384,512]{2,1,0:T(8,128)(2,1)} collective-permute-done((bf16[5,384,512]{2,1,0:T(8,128)(2,1)}, bf16[5,384,512]{2,1,0:T(8,128)(2,1)}, u32[]{:S(2)}, u32[]{:S(2)}) %collective-permute-start.19) | collective-permute-done | bytes 1966112 | tf_op jit(solution)/shard_map/ppermute | solution.py:398
  576.8 22.3 %shard_map.107.refs_2_.refs_3_.refs_4_.refs_5_.refs_1_ = bf16[5,1024,512]{2,1,0:T(8,128)(2,1)} custom-call(s32[2]{0:T(128)} %get-tuple-element.57.s_ref, bf16[10,1024,1536]{2,1,0:T(8,128)(2,1)} %bitcast.46, bf16[10,384,512]{2,1,0:T(8,128)(2,1)} %refs_0_.3, bf16[5,384,512]{2,1,0:T(8,128)(2,1)} %collective-permute-done.14.refs_1_, ...), custom_call_target="tpu_custom_call" | custom-call | flops 16106127360 | bytes 31457280 | tf_op jit(solution)/shard_map/pallas_call | solution.py:282
  620.2 16.6 %shard_map.110 = (f32[1024,384]{1,0:T(8,128)}, f32[1024,384]{1,0:T(8,128)}) custom-call(s32[2]{0:T(128)} %get-tuple-element.56.s_ref, f32[4,1024,128]{2,1,0:T(8,128)} %fusion.3.refs_0_.refs_1_, f32[4,1024,128]{2,1,0:T(8,128)} %fusion.3.refs_0_.refs_1_, bf16[5,1024,512]{2,1,0:T(8,128)(2,1)} %shard_map.106.refs_2_.refs_3_.refs_1_, ...), custom_call_target="tpu_custom_call" | custom-call | flops 6039797760 | bytes 10223616 | tf_op jit(solution)/shard_map/pallas_call | solution.py:361
  647.9 13.2 %collective-permute-done.25.refs_4_.refs_10_ = bf16[5,512,384]{2,1,0:T(8,128)(2,1)} collective-permute-done((bf16[5,512,384]{2,1,0:T(8,128)(2,1)S(1)}, bf16[5,512,384]{2,1,0:T(8,128)(2,1)}, u32[]{:S(2)}, u32[]{:S(2)}) %collective-permute-start.25) | collective-permute-done | bytes 1966112 | tf_op jit(solution)/shard_map/ppermute | solution.py:398
  684.2 17.3 %collective-permute-done.26.refs_4_.refs_11_.refs_2_ = bf16[3,512,384]{2,1,0:T(8,128)(2,1)} collective-permute-done((bf16[3,512,384]{2,1,0:T(8,128)(2,1)S(1)}, bf16[3,512,384]{2,1,0:T(8,128)(2,1)}, u32[]{:S(2)}, u32[]{:S(2)}) %collective-permute-start.26) | collective-permute-done | bytes 1179680 | tf_op jit(solution)/shard_map/ppermute | solution.py:398
  775.2 24.8 %shard_map.115.own_ref = f32[1024,1536]{1,0:T(8,128)} custom-call(s32[2]{0:T(128)} %get-tuple-element.56.s_ref, f32[4,1024,128]{2,1,0:T(8,128)} %fusion.3.refs_0_.refs_1_, bf16[5,1024,512]{2,1,0:T(8,128)(2,1)} %shard_map.106.refs_2_.refs_3_.refs_1_, bf16[5,1024,512]{2,1,0:T(8,128)(2,1)} %shard_map.107.refs_2_.refs_3_.refs_4_.refs_5_.refs_1_, ...), custom_call_target="tpu_custom_call" | custom-call | flops 12079595520 | bytes 28311552 | tf_op jit(solution)/shard_map/pallas_call | solution.py:361
  802.9 29.4 %collective-permute-done.37.far_ref = f32[1024,384]{1,0:T(8,128)} collective-permute-done((f32[1024,384]{1,0:T(8,128)}, f32[1024,384]{1,0:T(8,128)}, u32[]{:S(2)}, u32[]{:S(2)}) %collective-permute-start.37) | collective-permute-done | bytes 1572896 | tf_op jit(solution)/shard_map/ppermute | solution.py:398
  835.2 30.8 %collective-permute-done.35.far_ref = f32[1024,384]{1,0:T(8,128)} collective-permute-done((f32[1024,384]{1,0:T(8,128)}, f32[1024,384]{1,0:T(8,128)}, u32[]{:S(2)}, u32[]{:S(2)}) %collective-permute-start.35) | collective-permute-done | bytes 1572896 | tf_op jit(solution)/shard_map/ppermute | solution.py:398
  869.0 30.1 %collective-permute-done.33.far_ref = f32[1024,384]{1,0:T(8,128)S(1)} collective-permute-done((f32[1024,384]{1,0:T(8,128)}, f32[1024,384]{1,0:T(8,128)S(1)}, u32[]{:S(2)}, u32[]{:S(2)}) %collective-permute-start.33) | collective-permute-done | bytes 1572896 | tf_op jit(solution)/shard_map/ppermute | solution.py:398
  (142 shorter events, 235.4 us)
Async XLA Ops:
  0.0 92.4 %collective-permute-start = (s32[8,1024]{1,0:T(8,128)}, s32[8,1024]{1,0:T(8,128)S(1)}, u32[]{:S(2)}, u32[]{:S(2)}) collective-permute-start(s32[8,1024]{1,0:T(8,128)} %bitcast.50), channel_id=1, source_target_pairs={{0,1},{1,0},{2,3},{3,2},{4,5},{5,4},{6,7},{7,6},{8,9},{9,8},{10,11... | collective-permute-start | bytes 98312 | tf_op jit(solution)/shard_map/ppermute | solution.py:447
  0.5 91.9 %collective-permute-start.1 = (s32[8,1024]{1,0:T(8,128)}, s32[8,1024]{1,0:T(8,128)S(1)}, u32[]{:S(2)}, u32[]{:S(2)}) collective-permute-start(s32[8,1024]{1,0:T(8,128)} %bitcast.51), channel_id=1, source_target_pairs={{0,2},{1,3},{2,0},{3,1},{4,6},{5,7},{6,4},{7,5},{8,10},{9,11},{10,... | collective-permute-start | bytes 98312 | tf_op jit(solution)/shard_map/ppermute | solution.py:447
  3.1 89.4 %collective-permute-start.2 = (s32[8,1024]{1,0:T(8,128)}, s32[8,1024]{1,0:T(8,128)S(1)}, u32[]{:S(2)}, u32[]{:S(2)}) collective-permute-start(s32[8,1024]{1,0:T(8,128)} %bitcast.52), channel_id=1, source_target_pairs={{0,3},{1,2},{2,1},{3,0},{4,7},{5,6},{6,5},{7,4},{8,11},{9,10},{10,... | collective-permute-start | bytes 98312 | tf_op jit(solution)/shard_map/ppermute | solution.py:447
  3.1 92.2 %collective-permute-start.3 = (f32[8,1024]{1,0:T(8,128)}, f32[8,1024]{1,0:T(8,128)S(1)}, u32[]{:S(2)}, u32[]{:S(2)}) collective-permute-start(f32[8,1024]{1,0:T(8,128)} %bitcast.54), channel_id=1, source_target_pairs={{0,1},{1,0},{2,3},{3,2},{4,5},{5,4},{6,7},{7,6},{8,9},{9,8},{10,11... | collective-permute-start | bytes 98312 | tf_op jit(solution)/shard_map/ppermute | solution.py:448
  3.3 92.0 %collective-permute-start.4 = (f32[8,1024]{1,0:T(8,128)}, f32[8,1024]{1,0:T(8,128)S(1)}, u32[]{:S(2)}, u32[]{:S(2)}) collective-permute-start(f32[8,1024]{1,0:T(8,128)} %bitcast.55), channel_id=1, source_target_pairs={{0,2},{1,3},{2,0},{3,1},{4,6},{5,7},{6,4},{7,5},{8,10},{9,11},{10,... | collective-permute-start | bytes 98312 | tf_op jit(solution)/shard_map/ppermute | solution.py:448
  174.9 133.0 %collective-permute-start.6 = (bf16[1024,1536]{1,0:T(8,128)(2,1)}, bf16[1024,1536]{1,0:T(8,128)(2,1)}, u32[]{:S(2)}, u32[]{:S(2)}) collective-permute-start(bf16[1024,1536]{1,0:T(8,128)(2,1)} %get-tuple-element.33.rows_ref), channel_id=1, source_target_pairs={{0,2},{1,3},{2,0},{3,1},{4,6},{5,7},{6,4},{7,5},{8,10},{9,11},{10,... | collective-permute-start | bytes 9437192 | tf_op jit(solution)/shard_map/ppermute | solution.py:398
  177.5 88.2 %collective-permute-start.9 = (bf16[5,384,512]{2,1,0:T(8,128)(2,1)}, bf16[5,384,512]{2,1,0:T(8,128)(2,1)}, u32[]{:S(2)}, u32[]{:S(2)}) collective-permute-start(bf16[5,384,512]{2,1,0:T(8,128)(2,1)} %get-tuple-element.34.refs_1_), channel_id=1, source_target_pairs={{0,4},{4,8},{8,12},{12,0},{1,5},{5,9},{9,13},{13,1},{2,6},{6,10},{... | collective-permute-start | bytes 5898248 | tf_op jit(solution)/shard_map/ppermute | solution.py:398
  177.8 130.1 %collective-permute-start.20 = (bf16[5,512,384]{2,1,0:T(8,128)(2,1)S(1)}, bf16[5,512,384]{2,1,0:T(8,128)(2,1)}, u32[]{:S(2)}, u32[]{:S(2)}) collective-permute-start(bf16[5,512,384]{2,1,0:T(8,128)(2,1)S(1)} %constant_dynamic-slice_fusion), channel_id=1, source_target_pairs={{0,4},{4,8},{8,12},{12,0},{1,5},{5,9},{9,13},{13,1},{2,6},{6,10},{... | collective-permute-start | bytes 5898248 | tf_op jit(solution)/shard_map/ppermute | solution.py:398
  178.8 183.5 %collective-permute-start.8 = (bf16[1024,1536]{1,0:T(8,128)(2,1)}, bf16[1024,1536]{1,0:T(8,128)(2,1)}, u32[]{:S(2)}, u32[]{:S(2)}) collective-permute-start(bf16[1024,1536]{1,0:T(8,128)(2,1)} %get-tuple-element.33.rows_ref), channel_id=1, source_target_pairs={{0,1},{1,0},{2,3},{3,2},{4,5},{5,4},{6,7},{7,6},{8,9},{9,8},{10,11... | collective-permute-start | bytes 9437192 | tf_op jit(solution)/shard_map/ppermute | solution.py:398
  223.6 91.6 %collective-permute-start.14 = (bf16[5,384,512]{2,1,0:T(8,128)(2,1)}, bf16[5,384,512]{2,1,0:T(8,128)(2,1)}, u32[]{:S(2)}, u32[]{:S(2)}) collective-permute-start(bf16[5,384,512]{2,1,0:T(8,128)(2,1)} %get-tuple-element.34.refs_1_), channel_id=1, source_target_pairs={{0,16},{16,0},{1,17},{17,1},{2,18},{18,2},{3,19},{19,3},{4,20},{20... | collective-permute-start | bytes 5898248 | tf_op jit(solution)/shard_map/ppermute | solution.py:398
  265.7 84.3 %collective-permute-start.12 = (bf16[5,384,512]{2,1,0:T(8,128)(2,1)}, bf16[5,384,512]{2,1,0:T(8,128)(2,1)}, u32[]{:S(2)}, u32[]{:S(2)}) collective-permute-start(bf16[5,384,512]{2,1,0:T(8,128)(2,1)} %collective-permute-done.11.refs_5_), channel_id=1, source_target_pairs={{0,4},{4,8},{8,12},{12,0},{1,5},{5,9},{9,13},{13,1},{2,6},{6,10},{... | collective-permute-start | bytes 5898248 | tf_op jit(solution)/shard_map/ppermute | solution.py:398
  307.8 169.6 %collective-permute-start.7 = (bf16[1024,1536]{1,0:T(8,128)(2,1)}, bf16[1024,1536]{1,0:T(8,128)(2,1)}, u32[]{:S(2)}, u32[]{:S(2)}) collective-permute-start(bf16[1024,1536]{1,0:T(8,128)(2,1)} %collective-permute-done.6.rows_ref), channel_id=1, source_target_pairs={{0,1},{1,0},{2,3},{3,2},{4,5},{5,4},{6,7},{7,6},{8,9},{9,8},{10,11... | collective-permute-start | bytes 9437192 | tf_op jit(solution)/shard_map/ppermute | solution.py:398
  315.1 119.1 %collective-permute-start.10 = (bf16[5,384,512]{2,1,0:T(8,128)(2,1)}, bf16[5,384,512]{2,1,0:T(8,128)(2,1)}, u32[]{:S(2)}, u32[]{:S(2)}) collective-permute-start(bf16[5,384,512]{2,1,0:T(8,128)(2,1)} %collective-permute-done.9.refs_2_), channel_id=1, source_target_pairs={{0,4},{4,8},{8,12},{12,0},{1,5},{5,9},{9,13},{13,1},{2,6},{6,10},{... | collective-permute-start | bytes 5898248 | tf_op jit(solution)/shard_map/ppermute | solution.py:398
  350.0 126.0 %collective-permute-start.13 = (bf16[5,384,512]{2,1,0:T(8,128)(2,1)}, bf16[5,384,512]{2,1,0:T(8,128)(2,1)}, u32[]{:S(2)}, u32[]{:S(2)}) collective-permute-start(bf16[5,384,512]{2,1,0:T(8,128)(2,1)} %collective-permute-done.12.refs_6_), channel_id=1, source_target_pairs={{0,4},{4,8},{8,12},{12,0},{1,5},{5,9},{9,13},{13,1},{2,6},{6,10},{... | collective-permute-start | bytes 5898248 | tf_op jit(solution)/shard_map/ppermute | solution.py:398
  362.3 128.2 %collective-permute-start.17 = (bf16[5,384,512]{2,1,0:T(8,128)(2,1)}, bf16[5,384,512]{2,1,0:T(8,128)(2,1)}, u32[]{:S(2)}, u32[]{:S(2)}) collective-permute-start(bf16[5,384,512]{2,1,0:T(8,128)(2,1)} %collective-permute-done.11.refs_5_), channel_id=1, source_target_pairs={{0,16},{16,0},{1,17},{17,1},{2,18},{18,2},{3,19},{19,3},{4,20},{20... | collective-permute-start | bytes 5898248 | tf_op jit(solution)/shard_map/ppermute | solution.py:398
  392.0 98.5 %collective-permute-start.15 = (bf16[5,384,512]{2,1,0:T(8,128)(2,1)}, bf16[5,384,512]{2,1,0:T(8,128)(2,1)}, u32[]{:S(2)}, u32[]{:S(2)}) collective-permute-start(bf16[5,384,512]{2,1,0:T(8,128)(2,1)} %collective-permute-done.9.refs_2_), channel_id=1, source_target_pairs={{0,16},{16,0},{1,17},{17,1},{2,18},{18,2},{3,19},{19,3},{4,20},{20... | collective-permute-start | bytes 5898248 | tf_op jit(solution)/shard_map/ppermute | solution.py:398
  434.2 115.3 %collective-permute-start.18 = (bf16[5,384,512]{2,1,0:T(8,128)(2,1)}, bf16[5,384,512]{2,1,0:T(8,128)(2,1)}, u32[]{:S(2)}, u32[]{:S(2)}) collective-permute-start(bf16[5,384,512]{2,1,0:T(8,128)(2,1)} %collective-permute-done.12.refs_6_), channel_id=1, source_target_pairs={{0,16},{16,0},{1,17},{17,1},{2,18},{18,2},{3,19},{19,3},{4,20},{20... | collective-permute-start | bytes 5898248 | tf_op jit(solution)/shard_map/ppermute | solution.py:398
  477.4 99.4 %collective-permute-start.19 = (bf16[5,384,512]{2,1,0:T(8,128)(2,1)}, bf16[5,384,512]{2,1,0:T(8,128)(2,1)}, u32[]{:S(2)}, u32[]{:S(2)}) collective-permute-start(bf16[5,384,512]{2,1,0:T(8,128)(2,1)} %collective-permute-done.13.refs_7_), channel_id=1, source_target_pairs={{0,16},{16,0},{1,17},{17,1},{2,18},{18,2},{3,19},{19,3},{4,20},{20... | collective-permute-start | bytes 5898248 | tf_op jit(solution)/shard_map/ppermute | solution.py:398
  548.9 112.2 %collective-permute-start.25 = (bf16[5,512,384]{2,1,0:T(8,128)(2,1)S(1)}, bf16[5,512,384]{2,1,0:T(8,128)(2,1)}, u32[]{:S(2)}, u32[]{:S(2)}) collective-permute-start(bf16[5,512,384]{2,1,0:T(8,128)(2,1)S(1)} %collective-permute-done.21.refs_4_.refs_5_.refs_3_), channel_id=1, source_target_pairs={{0,16},{16,0},{1,17},{17,1},{2,18},{18,2},{3,19},{19,3},{4,20},{20... | collective-permute-start | bytes 5898248 | tf_op jit(solution)/shard_map/ppermute | solution.py:398
  549.5 134.7 %collective-permute-start.27 = (bf16[2,512,384]{2,1,0:T(8,128)(2,1)}, bf16[2,512,384]{2,1,0:T(8,128)(2,1)}, u32[]{:S(2)}, u32[]{:S(2)}) collective-permute-start(bf16[2,512,384]{2,1,0:T(8,128)(2,1)} %collective-permute-done.23.refs_5_.refs_7_.refs_3_), channel_id=1, source_target_pairs={{0,16},{16,0},{1,17},{17,1},{2,18},{18,2},{3,19},{19,3},{4,20},{20... | collective-permute-start | bytes 2359304 | tf_op jit(solution)/shard_map/ppermute | solution.py:398
  551.0 150.5 %collective-permute-start.26 = (bf16[3,512,384]{2,1,0:T(8,128)(2,1)S(1)}, bf16[3,512,384]{2,1,0:T(8,128)(2,1)}, u32[]{:S(2)}, u32[]{:S(2)}) collective-permute-start(bf16[3,512,384]{2,1,0:T(8,128)(2,1)S(1)} %collective-permute-done.22.refs_4_.refs_6_.refs_2_), channel_id=1, source_target_pairs={{0,16},{16,0},{1,17},{17,1},{2,18},{18,2},{3,19},{19,3},{4,20},{20... | collective-permute-start | bytes 3538952 | tf_op jit(solution)/shard_map/ppermute | solution.py:398
  611.1 103.3 %collective-permute-start.38 = (f32[1024,384]{1,0:T(8,128)}, f32[1024,384]{1,0:T(8,128)}, u32[]{:S(2)}, u32[]{:S(2)}) collective-permute-start(f32[1024,384]{1,0:T(8,128)} %get-tuple-element.48), channel_id=1, source_target_pairs={{0,1},{1,0},{2,3},{3,2},{4,5},{5,4},{6,7},{7,6},{8,9},{9,8},{10,11... | collective-permute-start | bytes 4718600 | tf_op jit(solution)/shard_map/ppermute | solution.py:398
  763.1 103.0 %collective-permute-start.35 = (f32[1024,384]{1,0:T(8,128)}, f32[1024,384]{1,0:T(8,128)}, u32[]{:S(2)}, u32[]{:S(2)}) collective-permute-start(f32[1024,384]{1,0:T(8,128)} %shard_map.118), channel_id=1, source_target_pairs={{0,2},{1,3},{2,0},{3,1},{4,6},{5,7},{6,4},{7,5},{8,10},{9,11},{10,... | collective-permute-start | bytes 4718600 | tf_op jit(solution)/shard_map/ppermute | solution.py:398
  773.2 125.8 %collective-permute-start.33 = (f32[1024,384]{1,0:T(8,128)}, f32[1024,384]{1,0:T(8,128)S(1)}, u32[]{:S(2)}, u32[]{:S(2)}) collective-permute-start(f32[1024,384]{1,0:T(8,128)} %shard_map.117), channel_id=1, source_target_pairs={{0,2},{1,3},{2,0},{3,1},{4,6},{5,7},{6,4},{7,5},{8,10},{9,11},{10,... | collective-permute-start | bytes 4718600 | tf_op jit(solution)/shard_map/ppermute | solution.py:398
  (31 other events, 1390.2 us)

commit v3 on v2

--- a/solution.py
+++ b/solution.py
@@ -295,7 +295,7 @@
 def combine_kernel(count, experts, halves, chunks, cuts, adds, s_ref, *refs):
     refs = list(refs)
     take = lambda n: [refs.pop(0) for _ in range(n)]
-    tables, mids = take(count), [take(count) for _ in halves]
+    tables, hots, mids = take(count), [take(count) for _ in halves], [take(count) for _ in halves]
     parts = [[take(len(cuts[t])) for t in range(chunks)] for _ in halves]
     added = [take(adds) for _ in range(count)]
     outs, (w_ref,) = take(count), take(1)
@@ -310,8 +310,11 @@
                     @pl.when((i >= start) & (i < start + size))
                     def _(j=j, t=t, piece=piece):
                         w_ref[j, :, spots[t]] = piece[0]
-    toks, cap = tables[0].shape[1], mids[0][0].shape[1]
-    slots = lax.broadcasted_iota(jnp.int32, (toks, cap), 1).astype(F32)
+    pairs = [(j, n) for j in range(len(halves)) for n in range(count)]
+    outcome = {}
+    for j, n in pairs:
+        w = parts[j][0][0][0] if plain else w_ref[j]
+        outcome[j, n] = jnp.dot(mids[j][n][0], w, preferred_element_type=F32).astype(BF16)
     for n in range(count):
         @pl.when(i == 0)
         def _(n=n):
@@ -322,20 +325,40 @@
                 outs[n][...] = added[n][0][...] if adds == 1 else added[n][0][...] + added[n][1][...]
             else:
                 outs[n][...] = jnp.zeros(outs[n].shape, F32)
-
+    toks = hots[0][0].shape[2]
+    tile = 256
+    for n in range(count):
         table = pltpu.roll(tables[n][0], lax.rem(128 - i, 128), 1)
-        total = None
-        for j, h in enumerate(halves):
-            e = h * (experts // 2)
-            w = parts[j][0][0][0] if plain else w_ref[j]
-            o = jnp.dot(mids[j][n][0], w, preferred_element_type=F32).astype(BF16)
-            hot = jnp.where(slots == table[:, e:e + 1], 1.0, 0.0).astype(BF16)
-            picked = jnp.dot(hot, o, preferred_element_type=F32) * table[:, experts + e:experts + e + 1]
-            total = picked if total is None else total + picked
-        outs[n][...] += total
-
-
-def combine(scal, table, ks, groups, adds):
+        for r in range(0, toks, tile):
+            total = None
+            for j, h in enumerate(halves):
+                e = experts + h * (experts // 2)
+                picked = jnp.dot(hots[j][n][0, 0, r:r + tile], outcome[j, n], preferred_element_type=F32) * table[r:r + tile, e:e + 1]
+                total = picked if total is None else total + picked
+            outs[n][r:r + tile] += total
+
+
+def select_kernel(experts, table_ref, hot_ref):
+    toks, cap = hot_ref.shape[2:]
+    slots = lax.broadcasted_iota(jnp.int32, (toks, cap), 1).astype(F32)
+    for e in range(experts):
+        hot_ref[0, e] = jnp.where(slots == table_ref[0][:, e:e + 1], 1.0, 0.0).astype(BF16)
+
+
+def selectors(table, experts, cap):
+    sources, toks, lanes = table.shape
+    return pl.pallas_call(
+        functools.partial(select_kernel, experts), name="selectors", grid=(sources,),
+        in_specs=[pl.BlockSpec((1, toks, lanes), lambda k: (k, 0, 0))],
+        out_specs=pl.BlockSpec((1, experts, toks, cap), lambda k: (k, 0, 0, 0)),
+        out_shape=jax.ShapeDtypeStruct((sources, experts, toks, cap), BF16),
+        cost_estimate=pl.CostEstimate(flops=4_000_000_000, bytes_accessed=2 * sources * experts * toks * cap, transcendentals=0),
+        compiler_params=pltpu.CompilerParams(vmem_limit_bytes=VMEM_LIMIT),
+    )(table)
+
+
+def combine(scal, tables, ks, groups, adds):
+    table, hot = tables
     sources, toks, lanes = table.shape
     half, rows, ff = groups[0][1].shape
     cap = rows // sources
@@ -345,6 +368,7 @@
     cuts = [[(start, size) for _, start, size in pieces] for pieces in groups[0][2]]
     table_spec = lambda k: pl.BlockSpec((1, toks, lanes), lambda i, s: (k, 0, 0))
     mid_spec = lambda k: pl.BlockSpec((1, cap, ff), lambda i, s: (i, k, 0))
+    hot_spec = lambda h, k: pl.BlockSpec((1, 1, toks, cap), lambda i, s: (k, h * half + i, 0, 0))
 
     def piece_spec(array, start, size, h):
         if array.shape[0] > half:
@@ -362,13 +386,13 @@
         functools.partial(combine_kernel, count, 2 * half, halves, chunks, cuts, len(adds[0])),
         grid_spec=pltpu.PrefetchScalarGridSpec(
             num_scalar_prefetch=1, grid=(half,),
-            in_specs=[table_spec(k) for k in ks] + [mid_spec(k) for _ in groups for k in ks] + [piece_spec(*p, h) for h, p in flat] + [single] * len(flat_adds),
+            in_specs=[table_spec(k) for k in ks] + [hot_spec(h, k) for h in halves for k in ks] + [mid_spec(k) for _ in groups for k in ks] + [piece_spec(*p, h) for h, p in flat] + [single] * len(flat_adds),
             out_specs=[whole] * count,
             scratch_shapes=[pltpu.VMEM((len(halves), ff, cols * chunks), BF16)]),
         out_shape=[jax.ShapeDtypeStruct((toks, cols * chunks), F32)] * count,
         cost_estimate=pl.CostEstimate(flops=flops, bytes_accessed=2 * len(halves) * half * ff * cols * chunks + count * 8 * toks * cols * chunks, transcendentals=0),
         compiler_params=pltpu.CompilerParams(vmem_limit_bytes=VMEM_LIMIT),
-    )(scal, *[table] * count, *[m for _, m, _ in groups for _ in ks], *[p[0] for _, p in flat], *flat_adds)
+    )(scal, *[table] * count, *[hot] * (count * len(halves)), *[m for _, m, _ in groups for _ in ks], *[p[0] for _, p in flat], *flat_adds)
 
 
 def finish_kernel(s_ref, h_ref, own_ref, far_ref, *refs):
@@ -472,13 +496,16 @@
         mid_near = gate_up(scal, x_all, 0, [gate_part] + g_near, [up_part] + u_near)
         mid_far = gate_up(scal_far, x_all, 1, [gate_part] + g_far, [up_part] + u_far)
 
+        table = (table, selectors(table, experts, cap))
         near = lambda t: (0, mid_near, d_near[t:t + 1])
         beyond = lambda t: (1, mid_far, d_far[t:t + 1])
         start31, start2 = {}, {}
-        for t in (0, 2, 3):
-            start31[t] = combine(scal, table, (3, 1), [near(t)], [[], []])
-        for t in (0, 3):
-            start2[t] = list(combine(scal, table, (2,), [near(t)], [[]]))
+        for t, ks in ((0, (3, 1, 2)), (2, (3, 1)), (3, (3, 1))):
+            sums = list(combine(scal, table, ks, [near(t)], [[]] * len(ks)))
+            start31[t] = sums[:2]
+            if sums[2:]:
+                start2[t] = sums[2:]
+        start2[3] = list(combine(scal, table, (2,), [near(3)], [[]]))
         r1, r3, far = [], [], []
         for t in range(steps):
             if t in start31:

time: 910 us -> 837 us (0.920)
  waiting for transfers between devices: 424 us -> 338 us
  Pallas kernels: 423 us -> 433 us
    ppermute x34, waiting for transfers between devices: 423 us -> 338 us  [perm(): return lax.ppermute(value, axis, pairs)]
    pallas_call x0 -> x1, Pallas kernels: none -> 10.2 us  [selectors(): pl.pallas_call(functools.partial(select_kernel, experts), name='selectors...]
    pallas_call x14 -> x13, Pallas kernels: 164 us -> 164 us  [combine(): pl.pallas_call(functools.partial(combine_kernel, count, 2 * half, halves,...]
  transfers between devices with their start and end apart: 40 -> 40, of which waited for: 16 -> 15; matrix products, arithmetic and copies ran while one was open for 2% -> 3% of each run, Pallas kernels for 39% -> 52%
where the time goes in v3:
time: 837 us; the launch traced here: 830 us
  Pallas kernels  433 us (52%)
  waiting for transfers between devices  338 us (40%)
  starting transfers between devices  26.8 us (3%)
  local copies, waits for them, and re-layouts  23.2 us (3%)
    ppermute x34, waiting for transfers between devices, perm(): return lax.ppermute(value, axis, pairs)  338 us
    pallas_call x13, Pallas kernels, combine(): pl.pallas_call(functools.partial(combine_kernel, count, 2 * half, halves,...  164 us
    pallas_call x1, Pallas kernels, gather_attn(): pl.pallas_call(functools.partial(gather_kernel, names, sizes), name='gath...  81.3 us
    pallas_call x4, Pallas kernels, dispatch(): pl.pallas_call(body, grid=(2,), out_shape=jax.ShapeDtypeStruct((experts,...  49.6 us
    pallas_call x2, Pallas kernels, attend(): pl.pallas_call(functools.partial(attend_kernel, group_len, head_dim), gri...  45.1 us
    pallas_call x2, Pallas kernels, gate_up(): pl.pallas_call(functools.partial(gate_up_kernel, steps), grid_spec=pltpu....  44.5 us
    ppermute x34, starting transfers between devices, perm(): return lax.ppermute(value, axis, pairs)  21.6 us
  transfers between devices with their start and end apart: 40, of which 15 were waited for; matrix products, arithmetic and copies ran while one was open for 3% of the time, Pallas kernels for 52%

profile of v3, /device:TPU:0, one launch (start us, length us, event | category | flops | bytes accessed | tf_op | source)
XLA Modules:
  0.0 830.0 jit_solution(12356485097077815620)
XLA Ops:
  13.6 81.3 %gather_attn.1 = (bf16[1536,2560]{1,0:T(8,128)(2,1)}, bf16[1536,1536]{1,0:T(8,128)(2,1)}, bf16[5,384,512]{2,1,0:T(8,128)(2,1)}) custom-call(bf16[96,2560]{1,0:T(8,128)(2,1)} %copy.46.q_ref, bf16[96,1536]{1,0:T(8,128)(2,1)} %bitcast.49, bf16[10,384,512]{2,1,0:T(8,128)(2,1)} %refs_0_.3), custom_call_target="tpu_custom_call" | custom-call | flops 60000002048 | bytes 12582912 | tf_op jit(solution)/shard_map/gather_attn/pallas_call | solution.py:102
  108.0 14.8 %k_qkv.1.q_ref.k_ref.v_ref = bf16[1024,2560]{1,0:T(8,128)(2,1)} custom-call(bf16[1024,1536]{1,0:T(8,128)(2,1)} %bitcast.64, f32[1,1536]{1,0:T(1,128)} %reshape.87.gain_ref, bf16[1536,2560]{1,0:T(8,128)(2,1)} %get-tuple-element.29.w_ref, f32[512,128]{1,0:T(8,128)} %get-tuple-element.60.cos_ref, f32[512,128]{1,0:T(8,128)} %get-tuple-element.61.sin_ref), custom_call_target="tpu_custom_call" | custom-call | flops 8053063680 | bytes 16252928 | tf_op jit(solution)/shard_map/k_qkv/pallas_call | solution.py:134
  122.8 22.6 %shard_map.100.rest_0_ = bf16[1024,1536]{1,0:T(8,128)(2,1)} custom-call(bf16[1024,2560]{1,0:T(8,128)(2,1)} %k_qkv.1.q_ref.k_ref.v_ref, bf16[1024,2560]{1,0:T(8,128)(2,1)} %k_qkv.1.q_ref.k_ref.v_ref, bf16[1024,2560]{1,0:T(8,128)(2,1)} %k_qkv.1.q_ref.k_ref.v_ref), custom_call_target="tpu_custom_call" | custom-call | flops 6442450944 | bytes 4194304 | tf_op jit(solution)/shard_map/pallas_call | solution.py:172
  145.4 22.6 %shard_map.101.a_ref = bf16[1024,1536]{1,0:T(8,128)(2,1)} custom-call(bf16[1024,2560]{1,0:T(8,128)(2,1)} %k_qkv.1.q_ref.k_ref.v_ref, bf16[1024,2560]{1,0:T(8,128)(2,1)} %k_qkv.1.q_ref.k_ref.v_ref, bf16[1024,2560]{1,0:T(8,128)(2,1)} %k_qkv.1.q_ref.k_ref.v_ref, bf16[1024,1536]{1,0:T(8,128)(2,1)} %shard_map.100.rest_0_), custom_call_target="tpu_custom_call", output_to_operand_aliasing={{}: (3, {})} | custom-call | flops 6442450944 | bytes 4194304 | tf_op jit(solution)/shard_map/pallas_call | solution.py:172
  185.3 42.3 %collective-permute-done.20.refs_10_.refs_6_.refs_5_ = bf16[5,512,384]{2,1,0:T(8,128)(2,1)} collective-permute-done((bf16[5,512,384]{2,1,0:T(8,128)(2,1)S(1)}, bf16[5,512,384]{2,1,0:T(8,128)(2,1)}, u32[]{:S(2)}, u32[]{:S(2)}) %collective-permute-start.20) | collective-permute-done | bytes 1966112 | tf_op jit(solution)/shard_map/ppermute | solution.py:422
  227.6 22.2 %collective-permute-done.6.rows_ref = bf16[1024,1536]{1,0:T(8,128)(2,1)} collective-permute-done((bf16[1024,1536]{1,0:T(8,128)(2,1)}, bf16[1024,1536]{1,0:T(8,128)(2,1)}, u32[]{:S(2)}, u32[]{:S(2)}) %collective-permute-start.6) | collective-permute-done | bytes 3145760 | tf_op jit(solution)/shard_map/ppermute | solution.py:422
  255.0 14.7 %collective-permute-done.12.refs_6_ = bf16[5,384,512]{2,1,0:T(8,128)(2,1)} collective-permute-done((bf16[5,384,512]{2,1,0:T(8,128)(2,1)}, bf16[5,384,512]{2,1,0:T(8,128)(2,1)}, u32[]{:S(2)}, u32[]{:S(2)}) %collective-permute-start.12) | collective-permute-done | bytes 1966112 | tf_op jit(solution)/shard_map/ppermute | solution.py:422
  269.7 12.4 %shard_map.102.buf_ref = bf16[10,4,256,1536]{3,2,1,0:T(8,128)(2,1)} custom-call(f32[16,1024]{1,0:T(8,128)} %copy.47.rank_ref, bf16[1024,1536]{1,0:T(8,128)(2,1)} %get-tuple-element.34.rows_ref), custom_call_target="tpu_custom_call" | custom-call | flops 8053063680 | bytes 11010048 | tf_op jit(solution)/shard_map/pallas_call | solution.py:249
  296.2 15.6 %collective-permute-done.21.refs_6_.refs_7_.refs_5_ = bf16[5,512,384]{2,1,0:T(8,128)(2,1)S(1)} collective-permute-done((bf16[5,512,384]{2,1,0:T(8,128)(2,1)}, bf16[5,512,384]{2,1,0:T(8,128)(2,1)S(1)}, u32[]{:S(2)}, u32[]{:S(2)}) %collective-permute-start.21) | collective-permute-done | bytes 1966112 | tf_op jit(solution)/shard_map/ppermute | solution.py:422
  339.2 14.8 %collective-permute-done.10.refs_3_ = bf16[5,384,512]{2,1,0:T(8,128)(2,1)} collective-permute-done((bf16[5,384,512]{2,1,0:T(8,128)(2,1)}, bf16[5,384,512]{2,1,0:T(8,128)(2,1)}, u32[]{:S(2)}, u32[]{:S(2)}) %collective-permute-start.10) | collective-permute-done | bytes 1966112 | tf_op jit(solution)/shard_map/ppermute | solution.py:422
  355.5 40.7 %collective-permute-done.13.refs_7_ = bf16[5,384,512]{2,1,0:T(8,128)(2,1)} collective-permute-done((bf16[5,384,512]{2,1,0:T(8,128)(2,1)}, bf16[5,384,512]{2,1,0:T(8,128)(2,1)}, u32[]{:S(2)}, u32[]{:S(2)}) %collective-permute-start.13) | collective-permute-done | bytes 1966112 | tf_op jit(solution)/shard_map/ppermute | solution.py:422
  398.2 12.5 %shard_map.105 = bf16[10,4,256,1536]{3,2,1,0:T(8,128)(2,1)} custom-call(f32[16,1024]{1,0:T(8,128)} %copy.50.rank_ref, bf16[1024,1536]{1,0:T(8,128)(2,1)} %collective-permute-done.7.rows_ref, bf16[10,4,256,1536]{3,2,1,0:T(8,128)(2,1)} %shard_map.104.buf_ref), custom_call_target="tpu_custom_call", output_to_operand_aliasing={{}: (2, {})} | custom-call | flops 8053063680 | bytes 11010048 | tf_op jit(solution)/shard_map/pallas_call | solution.py:249
  412.0 22.3 %shard_map.106.refs_6_.refs_7_.refs_8_.refs_4_.refs_5_.refs_3_.refs_2_ = bf16[5,1024,512]{2,1,0:T(8,128)(2,1)} custom-call(s32[2]{0:T(128)} %get-tuple-element.58.s_ref, bf16[10,1024,1536]{2,1,0:T(8,128)(2,1)} %bitcast.45, bf16[10,384,512]{2,1,0:T(8,128)(2,1)} %refs_0_.3, bf16[5,384,512]{2,1,0:T(8,128)(2,1)} %get-tuple-element.35.refs_1_, ...), custom_call_target="tpu_custom_call" | custom-call | flops 16106127360 | bytes 31457280 | tf_op jit(solution)/shard_map/pallas_call | solution.py:282
  434.2 22.8 %collective-permute-done.23.refs_7_.refs_9_.refs_4_ = bf16[2,512,384]{2,1,0:T(8,128)(2,1)} collective-permute-done((bf16[2,512,384]{2,1,0:T(8,128)(2,1)S(1)}, bf16[2,512,384]{2,1,0:T(8,128)(2,1)}, u32[]{:S(2)}, u32[]{:S(2)}) %collective-permute-start.23) | collective-permute-done | bytes 786464 | tf_op jit(solution)/shard_map/ppermute | solution.py:422
  458.6 13.8 %shard_map.108 = (f32[1024,384]{1,0:T(8,128)}, f32[1024,384]{1,0:T(8,128)}, f32[1024,384]{1,0:T(8,128)}) custom-call(s32[2]{0:T(128)} %get-tuple-element.58.s_ref, f32[4,1024,128]{2,1,0:T(8,128)} %fusion.3.table_ref.refs_0_.refs_1_.refs_2_, f32[4,1024,128]{2,1,0:T(8,128)} %fusion.3.table_ref.refs_0_.refs_1_.refs_2_, ...), custom_call_target="tpu_custom_call" | custom-call | flops 4529848320 | bytes 11403264 | tf_op jit(solution)/shard_map/pallas_call | solution.py:385
  475.0 34.2 %collective-permute-done.19.refs_7_ = bf16[5,384,512]{2,1,0:T(8,128)(2,1)} collective-permute-done((bf16[5,384,512]{2,1,0:T(8,128)(2,1)}, bf16[5,384,512]{2,1,0:T(8,128)(2,1)}, u32[]{:S(2)}, u32[]{:S(2)}) %collective-permute-start.19) | collective-permute-done | bytes 1966112 | tf_op jit(solution)/shard_map/ppermute | solution.py:422
  509.3 22.2 %shard_map.107.refs_4_.refs_5_.refs_8_.refs_9_.refs_2_ = bf16[5,1024,512]{2,1,0:T(8,128)(2,1)} custom-call(s32[2]{0:T(128)} %get-tuple-element.59.s_ref, bf16[10,1024,1536]{2,1,0:T(8,128)(2,1)} %bitcast.46, bf16[10,384,512]{2,1,0:T(8,128)(2,1)} %refs_0_.3, bf16[5,384,512]{2,1,0:T(8,128)(2,1)} %collective-permute-done.14.refs_1_, ...), custom_call_target="tpu_custom_call" | custom-call | flops 16106127360 | bytes 31457280 | tf_op jit(solution)/shard_map/pallas_call | solution.py:282
  552.6 16.0 %shard_map.110 = (f32[1024,384]{1,0:T(8,128)}, f32[1024,384]{1,0:T(8,128)}) custom-call(s32[2]{0:T(128)} %get-tuple-element.58.s_ref, f32[4,1024,128]{2,1,0:T(8,128)} %fusion.3.table_ref.refs_0_.refs_1_.refs_2_, f32[4,1024,128]{2,1,0:T(8,128)} %fusion.3.table_ref.refs_0_.refs_1_.refs_2_, ...), custom_call_target="tpu_custom_call" | custom-call | flops 6039797760 | bytes 10223616 | tf_op jit(solution)/shard_map/pallas_call | solution.py:385
  579.7 13.8 %collective-permute-done.25.refs_6_.refs_12_ = bf16[5,512,384]{2,1,0:T(8,128)(2,1)} collective-permute-done((bf16[5,512,384]{2,1,0:T(8,128)(2,1)S(1)}, bf16[5,512,384]{2,1,0:T(8,128)(2,1)}, u32[]{:S(2)}, u32[]{:S(2)}) %collective-permute-start.25) | collective-permute-done | bytes 1966112 | tf_op jit(solution)/shard_map/ppermute | solution.py:422
  616.7 18.1 %collective-permute-done.26.refs_6_.refs_13_.refs_3_ = bf16[3,512,384]{2,1,0:T(8,128)(2,1)} collective-permute-done((bf16[3,512,384]{2,1,0:T(8,128)(2,1)S(1)}, bf16[3,512,384]{2,1,0:T(8,128)(2,1)}, u32[]{:S(2)}, u32[]{:S(2)}) %collective-permute-start.26) | collective-permute-done | bytes 1179680 | tf_op jit(solution)/shard_map/ppermute | solution.py:422
  702.7 26.1 %shard_map.115.own_ref = f32[1024,1536]{1,0:T(8,128)} custom-call(s32[2]{0:T(128)} %get-tuple-element.58.s_ref, f32[4,1024,128]{2,1,0:T(8,128)} %fusion.3.table_ref.refs_0_.refs_1_.refs_2_, bf16[4,10,1024,256]{3,2,1,0:T(8,128)(2,1)} %selectors.1.refs_3_.refs_4_.refs_5_.refs_2_.refs_1_, ...), custom_call_target="tpu_custom_call" | custom-call | flops 12079595520 | bytes 28311552 | tf_op jit(solution)/shard_map/pallas_call | solution.py:385
  731.8 27.9 %collective-permute-done.37.far_ref = f32[1024,384]{1,0:T(8,128)S(1)} collective-permute-done((f32[1024,384]{1,0:T(8,128)}, f32[1024,384]{1,0:T(8,128)S(1)}, u32[]{:S(2)}, u32[]{:S(2)}) %collective-permute-start.37) | collective-permute-done | bytes 1572896 | tf_op jit(solution)/shard_map/ppermute | solution.py:422
  763.8 29.7 %collective-permute-done.35.far_ref = f32[1024,384]{1,0:T(8,128)} collective-permute-done((f32[1024,384]{1,0:T(8,128)}, f32[1024,384]{1,0:T(8,128)}, u32[]{:S(2)}, u32[]{:S(2)}) %collective-permute-start.35) | collective-permute-done | bytes 1572896 | tf_op jit(solution)/shard_map/ppermute | solution.py:422
  796.4 30.2 %collective-permute-done.33.far_ref = f32[1024,384]{1,0:T(8,128)} collective-permute-done((f32[1024,384]{1,0:T(8,128)}, f32[1024,384]{1,0:T(8,128)}, u32[]{:S(2)}, u32[]{:S(2)}) %collective-permute-start.33) | collective-permute-done | bytes 1572896 | tf_op jit(solution)/shard_map/ppermute | solution.py:422
  (140 shorter events, 235.9 us)
Async XLA Ops:
  0.0 95.5 %collective-permute-start = (s32[8,1024]{1,0:T(8,128)}, s32[8,1024]{1,0:T(8,128)S(1)}, u32[]{:S(2)}, u32[]{:S(2)}) collective-permute-start(s32[8,1024]{1,0:T(8,128)} %bitcast.50), channel_id=1, source_target_pairs={{0,1},{1,0},{2,3},{3,2},{4,5},{5,4},{6,7},{7,6},{8,9},{9,8},{10,11... | collective-permute-start | bytes 98312 | tf_op jit(solution)/shard_map/ppermute | solution.py:471
  0.5 95.0 %collective-permute-start.1 = (s32[8,1024]{1,0:T(8,128)}, s32[8,1024]{1,0:T(8,128)S(1)}, u32[]{:S(2)}, u32[]{:S(2)}) collective-permute-start(s32[8,1024]{1,0:T(8,128)} %bitcast.51), channel_id=1, source_target_pairs={{0,2},{1,3},{2,0},{3,1},{4,6},{5,7},{6,4},{7,5},{8,10},{9,11},{10,... | collective-permute-start | bytes 98312 | tf_op jit(solution)/shard_map/ppermute | solution.py:471
  3.1 94.0 %collective-permute-start.2 = (s32[8,1024]{1,0:T(8,128)}, s32[8,1024]{1,0:T(8,128)S(1)}, u32[]{:S(2)}, u32[]{:S(2)}) collective-permute-start(s32[8,1024]{1,0:T(8,128)} %bitcast.52), channel_id=1, source_target_pairs={{0,3},{1,2},{2,1},{3,0},{4,7},{5,6},{6,5},{7,4},{8,11},{9,10},{10,... | collective-permute-start | bytes 98312 | tf_op jit(solution)/shard_map/ppermute | solution.py:471
  3.1 96.8 %collective-permute-start.3 = (f32[8,1024]{1,0:T(8,128)}, f32[8,1024]{1,0:T(8,128)S(1)}, u32[]{:S(2)}, u32[]{:S(2)}) collective-permute-start(f32[8,1024]{1,0:T(8,128)} %bitcast.54), channel_id=1, source_target_pairs={{0,1},{1,0},{2,3},{3,2},{4,5},{5,4},{6,7},{7,6},{8,9},{9,8},{10,11... | collective-permute-start | bytes 98312 | tf_op jit(solution)/shard_map/ppermute | solution.py:472
  3.3 96.7 %collective-permute-start.4 = (f32[8,1024]{1,0:T(8,128)}, f32[8,1024]{1,0:T(8,128)S(1)}, u32[]{:S(2)}, u32[]{:S(2)}) collective-permute-start(f32[8,1024]{1,0:T(8,128)} %bitcast.55), channel_id=1, source_target_pairs={{0,2},{1,3},{2,0},{3,1},{4,6},{5,7},{6,4},{7,5},{8,10},{9,11},{10,... | collective-permute-start | bytes 98312 | tf_op jit(solution)/shard_map/ppermute | solution.py:472
  95.5 85.6 %collective-permute-start.11 = (bf16[5,384,512]{2,1,0:T(8,128)(2,1)}, bf16[5,384,512]{2,1,0:T(8,128)(2,1)}, u32[]{:S(2)}, u32[]{:S(2)}) collective-permute-start(bf16[5,384,512]{2,1,0:T(8,128)(2,1)} %constant_dynamic-slice_fusion.1), channel_id=1, source_target_pairs={{0,4},{4,8},{8,12},{12,0},{1,5},{5,9},{9,13},{13,1},{2,6},{6,10},{... | collective-permute-start | bytes 5898248 | tf_op jit(solution)/shard_map/ppermute | solution.py:422
  97.1 88.0 %collective-permute-start.9 = (bf16[5,384,512]{2,1,0:T(8,128)(2,1)}, bf16[5,384,512]{2,1,0:T(8,128)(2,1)}, u32[]{:S(2)}, u32[]{:S(2)}) collective-permute-start(bf16[5,384,512]{2,1,0:T(8,128)(2,1)} %get-tuple-element.35.refs_1_), channel_id=1, source_target_pairs={{0,4},{4,8},{8,12},{12,0},{1,5},{5,9},{9,13},{13,1},{2,6},{6,10},{... | collective-permute-start | bytes 5898248 | tf_op jit(solution)/shard_map/ppermute | solution.py:422
  180.7 114.1 %collective-permute-start.8 = (bf16[1024,1536]{1,0:T(8,128)(2,1)}, bf16[1024,1536]{1,0:T(8,128)(2,1)}, u32[]{:S(2)}, u32[]{:S(2)}) collective-permute-start(bf16[1024,1536]{1,0:T(8,128)(2,1)} %get-tuple-element.34.rows_ref), channel_id=1, source_target_pairs={{0,1},{1,0},{2,3},{3,2},{4,5},{5,4},{6,7},{7,6},{8,9},{9,8},{10,11... | collective-permute-start | bytes 9437192 | tf_op jit(solution)/shard_map/ppermute | solution.py:422
  185.1 84.6 %collective-permute-start.12 = (bf16[5,384,512]{2,1,0:T(8,128)(2,1)}, bf16[5,384,512]{2,1,0:T(8,128)(2,1)}, u32[]{:S(2)}, u32[]{:S(2)}) collective-permute-start(bf16[5,384,512]{2,1,0:T(8,128)(2,1)} %collective-permute-done.11.refs_5_), channel_id=1, source_target_pairs={{0,4},{4,8},{8,12},{12,0},{1,5},{5,9},{9,13},{13,1},{2,6},{6,10},{... | collective-permute-start | bytes 5898248 | tf_op jit(solution)/shard_map/ppermute | solution.py:422
  227.6 84.2 %collective-permute-start.21 = (bf16[5,512,384]{2,1,0:T(8,128)(2,1)}, bf16[5,512,384]{2,1,0:T(8,128)(2,1)S(1)}, u32[]{:S(2)}, u32[]{:S(2)}) collective-permute-start(bf16[5,512,384]{2,1,0:T(8,128)(2,1)} %collective-permute-done.20.refs_10_.refs_6_.refs_5_), channel_id=1, source_target_pairs={{0,4},{4,8},{8,12},{12,0},{1,5},{5,9},{9,13},{13,1},{2,6},{6,10},{... | collective-permute-start | bytes 5898248 | tf_op jit(solution)/shard_map/ppermute | solution.py:422
  249.8 147.8 %collective-permute-start.7 = (bf16[1024,1536]{1,0:T(8,128)(2,1)}, bf16[1024,1536]{1,0:T(8,128)(2,1)}, u32[]{:S(2)}, u32[]{:S(2)}) collective-permute-start(bf16[1024,1536]{1,0:T(8,128)(2,1)} %collective-permute-done.6.rows_ref), channel_id=1, source_target_pairs={{0,1},{1,0},{2,3},{3,2},{4,5},{5,4},{6,7},{7,6},{8,9},{9,8},{10,11... | collective-permute-start | bytes 9437192 | tf_op jit(solution)/shard_map/ppermute | solution.py:422
  254.7 99.3 %collective-permute-start.10 = (bf16[5,384,512]{2,1,0:T(8,128)(2,1)}, bf16[5,384,512]{2,1,0:T(8,128)(2,1)}, u32[]{:S(2)}, u32[]{:S(2)}) collective-permute-start(bf16[5,384,512]{2,1,0:T(8,128)(2,1)} %collective-permute-done.9.refs_2_), channel_id=1, source_target_pairs={{0,4},{4,8},{8,12},{12,0},{1,5},{5,9},{9,13},{13,1},{2,6},{6,10},{... | collective-permute-start | bytes 5898248 | tf_op jit(solution)/shard_map/ppermute | solution.py:422
  269.7 126.4 %collective-permute-start.13 = (bf16[5,384,512]{2,1,0:T(8,128)(2,1)}, bf16[5,384,512]{2,1,0:T(8,128)(2,1)}, u32[]{:S(2)}, u32[]{:S(2)}) collective-permute-start(bf16[5,384,512]{2,1,0:T(8,128)(2,1)} %collective-permute-done.12.refs_6_), channel_id=1, source_target_pairs={{0,4},{4,8},{8,12},{12,0},{1,5},{5,9},{9,13},{13,1},{2,6},{6,10},{... | collective-permute-start | bytes 5898248 | tf_op jit(solution)/shard_map/ppermute | solution.py:422
  294.7 116.0 %collective-permute-start.17 = (bf16[5,384,512]{2,1,0:T(8,128)(2,1)}, bf16[5,384,512]{2,1,0:T(8,128)(2,1)}, u32[]{:S(2)}, u32[]{:S(2)}) collective-permute-start(bf16[5,384,512]{2,1,0:T(8,128)(2,1)} %collective-permute-done.11.refs_5_), channel_id=1, source_target_pairs={{0,16},{16,0},{1,17},{17,1},{2,18},{18,2},{3,19},{19,3},{4,20},{20... | collective-permute-start | bytes 5898248 | tf_op jit(solution)/shard_map/ppermute | solution.py:422
  311.8 98.9 %collective-permute-start.15 = (bf16[5,384,512]{2,1,0:T(8,128)(2,1)}, bf16[5,384,512]{2,1,0:T(8,128)(2,1)}, u32[]{:S(2)}, u32[]{:S(2)}) collective-permute-start(bf16[5,384,512]{2,1,0:T(8,128)(2,1)} %collective-permute-done.9.refs_2_), channel_id=1, source_target_pairs={{0,16},{16,0},{1,17},{17,1},{2,18},{18,2},{3,19},{19,3},{4,20},{20... | collective-permute-start | bytes 5898248 | tf_op jit(solution)/shard_map/ppermute | solution.py:422
  354.0 119.0 %collective-permute-start.18 = (bf16[5,384,512]{2,1,0:T(8,128)(2,1)}, bf16[5,384,512]{2,1,0:T(8,128)(2,1)}, u32[]{:S(2)}, u32[]{:S(2)}) collective-permute-start(bf16[5,384,512]{2,1,0:T(8,128)(2,1)} %collective-permute-done.12.refs_6_), channel_id=1, source_target_pairs={{0,16},{16,0},{1,17},{17,1},{2,18},{18,2},{3,19},{19,3},{4,20},{20... | collective-permute-start | bytes 5898248 | tf_op jit(solution)/shard_map/ppermute | solution.py:422
  397.6 111.6 %collective-permute-start.19 = (bf16[5,384,512]{2,1,0:T(8,128)(2,1)}, bf16[5,384,512]{2,1,0:T(8,128)(2,1)}, u32[]{:S(2)}, u32[]{:S(2)}) collective-permute-start(bf16[5,384,512]{2,1,0:T(8,128)(2,1)} %collective-permute-done.13.refs_7_), channel_id=1, source_target_pairs={{0,16},{16,0},{1,17},{17,1},{2,18},{18,2},{3,19},{19,3},{4,20},{20... | collective-permute-start | bytes 5898248 | tf_op jit(solution)/shard_map/ppermute | solution.py:422
  457.1 94.2 %collective-permute-start.24 = (bf16[5,512,384]{2,1,0:T(8,128)(2,1)}, bf16[5,512,384]{2,1,0:T(8,128)(2,1)S(1)}, u32[]{:S(2)}, u32[]{:S(2)}) collective-permute-start(bf16[5,512,384]{2,1,0:T(8,128)(2,1)} %collective-permute-done.20.refs_10_.refs_6_.refs_5_), channel_id=1, source_target_pairs={{0,16},{16,0},{1,17},{17,1},{2,18},{18,2},{3,19},{19,3},{4,20},{20... | collective-permute-start | bytes 5898248 | tf_op jit(solution)/shard_map/ppermute | solution.py:422
  472.4 121.2 %collective-permute-start.25 = (bf16[5,512,384]{2,1,0:T(8,128)(2,1)S(1)}, bf16[5,512,384]{2,1,0:T(8,128)(2,1)}, u32[]{:S(2)}, u32[]{:S(2)}) collective-permute-start(bf16[5,512,384]{2,1,0:T(8,128)(2,1)S(1)} %collective-permute-done.21.refs_6_.refs_7_.refs_5_), channel_id=1, source_target_pairs={{0,16},{16,0},{1,17},{17,1},{2,18},{18,2},{3,19},{19,3},{4,20},{20... | collective-permute-start | bytes 5898248 | tf_op jit(solution)/shard_map/ppermute | solution.py:422
  473.0 143.7 %collective-permute-start.27 = (bf16[2,512,384]{2,1,0:T(8,128)(2,1)}, bf16[2,512,384]{2,1,0:T(8,128)(2,1)}, u32[]{:S(2)}, u32[]{:S(2)}) collective-permute-start(bf16[2,512,384]{2,1,0:T(8,128)(2,1)} %collective-permute-done.23.refs_7_.refs_9_.refs_4_), channel_id=1, source_target_pairs={{0,16},{16,0},{1,17},{17,1},{2,18},{18,2},{3,19},{19,3},{4,20},{20... | collective-permute-start | bytes 2359304 | tf_op jit(solution)/shard_map/ppermute | solution.py:422
  474.5 160.3 %collective-permute-start.26 = (bf16[3,512,384]{2,1,0:T(8,128)(2,1)S(1)}, bf16[3,512,384]{2,1,0:T(8,128)(2,1)}, u32[]{:S(2)}, u32[]{:S(2)}) collective-permute-start(bf16[3,512,384]{2,1,0:T(8,128)(2,1)S(1)} %collective-permute-done.22.refs_6_.refs_8_.refs_3_), channel_id=1, source_target_pairs={{0,16},{16,0},{1,17},{17,1},{2,18},{18,2},{3,19},{19,3},{4,20},{20... | collective-permute-start | bytes 3538952 | tf_op jit(solution)/shard_map/ppermute | solution.py:422
  543.4 104.1 %collective-permute-start.38 = (f32[1024,384]{1,0:T(8,128)}, f32[1024,384]{1,0:T(8,128)}, u32[]{:S(2)}, u32[]{:S(2)}) collective-permute-start(f32[1024,384]{1,0:T(8,128)} %get-tuple-element.50), channel_id=1, source_target_pairs={{0,1},{1,0},{2,3},{3,2},{4,5},{5,4},{6,7},{7,6},{8,9},{9,8},{10,11... | collective-permute-start | bytes 4718600 | tf_op jit(solution)/shard_map/ppermute | solution.py:422
  690.7 102.7 %collective-permute-start.35 = (f32[1024,384]{1,0:T(8,128)}, f32[1024,384]{1,0:T(8,128)}, u32[]{:S(2)}, u32[]{:S(2)}) collective-permute-start(f32[1024,384]{1,0:T(8,128)} %shard_map.118), channel_id=1, source_target_pairs={{0,2},{1,3},{2,0},{3,1},{4,6},{5,7},{6,4},{7,5},{8,10},{9,11},{10,... | collective-permute-start | bytes 4718600 | tf_op jit(solution)/shard_map/ppermute | solution.py:422
  701.6 125.0 %collective-permute-start.33 = (f32[1024,384]{1,0:T(8,128)}, f32[1024,384]{1,0:T(8,128)}, u32[]{:S(2)}, u32[]{:S(2)}) collective-permute-start(f32[1024,384]{1,0:T(8,128)} %shard_map.117), channel_id=1, source_target_pairs={{0,2},{1,3},{2,0},{3,1},{4,6},{5,7},{6,4},{7,5},{8,10},{9,11},{10,... | collective-permute-start | bytes 4718600 | tf_op jit(solution)/shard_map/ppermute | solution.py:422
  (30 other events, 1363.6 us)

commit v4 on v2

--- a/solution.py
+++ b/solution.py
@@ -475,10 +475,12 @@
         near = lambda t: (0, mid_near, d_near[t:t + 1])
         beyond = lambda t: (1, mid_far, d_far[t:t + 1])
         start31, start2 = {}, {}
-        for t in (0, 2, 3):
-            start31[t] = combine(scal, table, (3, 1), [near(t)], [[], []])
-        for t in (0, 3):
-            start2[t] = list(combine(scal, table, (2,), [near(t)], [[]]))
+        for t, ks in ((0, (3, 1, 2)), (2, (3, 1)), (3, (3, 1))):
+            sums = list(combine(scal, table, ks, [near(t)], [[]] * len(ks)))
+            start31[t] = sums[:2]
+            if sums[2:]:
+                start2[t] = sums[2:]
+        start2[3] = list(combine(scal, table, (2,), [near(3)], [[]]))
         r1, r3, far = [], [], []
         for t in range(steps):
             if t in start31:

time: 910 us -> 903 us (level)
    pallas_call x14 -> x13, Pallas kernels: 164 us -> 161 us  [combine(): pl.pallas_call(functools.partial(combine_kernel, count, 2 * half, halves,...]
where the time goes in v4:
time: 903 us; the launch traced here: 896 us
  waiting for transfers between devices  420 us (47%)
  Pallas kernels  419 us (46%)
  starting transfers between devices  25.9 us (3%)
  local copies, waits for them, and re-layouts  21.6 us (2%)
    ppermute x34, waiting for transfers between devices, perm(): return lax.ppermute(value, axis, pairs)  419 us
    pallas_call x13, Pallas kernels, combine(): pl.pallas_call(functools.partial(combine_kernel, count, 2 * half, halves,...  161 us
    pallas_call x1, Pallas kernels, gather_attn(): pl.pallas_call(functools.partial(gather_kernel, names, sizes), name='gath...  81.3 us
    pallas_call x4, Pallas kernels, dispatch(): pl.pallas_call(body, grid=(2,), out_shape=jax.ShapeDtypeStruct((experts,...  49.5 us
    pallas_call x2, Pallas kernels, attend(): pl.pallas_call(functools.partial(attend_kernel, group_len, head_dim), gri...  45.1 us
    pallas_call x2, Pallas kernels, gate_up(): pl.pallas_call(functools.partial(gate_up_kernel, steps), grid_spec=pltpu....  44.6 us
    ppermute x34, starting transfers between devices, perm(): return lax.ppermute(value, axis, pairs)  20.7 us
  transfers between devices with their start and end apart: 40, of which 16 were waited for; matrix products, arithmetic and copies ran while one was open for 2% of the time, Pallas kernels for 39%

profile of v4, /device:TPU:0, one launch (start us, length us, event | category | flops | bytes accessed | tf_op | source)
XLA Modules:
  0.0 896.1 jit_solution(502405880810331451)
XLA Ops:
  10.5 81.3 %gather_attn.1 = (bf16[1536,2560]{1,0:T(8,128)(2,1)}, bf16[1536,1536]{1,0:T(8,128)(2,1)}, bf16[5,384,512]{2,1,0:T(8,128)(2,1)}) custom-call(bf16[96,2560]{1,0:T(8,128)(2,1)} %copy.46.q_ref, bf16[96,1536]{1,0:T(8,128)(2,1)} %bitcast.49, bf16[10,384,512]{2,1,0:T(8,128)(2,1)} %refs_0_.3), custom_call_target="tpu_custom_call" | custom-call | flops 60000002048 | bytes 12582912 | tf_op jit(solution)/shard_map/gather_attn/pallas_call | solution.py:102
  103.8 14.7 %k_qkv.1.q_ref.k_ref.v_ref = bf16[1024,2560]{1,0:T(8,128)(2,1)} custom-call(bf16[1024,1536]{1,0:T(8,128)(2,1)} %bitcast.64, f32[1,1536]{1,0:T(1,128)} %reshape.87.gain_ref, bf16[1536,2560]{1,0:T(8,128)(2,1)} %get-tuple-element.29.w_ref, f32[512,128]{1,0:T(8,128)} %get-tuple-element.60.cos_ref, f32[512,128]{1,0:T(8,128)} %get-tuple-element.61.sin_ref), custom_call_target="tpu_custom_call" | custom-call | flops 8053063680 | bytes 16252928 | tf_op jit(solution)/shard_map/k_qkv/pallas_call | solution.py:134
  118.4 22.6 %shard_map.100.rest_0_ = bf16[1024,1536]{1,0:T(8,128)(2,1)} custom-call(bf16[1024,2560]{1,0:T(8,128)(2,1)} %k_qkv.1.q_ref.k_ref.v_ref, bf16[1024,2560]{1,0:T(8,128)(2,1)} %k_qkv.1.q_ref.k_ref.v_ref, bf16[1024,2560]{1,0:T(8,128)(2,1)} %k_qkv.1.q_ref.k_ref.v_ref), custom_call_target="tpu_custom_call" | custom-call | flops 6442450944 | bytes 4194304 | tf_op jit(solution)/shard_map/pallas_call | solution.py:172
  141.0 22.6 %shard_map.101.a_ref = bf16[1024,1536]{1,0:T(8,128)(2,1)} custom-call(bf16[1024,2560]{1,0:T(8,128)(2,1)} %k_qkv.1.q_ref.k_ref.v_ref, bf16[1024,2560]{1,0:T(8,128)(2,1)} %k_qkv.1.q_ref.k_ref.v_ref, bf16[1024,2560]{1,0:T(8,128)(2,1)} %k_qkv.1.q_ref.k_ref.v_ref, bf16[1024,1536]{1,0:T(8,128)(2,1)} %shard_map.100.rest_0_), custom_call_target="tpu_custom_call", output_to_operand_aliasing={{}: (3, {})} | custom-call | flops 6442450944 | bytes 4194304 | tf_op jit(solution)/shard_map/pallas_call | solution.py:172
  178.8 44.8 %collective-permute-done.11.refs_5_ = bf16[5,384,512]{2,1,0:T(8,128)(2,1)} collective-permute-done((bf16[5,384,512]{2,1,0:T(8,128)(2,1)S(1)}, bf16[5,384,512]{2,1,0:T(8,128)(2,1)}, u32[]{:S(2)}, u32[]{:S(2)}) %collective-permute-start.11) | collective-permute-done | bytes 1966112 | tf_op jit(solution)/shard_map/ppermute | solution.py:398
  225.0 40.7 %collective-permute-done.9.refs_2_ = bf16[5,384,512]{2,1,0:T(8,128)(2,1)} collective-permute-done((bf16[5,384,512]{2,1,0:T(8,128)(2,1)}, bf16[5,384,512]{2,1,0:T(8,128)(2,1)}, u32[]{:S(2)}, u32[]{:S(2)}) %collective-permute-start.9) | collective-permute-done | bytes 1966112 | tf_op jit(solution)/shard_map/ppermute | solution.py:398
  265.7 42.1 %collective-permute-done.20.refs_6_.refs_4_.refs_3_ = bf16[5,512,384]{2,1,0:T(8,128)(2,1)} collective-permute-done((bf16[5,512,384]{2,1,0:T(8,128)(2,1)S(1)}, bf16[5,512,384]{2,1,0:T(8,128)(2,1)}, u32[]{:S(2)}, u32[]{:S(2)}) %collective-permute-start.20) | collective-permute-done | bytes 1966112 | tf_op jit(solution)/shard_map/ppermute | solution.py:398
  315.1 34.9 %collective-permute-done.12.refs_6_ = bf16[5,384,512]{2,1,0:T(8,128)(2,1)} collective-permute-done((bf16[5,384,512]{2,1,0:T(8,128)(2,1)}, bf16[5,384,512]{2,1,0:T(8,128)(2,1)}, u32[]{:S(2)}, u32[]{:S(2)}) %collective-permute-start.12) | collective-permute-done | bytes 1966112 | tf_op jit(solution)/shard_map/ppermute | solution.py:398
  363.7 28.3 %collective-permute-done.21.refs_4_.refs_5_.refs_3_ = bf16[5,512,384]{2,1,0:T(8,128)(2,1)S(1)} collective-permute-done((bf16[5,512,384]{2,1,0:T(8,128)(2,1)}, bf16[5,512,384]{2,1,0:T(8,128)(2,1)S(1)}, u32[]{:S(2)}, u32[]{:S(2)}) %collective-permute-start.21) | collective-permute-done | bytes 1966112 | tf_op jit(solution)/shard_map/ppermute | solution.py:398
  419.3 14.9 %collective-permute-done.10.refs_3_ = bf16[5,384,512]{2,1,0:T(8,128)(2,1)} collective-permute-done((bf16[5,384,512]{2,1,0:T(8,128)(2,1)}, bf16[5,384,512]{2,1,0:T(8,128)(2,1)}, u32[]{:S(2)}, u32[]{:S(2)}) %collective-permute-start.10) | collective-permute-done | bytes 1966112 | tf_op jit(solution)/shard_map/ppermute | solution.py:398
  435.7 40.3 %collective-permute-done.13.refs_7_ = bf16[5,384,512]{2,1,0:T(8,128)(2,1)} collective-permute-done((bf16[5,384,512]{2,1,0:T(8,128)(2,1)}, bf16[5,384,512]{2,1,0:T(8,128)(2,1)}, u32[]{:S(2)}, u32[]{:S(2)}) %collective-permute-start.13) | collective-permute-done | bytes 1966112 | tf_op jit(solution)/shard_map/ppermute | solution.py:398
  478.0 12.6 %shard_map.105 = bf16[10,4,256,1536]{3,2,1,0:T(8,128)(2,1)} custom-call(f32[16,1024]{1,0:T(8,128)} %copy.50.rank_ref, bf16[1024,1536]{1,0:T(8,128)(2,1)} %collective-permute-done.7.rows_ref, bf16[10,4,256,1536]{3,2,1,0:T(8,128)(2,1)} %shard_map.104.buf_ref), custom_call_target="tpu_custom_call", output_to_operand_aliasing={{}: (2, {})} | custom-call | flops 8053063680 | bytes 11010048 | tf_op jit(solution)/shard_map/pallas_call | solution.py:249
  490.6 22.3 %shard_map.106.refs_3_.refs_4_.refs_5_.refs_2_.refs_1_ = bf16[5,1024,512]{2,1,0:T(8,128)(2,1)} custom-call(s32[2]{0:T(128)} %get-tuple-element.58.s_ref, bf16[10,1024,1536]{2,1,0:T(8,128)(2,1)} %bitcast.45, bf16[10,384,512]{2,1,0:T(8,128)(2,1)} %refs_0_.3, bf16[5,384,512]{2,1,0:T(8,128)(2,1)} %get-tuple-element.35.refs_1_, ...), custom_call_target="tpu_custom_call" | custom-call | flops 16106127360 | bytes 31457280 | tf_op jit(solution)/shard_map/pallas_call | solution.py:282
  513.0 23.6 %collective-permute-done.23.refs_5_.refs_7_.refs_3_ = bf16[2,512,384]{2,1,0:T(8,128)(2,1)} collective-permute-done((bf16[2,512,384]{2,1,0:T(8,128)(2,1)S(1)}, bf16[2,512,384]{2,1,0:T(8,128)(2,1)}, u32[]{:S(2)}, u32[]{:S(2)}) %collective-permute-start.23) | collective-permute-done | bytes 786464 | tf_op jit(solution)/shard_map/ppermute | solution.py:398
  538.1 15.0 %shard_map.108 = (f32[1024,384]{1,0:T(8,128)}, f32[1024,384]{1,0:T(8,128)}, f32[1024,384]{1,0:T(8,128)}) custom-call(s32[2]{0:T(128)} %get-tuple-element.58.s_ref, f32[4,1024,128]{2,1,0:T(8,128)} %fusion.3.refs_0_.refs_1_.refs_2_, f32[4,1024,128]{2,1,0:T(8,128)} %fusion.3.refs_0_.refs_1_.refs_2_, f32[4,1024,128]{2,1,0:T(8,128)} %fusion.3.refs_0_.refs_1_.refs_2_, ...), custom_call_target="tpu_custom_call" | custom-call | flops 4529848320 | bytes 11403264 | tf_op jit(solution)/shard_map/pallas_call | solution.py:361
  555.7 21.1 %collective-permute-done.19.refs_7_ = bf16[5,384,512]{2,1,0:T(8,128)(2,1)} collective-permute-done((bf16[5,384,512]{2,1,0:T(8,128)(2,1)}, bf16[5,384,512]{2,1,0:T(8,128)(2,1)}, u32[]{:S(2)}, u32[]{:S(2)}) %collective-permute-start.19) | collective-permute-done | bytes 1966112 | tf_op jit(solution)/shard_map/ppermute | solution.py:398
  576.8 22.3 %shard_map.107.refs_2_.refs_3_.refs_4_.refs_5_.refs_1_ = bf16[5,1024,512]{2,1,0:T(8,128)(2,1)} custom-call(s32[2]{0:T(128)} %get-tuple-element.59.s_ref, bf16[10,1024,1536]{2,1,0:T(8,128)(2,1)} %bitcast.46, bf16[10,384,512]{2,1,0:T(8,128)(2,1)} %refs_0_.3, bf16[5,384,512]{2,1,0:T(8,128)(2,1)} %collective-permute-done.14.refs_1_, ...), custom_call_target="tpu_custom_call" | custom-call | flops 16106127360 | bytes 31457280 | tf_op jit(solution)/shard_map/pallas_call | solution.py:282
  620.2 16.8 %shard_map.110 = (f32[1024,384]{1,0:T(8,128)}, f32[1024,384]{1,0:T(8,128)}) custom-call(s32[2]{0:T(128)} %get-tuple-element.58.s_ref, f32[4,1024,128]{2,1,0:T(8,128)} %fusion.3.refs_0_.refs_1_.refs_2_, f32[4,1024,128]{2,1,0:T(8,128)} %fusion.3.refs_0_.refs_1_.refs_2_, bf16[5,1024,512]{2,1,0:T(8,128)(2,1)} %shard_map.106.refs_3_.refs_4_.refs_5_.refs_2_.refs_1_, ...), custom_call_target="tpu_custom_call" | custom-call | flops 6039797760 | bytes 10223616 | tf_op jit(solution)/shard_map/pallas_call | solution.py:361
  647.8 13.2 %collective-permute-done.25.refs_4_.refs_10_ = bf16[5,512,384]{2,1,0:T(8,128)(2,1)} collective-permute-done((bf16[5,512,384]{2,1,0:T(8,128)(2,1)S(1)}, bf16[5,512,384]{2,1,0:T(8,128)(2,1)}, u32[]{:S(2)}, u32[]{:S(2)}) %collective-permute-start.25) | collective-permute-done | bytes 1966112 | tf_op jit(solution)/shard_map/ppermute | solution.py:398
  684.2 17.3 %collective-permute-done.26.refs_4_.refs_11_.refs_2_ = bf16[3,512,384]{2,1,0:T(8,128)(2,1)} collective-permute-done((bf16[3,512,384]{2,1,0:T(8,128)(2,1)S(1)}, bf16[3,512,384]{2,1,0:T(8,128)(2,1)}, u32[]{:S(2)}, u32[]{:S(2)}) %collective-permute-start.26) | collective-permute-done | bytes 1179680 | tf_op jit(solution)/shard_map/ppermute | solution.py:398
  767.6 24.8 %shard_map.115.own_ref = f32[1024,1536]{1,0:T(8,128)} custom-call(s32[2]{0:T(128)} %get-tuple-element.58.s_ref, f32[4,1024,128]{2,1,0:T(8,128)} %fusion.3.refs_0_.refs_1_.refs_2_, bf16[5,1024,512]{2,1,0:T(8,128)(2,1)} %shard_map.106.refs_3_.refs_4_.refs_5_.refs_2_.refs_1_, bf16[5,1024,512]{2,1,0:T(8,128)(2,1)} %shard_map.107.refs_2_.refs_3_.refs_4_.refs_5_.refs_1_, ...), custom_call_target="tpu_custom_call" | custom-call | flops 12079595520 | bytes 28311552 | tf_op jit(solution)/shard_map/pallas_call | solution.py:361
  795.4 29.4 %collective-permute-done.37.far_ref = f32[1024,384]{1,0:T(8,128)} collective-permute-done((f32[1024,384]{1,0:T(8,128)}, f32[1024,384]{1,0:T(8,128)}, u32[]{:S(2)}, u32[]{:S(2)}) %collective-permute-start.37) | collective-permute-done | bytes 1572896 | tf_op jit(solution)/shard_map/ppermute | solution.py:398
  827.7 30.8 %collective-permute-done.35.far_ref = f32[1024,384]{1,0:T(8,128)} collective-permute-done((f32[1024,384]{1,0:T(8,128)}, f32[1024,384]{1,0:T(8,128)}, u32[]{:S(2)}, u32[]{:S(2)}) %collective-permute-start.35) | collective-permute-done | bytes 1572896 | tf_op jit(solution)/shard_map/ppermute | solution.py:398
  861.4 30.1 %collective-permute-done.33.far_ref = f32[1024,384]{1,0:T(8,128)S(1)} collective-permute-done((f32[1024,384]{1,0:T(8,128)}, f32[1024,384]{1,0:T(8,128)S(1)}, u32[]{:S(2)}, u32[]{:S(2)}) %collective-permute-start.33) | collective-permute-done | bytes 1572896 | tf_op jit(solution)/shard_map/ppermute | solution.py:398
  (141 shorter events, 229.2 us)
Async XLA Ops:
  0.0 92.4 %collective-permute-start = (s32[8,1024]{1,0:T(8,128)}, s32[8,1024]{1,0:T(8,128)S(1)}, u32[]{:S(2)}, u32[]{:S(2)}) collective-permute-start(s32[8,1024]{1,0:T(8,128)} %bitcast.50), channel_id=1, source_target_pairs={{0,1},{1,0},{2,3},{3,2},{4,5},{5,4},{6,7},{7,6},{8,9},{9,8},{10,11... | collective-permute-start | bytes 98312 | tf_op jit(solution)/shard_map/ppermute | solution.py:447
  0.5 91.9 %collective-permute-start.1 = (s32[8,1024]{1,0:T(8,128)}, s32[8,1024]{1,0:T(8,128)S(1)}, u32[]{:S(2)}, u32[]{:S(2)}) collective-permute-start(s32[8,1024]{1,0:T(8,128)} %bitcast.51), channel_id=1, source_target_pairs={{0,2},{1,3},{2,0},{3,1},{4,6},{5,7},{6,4},{7,5},{8,10},{9,11},{10,... | collective-permute-start | bytes 98312 | tf_op jit(solution)/shard_map/ppermute | solution.py:447
  3.1 89.4 %collective-permute-start.2 = (s32[8,1024]{1,0:T(8,128)}, s32[8,1024]{1,0:T(8,128)S(1)}, u32[]{:S(2)}, u32[]{:S(2)}) collective-permute-start(s32[8,1024]{1,0:T(8,128)} %bitcast.52), channel_id=1, source_target_pairs={{0,3},{1,2},{2,1},{3,0},{4,7},{5,6},{6,5},{7,4},{8,11},{9,10},{10,... | collective-permute-start | bytes 98312 | tf_op jit(solution)/shard_map/ppermute | solution.py:447
  3.1 92.2 %collective-permute-start.3 = (f32[8,1024]{1,0:T(8,128)}, f32[8,1024]{1,0:T(8,128)S(1)}, u32[]{:S(2)}, u32[]{:S(2)}) collective-permute-start(f32[8,1024]{1,0:T(8,128)} %bitcast.54), channel_id=1, source_target_pairs={{0,1},{1,0},{2,3},{3,2},{4,5},{5,4},{6,7},{7,6},{8,9},{9,8},{10,11... | collective-permute-start | bytes 98312 | tf_op jit(solution)/shard_map/ppermute | solution.py:448
  3.3 92.0 %collective-permute-start.4 = (f32[8,1024]{1,0:T(8,128)}, f32[8,1024]{1,0:T(8,128)S(1)}, u32[]{:S(2)}, u32[]{:S(2)}) collective-permute-start(f32[8,1024]{1,0:T(8,128)} %bitcast.55), channel_id=1, source_target_pairs={{0,2},{1,3},{2,0},{3,1},{4,6},{5,7},{6,4},{7,5},{8,10},{9,11},{10,... | collective-permute-start | bytes 98312 | tf_op jit(solution)/shard_map/ppermute | solution.py:448
  174.9 132.9 %collective-permute-start.6 = (bf16[1024,1536]{1,0:T(8,128)(2,1)}, bf16[1024,1536]{1,0:T(8,128)(2,1)}, u32[]{:S(2)}, u32[]{:S(2)}) collective-permute-start(bf16[1024,1536]{1,0:T(8,128)(2,1)} %get-tuple-element.34.rows_ref), channel_id=1, source_target_pairs={{0,2},{1,3},{2,0},{3,1},{4,6},{5,7},{6,4},{7,5},{8,10},{9,11},{10,... | collective-permute-start | bytes 9437192 | tf_op jit(solution)/shard_map/ppermute | solution.py:398
  177.5 88.2 %collective-permute-start.9 = (bf16[5,384,512]{2,1,0:T(8,128)(2,1)}, bf16[5,384,512]{2,1,0:T(8,128)(2,1)}, u32[]{:S(2)}, u32[]{:S(2)}) collective-permute-start(bf16[5,384,512]{2,1,0:T(8,128)(2,1)} %get-tuple-element.35.refs_1_), channel_id=1, source_target_pairs={{0,4},{4,8},{8,12},{12,0},{1,5},{5,9},{9,13},{13,1},{2,6},{6,10},{... | collective-permute-start | bytes 5898248 | tf_op jit(solution)/shard_map/ppermute | solution.py:398
  177.8 130.1 %collective-permute-start.20 = (bf16[5,512,384]{2,1,0:T(8,128)(2,1)S(1)}, bf16[5,512,384]{2,1,0:T(8,128)(2,1)}, u32[]{:S(2)}, u32[]{:S(2)}) collective-permute-start(bf16[5,512,384]{2,1,0:T(8,128)(2,1)S(1)} %constant_dynamic-slice_fusion), channel_id=1, source_target_pairs={{0,4},{4,8},{8,12},{12,0},{1,5},{5,9},{9,13},{13,1},{2,6},{6,10},{... | collective-permute-start | bytes 5898248 | tf_op jit(solution)/shard_map/ppermute | solution.py:398
  178.8 183.5 %collective-permute-start.8 = (bf16[1024,1536]{1,0:T(8,128)(2,1)}, bf16[1024,1536]{1,0:T(8,128)(2,1)}, u32[]{:S(2)}, u32[]{:S(2)}) collective-permute-start(bf16[1024,1536]{1,0:T(8,128)(2,1)} %get-tuple-element.34.rows_ref), channel_id=1, source_target_pairs={{0,1},{1,0},{2,3},{3,2},{4,5},{5,4},{6,7},{7,6},{8,9},{9,8},{10,11... | collective-permute-start | bytes 9437192 | tf_op jit(solution)/shard_map/ppermute | solution.py:398
  223.6 91.5 %collective-permute-start.14 = (bf16[5,384,512]{2,1,0:T(8,128)(2,1)}, bf16[5,384,512]{2,1,0:T(8,128)(2,1)}, u32[]{:S(2)}, u32[]{:S(2)}) collective-permute-start(bf16[5,384,512]{2,1,0:T(8,128)(2,1)} %get-tuple-element.35.refs_1_), channel_id=1, source_target_pairs={{0,16},{16,0},{1,17},{17,1},{2,18},{18,2},{3,19},{19,3},{4,20},{20... | collective-permute-start | bytes 5898248 | tf_op jit(solution)/shard_map/ppermute | solution.py:398
  265.7 84.3 %collective-permute-start.12 = (bf16[5,384,512]{2,1,0:T(8,128)(2,1)}, bf16[5,384,512]{2,1,0:T(8,128)(2,1)}, u32[]{:S(2)}, u32[]{:S(2)}) collective-permute-start(bf16[5,384,512]{2,1,0:T(8,128)(2,1)} %collective-permute-done.11.refs_5_), channel_id=1, source_target_pairs={{0,4},{4,8},{8,12},{12,0},{1,5},{5,9},{9,13},{13,1},{2,6},{6,10},{... | collective-permute-start | bytes 5898248 | tf_op jit(solution)/shard_map/ppermute | solution.py:398
  307.8 169.6 %collective-permute-start.7 = (bf16[1024,1536]{1,0:T(8,128)(2,1)}, bf16[1024,1536]{1,0:T(8,128)(2,1)}, u32[]{:S(2)}, u32[]{:S(2)}) collective-permute-start(bf16[1024,1536]{1,0:T(8,128)(2,1)} %collective-permute-done.6.rows_ref), channel_id=1, source_target_pairs={{0,1},{1,0},{2,3},{3,2},{4,5},{5,4},{6,7},{7,6},{8,9},{9,8},{10,11... | collective-permute-start | bytes 9437192 | tf_op jit(solution)/shard_map/ppermute | solution.py:398
  315.1 119.1 %collective-permute-start.10 = (bf16[5,384,512]{2,1,0:T(8,128)(2,1)}, bf16[5,384,512]{2,1,0:T(8,128)(2,1)}, u32[]{:S(2)}, u32[]{:S(2)}) collective-permute-start(bf16[5,384,512]{2,1,0:T(8,128)(2,1)} %collective-permute-done.9.refs_2_), channel_id=1, source_target_pairs={{0,4},{4,8},{8,12},{12,0},{1,5},{5,9},{9,13},{13,1},{2,6},{6,10},{... | collective-permute-start | bytes 5898248 | tf_op jit(solution)/shard_map/ppermute | solution.py:398
  350.0 126.0 %collective-permute-start.13 = (bf16[5,384,512]{2,1,0:T(8,128)(2,1)}, bf16[5,384,512]{2,1,0:T(8,128)(2,1)}, u32[]{:S(2)}, u32[]{:S(2)}) collective-permute-start(bf16[5,384,512]{2,1,0:T(8,128)(2,1)} %collective-permute-done.12.refs_6_), channel_id=1, source_target_pairs={{0,4},{4,8},{8,12},{12,0},{1,5},{5,9},{9,13},{13,1},{2,6},{6,10},{... | collective-permute-start | bytes 5898248 | tf_op jit(solution)/shard_map/ppermute | solution.py:398
  362.3 128.3 %collective-permute-start.17 = (bf16[5,384,512]{2,1,0:T(8,128)(2,1)}, bf16[5,384,512]{2,1,0:T(8,128)(2,1)}, u32[]{:S(2)}, u32[]{:S(2)}) collective-permute-start(bf16[5,384,512]{2,1,0:T(8,128)(2,1)} %collective-permute-done.11.refs_5_), channel_id=1, source_target_pairs={{0,16},{16,0},{1,17},{17,1},{2,18},{18,2},{3,19},{19,3},{4,20},{20... | collective-permute-start | bytes 5898248 | tf_op jit(solution)/shard_map/ppermute | solution.py:398
  392.0 98.6 %collective-permute-start.15 = (bf16[5,384,512]{2,1,0:T(8,128)(2,1)}, bf16[5,384,512]{2,1,0:T(8,128)(2,1)}, u32[]{:S(2)}, u32[]{:S(2)}) collective-permute-start(bf16[5,384,512]{2,1,0:T(8,128)(2,1)} %collective-permute-done.9.refs_2_), channel_id=1, source_target_pairs={{0,16},{16,0},{1,17},{17,1},{2,18},{18,2},{3,19},{19,3},{4,20},{20... | collective-permute-start | bytes 5898248 | tf_op jit(solution)/shard_map/ppermute | solution.py:398
  434.2 119.5 %collective-permute-start.18 = (bf16[5,384,512]{2,1,0:T(8,128)(2,1)}, bf16[5,384,512]{2,1,0:T(8,128)(2,1)}, u32[]{:S(2)}, u32[]{:S(2)}) collective-permute-start(bf16[5,384,512]{2,1,0:T(8,128)(2,1)} %collective-permute-done.12.refs_6_), channel_id=1, source_target_pairs={{0,16},{16,0},{1,17},{17,1},{2,18},{18,2},{3,19},{19,3},{4,20},{20... | collective-permute-start | bytes 5898248 | tf_op jit(solution)/shard_map/ppermute | solution.py:398
  477.4 99.4 %collective-permute-start.19 = (bf16[5,384,512]{2,1,0:T(8,128)(2,1)}, bf16[5,384,512]{2,1,0:T(8,128)(2,1)}, u32[]{:S(2)}, u32[]{:S(2)}) collective-permute-start(bf16[5,384,512]{2,1,0:T(8,128)(2,1)} %collective-permute-done.13.refs_7_), channel_id=1, source_target_pairs={{0,16},{16,0},{1,17},{17,1},{2,18},{18,2},{3,19},{19,3},{4,20},{20... | collective-permute-start | bytes 5898248 | tf_op jit(solution)/shard_map/ppermute | solution.py:398
  553.1 108.0 %collective-permute-start.25 = (bf16[5,512,384]{2,1,0:T(8,128)(2,1)S(1)}, bf16[5,512,384]{2,1,0:T(8,128)(2,1)}, u32[]{:S(2)}, u32[]{:S(2)}) collective-permute-start(bf16[5,512,384]{2,1,0:T(8,128)(2,1)S(1)} %collective-permute-done.21.refs_4_.refs_5_.refs_3_), channel_id=1, source_target_pairs={{0,16},{16,0},{1,17},{17,1},{2,18},{18,2},{3,19},{19,3},{4,20},{20... | collective-permute-start | bytes 5898248 | tf_op jit(solution)/shard_map/ppermute | solution.py:398
  553.7 130.5 %collective-permute-start.27 = (bf16[2,512,384]{2,1,0:T(8,128)(2,1)}, bf16[2,512,384]{2,1,0:T(8,128)(2,1)}, u32[]{:S(2)}, u32[]{:S(2)}) collective-permute-start(bf16[2,512,384]{2,1,0:T(8,128)(2,1)} %collective-permute-done.23.refs_5_.refs_7_.refs_3_), channel_id=1, source_target_pairs={{0,16},{16,0},{1,17},{17,1},{2,18},{18,2},{3,19},{19,3},{4,20},{20... | collective-permute-start | bytes 2359304 | tf_op jit(solution)/shard_map/ppermute | solution.py:398
  555.2 146.3 %collective-permute-start.26 = (bf16[3,512,384]{2,1,0:T(8,128)(2,1)S(1)}, bf16[3,512,384]{2,1,0:T(8,128)(2,1)}, u32[]{:S(2)}, u32[]{:S(2)}) collective-permute-start(bf16[3,512,384]{2,1,0:T(8,128)(2,1)S(1)} %collective-permute-done.22.refs_4_.refs_6_.refs_2_), channel_id=1, source_target_pairs={{0,16},{16,0},{1,17},{17,1},{2,18},{18,2},{3,19},{19,3},{4,20},{20... | collective-permute-start | bytes 3538952 | tf_op jit(solution)/shard_map/ppermute | solution.py:398
  611.1 103.3 %collective-permute-start.38 = (f32[1024,384]{1,0:T(8,128)}, f32[1024,384]{1,0:T(8,128)}, u32[]{:S(2)}, u32[]{:S(2)}) collective-permute-start(f32[1024,384]{1,0:T(8,128)} %get-tuple-element.50), channel_id=1, source_target_pairs={{0,1},{1,0},{2,3},{3,2},{4,5},{5,4},{6,7},{7,6},{8,9},{9,8},{10,11... | collective-permute-start | bytes 4718600 | tf_op jit(solution)/shard_map/ppermute | solution.py:398
  755.5 103.0 %collective-permute-start.35 = (f32[1024,384]{1,0:T(8,128)}, f32[1024,384]{1,0:T(8,128)}, u32[]{:S(2)}, u32[]{:S(2)}) collective-permute-start(f32[1024,384]{1,0:T(8,128)} %shard_map.118), channel_id=1, source_target_pairs={{0,2},{1,3},{2,0},{3,1},{4,6},{5,7},{6,4},{7,5},{8,10},{9,11},{10,... | collective-permute-start | bytes 4718600 | tf_op jit(solution)/shard_map/ppermute | solution.py:398
  765.7 125.9 %collective-permute-start.33 = (f32[1024,384]{1,0:T(8,128)}, f32[1024,384]{1,0:T(8,128)S(1)}, u32[]{:S(2)}, u32[]{:S(2)}) collective-permute-start(f32[1024,384]{1,0:T(8,128)} %shard_map.117), channel_id=1, source_target_pairs={{0,2},{1,3},{2,0},{3,1},{4,6},{5,7},{6,4},{7,5},{8,10},{9,11},{10,... | collective-permute-start | bytes 4718600 | tf_op jit(solution)/shard_map/ppermute | solution.py:398
  (31 other events, 1360.7 us)
